TPU v7x, 64 devices: a 2x2x8 block of a 4x4x8 slice. The times are simulated.
64 devices in a mesh: data: 4 (over x, y), dap: 16 (over z, core).
Axes of the slice: x: 2, y: 2, z: 8, core: 2. Of those that a mesh axis runs over, the one named last changes fastest.
The devices are a block of a 4x4x8 slice.
Arguments:
- msa_act: bfloat16 [512, 192, 256], P(('data', 'dap')), parts along dimension 0
- pair_act: bfloat16 [768, 192, 128], P(('data', 'dap')), parts along dimension 0
- msa_mask: int32 [512, 192], P('data'), parts along dimension 0
- res_mask: int32 [768], P('data'), parts along dimension 0
- w_row_bias: bfloat16 [2, 128, 8], replicated
- w_row_in: bfloat16 [2, 256, 4, 8, 32], replicated
- w_row_out: bfloat16 [2, 8, 32, 256], replicated
- w_col_in: bfloat16 [2, 256, 4, 8, 32], replicated
- w_col_out: bfloat16 [2, 8, 32, 256], replicated
- w_opm_in: bfloat16 [2, 256, 2, 32], replicated
- w_opm_out: bfloat16 [2, 32, 32, 128], replicated
- w_ts_bias: bfloat16 [2, 128, 4], replicated
- w_ts_in: bfloat16 [2, 128, 4, 4, 32], replicated
- w_ts_out: bfloat16 [2, 4, 32, 128], replicated
- w_te_bias: bfloat16 [2, 128, 4], replicated
- w_te_in: bfloat16 [2, 128, 4, 4, 32], replicated
- w_te_out: bfloat16 [2, 4, 32, 128], replicated
Outputs:
- output 1: bfloat16 [512, 192, 256], P(('data', 'dap')), parts along dimension 0
- output 2: bfloat16 [768, 192, 128], P(('data', 'dap')), parts along dimension 0
There are 4 independent parts. A program takes and returns all parts, laid end to end along the dimension named above; an argument that names none is the same for every part.
All inputs are finite; a program needn't handle non-finite values.
Results may differ from a plain program's by a relative error of at most 0.0162995.
Values are sent between devices in bfloat16 or wider.
A program may use at most 768 MiB of HBM per device.

v0:
```python
import jax
import jax.numpy as jnp
from jax import lax
from jax.sharding import PartitionSpec as P


def layer_norm(values):
    flat = values.astype(jnp.float32)
    row_mean = jnp.mean(flat, axis=-1, keepdims=True)
    centered = flat - row_mean
    row_var = jnp.mean(centered * centered, axis=-1, keepdims=True)
    return (centered * lax.rsqrt(row_var + 1e-5)).astype(jnp.bfloat16)


def add_residual(current, update):
    return (current.astype(jnp.float32) + update).astype(jnp.bfloat16)


def pair_bias(pair_ln, w_bias, form):
    return jnp.einsum(form, pair_ln, w_bias, preferred_element_type=jnp.float32).astype(jnp.bfloat16)


def gated_attention(x_ln, w_in, w_out, bias_hqk, key_mask, batch_first):
    head_dim = w_in.shape[3]
    projected = jnp.einsum('abc,cfhd->abfhd', x_ln, w_in, preferred_element_type=jnp.float32).astype(jnp.bfloat16)
    query = projected[:, :, 0]
    keys = projected[:, :, 1]
    values = projected[:, :, 2]
    gate_raw = projected[:, :, 3]
    if batch_first:
        logits = jnp.einsum('bqhd,bkhd->bhqk', query, keys, preferred_element_type=jnp.float32)
    else:
        logits = jnp.einsum('qbhd,kbhd->bhqk', query, keys, preferred_element_type=jnp.float32)
    logits = logits * head_dim ** -0.5
    if bias_hqk is not None:
        logits = logits + bias_hqk.astype(jnp.float32)
    logits = jnp.where(key_mask > 0, logits, -1e9)
    attn_probs = jax.nn.softmax(logits, axis=-1).astype(jnp.bfloat16)
    if batch_first:
        attended = jnp.einsum('bhqk,bkhd->bqhd', attn_probs, values, preferred_element_type=jnp.float32)
    else:
        attended = jnp.einsum('bhqk,kbhd->qbhd', attn_probs, values, preferred_element_type=jnp.float32)
    gated = (attended * jax.nn.sigmoid(gate_raw.astype(jnp.float32))).astype(jnp.bfloat16)
    return jnp.einsum('abhd,hdc->abc', gated, w_out, preferred_element_type=jnp.float32)


def opm_halves(value_a8, mask_cols, w_in):
    projected = jnp.einsum('sic,cfp->sifp', layer_norm(value_a8), w_in, preferred_element_type=jnp.float32)
    projected = (projected * mask_cols.astype(jnp.float32)[:, :, None, None]).astype(jnp.bfloat16)
    return projected[:, :, 0], projected[:, :, 1]


def opm_update(pair_act, left, right, left_mask, right_mask, w_out):
    outer = jnp.einsum('sip,sjq->ijpq', left, right, preferred_element_type=jnp.float32).astype(jnp.bfloat16)
    update = jnp.einsum('ijpq,pqc->ijc', outer, w_out, preferred_element_type=jnp.float32)
    pair_norm = jnp.einsum('si,sj->ij', left_mask.astype(jnp.bfloat16), right_mask.astype(jnp.bfloat16), preferred_element_type=jnp.float32)
    return add_residual(pair_act, update / (1e-3 + pair_norm)[:, :, None])


def solution(mesh):
    def local_step(value_a7, pair_blk, array_b8, res_mask, w_row_bias, w_row_in, w_row_out, w_col_in, w_col_out, w_opm_in, w_opm_out, w_ts_bias, w_ts_in, w_ts_out, w_te_bias, w_te_in, w_te_out):
        dev_index = lax.axis_index('dap')
        seq_loc = value_a7.shape[0]
        res_loc = pair_blk.shape[0]
        mask_seq = lax.dynamic_slice_in_dim(array_b8, dev_index * seq_loc, seq_loc, 0)
        mask_cols = lax.dynamic_slice_in_dim(array_b8, dev_index * res_loc, res_loc, 1)
        row_keys = mask_seq[:, None, None, :]
        col_keys = mask_cols.T[:, None, None, :]
        tri_keys = res_mask[None, None, None, :]

        row_bias = lax.all_gather(pair_bias(layer_norm(pair_blk), w_row_bias[0], 'ijc,ch->hij'), 'dap', axis=1, tiled=True)
        value_a7 = add_residual(value_a7, gated_attention(layer_norm(value_a7), w_row_in[0], w_row_out[0], row_bias, row_keys, True))
        value_a7 = lax.all_to_all(value_a7, 'dap', 1, 0, tiled=True)
        value_a7 = add_residual(value_a7, gated_attention(layer_norm(value_a7), w_col_in[0], w_col_out[0], None, col_keys, False))
        left, right = opm_halves(value_a7, mask_cols, w_opm_in[0])
        right_full = lax.all_gather(right, 'dap', axis=1, tiled=True)
        pair_blk = opm_update(pair_blk, left, right_full, mask_cols, array_b8, w_opm_out[0])
        pair_ln = layer_norm(pair_blk)
        tri_bias = lax.all_gather(pair_bias(pair_ln, w_ts_bias[0], 'ijc,ch->hij'), 'dap', axis=1, tiled=True)
        pair_blk = add_residual(pair_blk, gated_attention(pair_ln, w_ts_in[0], w_ts_out[0], tri_bias, tri_keys, True))
        pair_blk = lax.all_to_all(pair_blk, 'dap', 1, 0, tiled=True)
        pair_ln = layer_norm(pair_blk)
        tri_bias = lax.all_gather(pair_bias(pair_ln, w_te_bias[0], 'kic,ch->hik'), 'dap', axis=1, tiled=True)
        pair_blk = add_residual(pair_blk, gated_attention(pair_ln, w_te_in[0], w_te_out[0], tri_bias, tri_keys, False))

        row_bias = lax.all_gather(pair_bias(layer_norm(pair_blk), w_row_bias[1], 'ijc,ch->hij'), 'dap', axis=2, tiled=True)
        value_a7 = add_residual(value_a7, gated_attention(layer_norm(value_a7), w_col_in[1], w_col_out[1], None, col_keys, False))
        left, right = opm_halves(value_a7, mask_cols, w_opm_in[1])
        left_full = lax.all_gather(left, 'dap', axis=1, tiled=True)
        pair_blk = opm_update(pair_blk, left_full, right, array_b8, mask_cols, w_opm_out[1])
        value_a7 = lax.all_to_all(value_a7, 'dap', 0, 1, tiled=True)
        value_a7 = add_residual(value_a7, gated_attention(layer_norm(value_a7), w_row_in[1], w_row_out[1], row_bias, row_keys, True))
        pair_ln = layer_norm(pair_blk)
        tri_bias = lax.all_gather(pair_bias(pair_ln, w_te_bias[1], 'kic,ch->hik'), 'dap', axis=1, tiled=True)
        pair_blk = add_residual(pair_blk, gated_attention(pair_ln, w_te_in[1], w_te_out[1], tri_bias, tri_keys, False))
        pair_blk = lax.all_to_all(pair_blk, 'dap', 0, 1, tiled=True)
        pair_ln = layer_norm(pair_blk)
        tri_bias = lax.all_gather(pair_bias(pair_ln, w_ts_bias[1], 'ijc,ch->hij'), 'dap', axis=1, tiled=True)
        pair_blk = add_residual(pair_blk, gated_attention(pair_ln, w_ts_in[1], w_ts_out[1], tri_bias, tri_keys, True))
        return value_a7, pair_blk

    in_specs = (P(('data', 'dap')), P(('data', 'dap')), P('data'), P('data')) + (P(),) * 13
    out_specs = (P(('data', 'dap')), P(('data', 'dap')))
    return jax.shard_map(local_step, mesh=mesh, in_specs=in_specs, out_specs=out_specs, check_vma=False)
```

profile of v0, /device:TPU:21, one launch (start us, length us, event | category | flops | bytes accessed | tf_op | source)
XLA Modules:
  0.0 451.7 jit_solution(5029166166818341037)
XLA Ops:
  13.8 24.8 %all_gather.24 = bf16[8,192,192]{2,0,1:T(8,128)(2,1)S(1)} all-gather(bf16[8,12,192]{2,0,1:T(8,128)(2,1)S(1)} %fusion.139), channel_id=1, replica_groups=mesh['data'=4,'dap'=16] {'dap'}, dimensions={1}, use_global_device_ids=true | all-gather | bytes 626688 | tf_op jit(solution)/shard_map/all_gather | solution.py:71
  43.3 9.2 %fusion.280 = (f32[8,8,192]{2,1,0:T(8,128)S(1)}, f32[8,8,192,192]{2,3,1,0:T(8,128)}) fusion(f32[8,192,192]{1,2,0:T(8,128)S(1)} %copy.143, pred[8,192]{1,0:T(8,128)(4,1)S(1)} %broadcast_compare_fusion, bf16[8,192,4,8,32]{1,4,3,2,0:T(8,128)(2,1)} %convolution_convert_fusion.1), kind=kOutput, calls=%fused_computation.394 | convolution fusion | flops 162791616 | bytes 12764672 | tf_op jit(solution)/shard_map/sub | solution.py:38
  52.6 6.9 %fusion.77 = bf16[8,192,256]{2,1,0:T(8,128)(2,1)S(1)} fusion(bf16[8,192,256]{2,1,0:T(8,128)(2,1)S(1)} %copy-done, f32[8,8,192,192]{2,3,1,0:T(8,128)} %get-tuple-element.3, f32[8,8,192]{2,1,0:T(8,128)S(1)} %get-tuple-element.2, bf16[8,192,4,8,32]{1,4,3,2,0:T(8,128)(2,1)} %convolution_convert_fusion.1, bf16[2,8,32,256]{3,2,1,0:T(8,128)(2,1)S(1)} %copy-done.23), kind=kOutput, calls=%fused_computation.129 | convolution fusion | flops 360579072 | bytes 16449536 | tf_op jit(solution)/shard_map/abhd,hdc->abc/dot_general | solution.py:44
  65.1 21.3 %all-to-all-done = bf16[8,192,256]{2,0,1:T(8,128)(2,1)S(1)} async-done(((bf16[8,192,256]{2,0,1:T(8,128)(2,1)}), bf16[8,192,256]{2,0,1:T(8,128)(2,1)S(1)}, u32[]{:S(2)}, u32[]{:S(2)}) %all-to-all-start) | async-done | bytes 786464 | tf_op jit(solution)/shard_map/all_to_all | solution.py:73
  108.5 9.1 %fusion.282 = (f32[12,8,128]{2,1,0:T(8,128)}, f32[12,8,128,128]{2,3,1,0:T(8,128)}) fusion(f32[12,8,128,128]{2,3,1,0:T(8,128)} %fusion.164, pred[12,128]{1,0:T(8,128)(4,1)S(1)} %compare_bitcast_fusion), kind=kOutput, calls=%fused_computation.396 | output fusion | flops 9437311 | bytes 12633600 | tf_op jit(solution)/shard_map/sub | solution.py:38
  131.8 26.9 %all-to-all-done.1 = bf16[128,12,256]{2,1,0:T(8,128)(2,1)S(1)} async-done(((bf16[128,12,256]{2,1,0:T(8,128)(2,1)}), bf16[128,12,256]{2,1,0:T(8,128)(2,1)S(1)}, u32[]{:S(2)}, u32[]{:S(2)}) %all-to-all-start.1) | async-done | bytes 786464 | tf_op jit(solution)/shard_map/all_to_all | solution.py:91
  160.3 10.5 %convert_bitcast_fusion = bf16[12,192,32,32]{2,3,0,1:T(8,128)(2,1)} fusion(bf16[128,192,1,32]{0,3,2,1:T(8,128)(2,1)} %all-gather.5.cloned.1.call-done, bf16[128,12,2,32]{0,3,2,1:T(8,128)(2,1)S(1)} %fusion.137), kind=kOutput, calls=%fused_computation.8 | convolution fusion | flops 606339072 | bytes 6389760 | tf_op jit(solution)/shard_map/sip,sjq->ijpq/dot_general | solution.py:54
  170.8 21.6 %copy.155 = bf16[12,192,32,32]{1,3,2,0:T(8,128)(2,1)} copy(bf16[12,192,32,32]{2,3,0,1:T(8,128)(2,1)} %convert_bitcast_fusion) | data formatting | bytes 9437184 | tf_op jit(solution)/shard_map/convert_element_type | solution.py:54
  202.3 15.8 %all_gather.26 = bf16[4,192,192]{2,0,1:T(4,128)(2,1)S(1)} all-gather(bf16[4,12,192]{2,0,1:T(4,128)(2,1)S(1)} %fusion.141), channel_id=1, replica_groups=mesh['data'=4,'dap'=16] {'dap'}, dimensions={1}, use_global_device_ids=true | all-gather | bytes 313344 | tf_op jit(solution)/shard_map/all_gather | solution.py:79
  218.5 9.4 %fusion.283 = (f32[12,4,192]{2,1,0:T(4,128)S(1)}, f32[12,4,192,192]{2,3,1,0:T(8,128)}) fusion(f32[4,192,192]{1,2,0:T(8,128)S(1)} %copy.157, pred[192]{0:T(512)(128)(4,1)S(1)} %broadcast_compare_fusion.1, bf16[12,192,4,4,32]{1,4,3,2,0:T(8,128)(2,1)} %convolution_convert_fusion.5), kind=kOutput, calls=%fused_computation.397 | convolution fusion | flops 122093760 | bytes 9277632 | tf_op jit(solution)/shard_map/sub | solution.py:38
  228.0 5.5 %fusion.109 = bf16[12,192,128]{2,1,0:T(8,128)(2,1)S(1)} fusion(bf16[12,192,128]{2,1,0:T(8,128)(2,1)S(1)} %get-tuple-element.11, f32[12,4,192,192]{2,3,1,0:T(8,128)} %get-tuple-element.13, f32[12,4,192]{2,1,0:T(4,128)S(1)} %get-tuple-element.12, bf16[12,192,4,4,32]{1,4,3,2,0:T(8,128)(2,1)} %convolution_convert_fusion.5, ...), kind=kOutput, calls=%fused_computation.178 | convolution fusion | flops 194936832 | bytes 12271616 | tf_op jit(solution)/shard_map/abhd,hdc->abc/dot_general | solution.py:44
  245.8 16.1 %all-to-all-done.2 = bf16[12,192,128]{2,0,1:T(8,128)(2,1)S(1)} async-done(((bf16[12,192,128]{2,0,1:T(8,128)(2,1)}), bf16[12,192,128]{2,0,1:T(8,128)(2,1)S(1)}, u32[]{:S(2)}, u32[]{:S(2)}) %all-to-all-start.2) | async-done | bytes 589856 | tf_op jit(solution)/shard_map/all_to_all | solution.py:81
  266.5 15.9 %all_gather.27 = bf16[4,192,192]{2,0,1:T(4,128)(2,1)S(1)} all-gather(bf16[4,12,192]{2,0,1:T(4,128)(2,1)S(1)} %fusion.142), channel_id=1, replica_groups=mesh['data'=4,'dap'=16] {'dap'}, dimensions={1}, use_global_device_ids=true | all-gather | bytes 313344 | tf_op jit(solution)/shard_map/all_gather | solution.py:83
  287.6 8.0 %fusion.284 = (f32[12,4,192]{2,1,0:T(4,128)}, f32[12,4,192,192]{2,3,1,0:T(8,128)}) fusion(f32[4,192,192]{1,2,0:T(8,128)} %copy.164, pred[192]{0:T(512)(128)(4,1)S(1)} %copy-done.33, bf16[192,12,4,4,32]{0,4,3,2,1:T(8,128)(2,1)S(1)} %convolution_convert_fusion.4), kind=kOutput, calls=%fused_computation.398 | convolution fusion | flops 122093760 | bytes 9277952 | tf_op jit(solution)/shard_map/sub | solution.py:38
  295.6 6.2 %convert_reduce_fusion.4 = (f32[192,12]{0,1:T(8,128)S(1)}, bf16[192,12,128]{2,0,1:T(8,128)(2,1)}) fusion(f32[192,12,128]{2,0,1:T(8,128)} %reshape.303, bf16[2,4,32,128]{3,2,1,0:T(8,128)(2,1)S(1)} %copy-done.26, f32[12,4,192,192]{2,3,1,0:T(8,128)} %get-tuple-element.15, f32[12,4,192]{2,1,0:T(4,128)} %get-tuple-element.14, ...), kind=kOutput, calls=%fused_computation.116 | convolution fusion | flops 195229440 | bytes 10499072 | tf_op jit(solution)/shard_map/abhd,hdc->abc/dot_general | solution.py:44
  311.2 17.6 %all_gather.30 = bf16[4,192,192]{2,0,1:T(4,128)(2,1)S(1)} all-gather(bf16[4,12,192]{2,0,1:T(4,128)(2,1)S(1)} %fusion.143), channel_id=1, replica_groups=mesh['data'=4,'dap'=16] {'dap'}, dimensions={1}, use_global_device_ids=true | all-gather | bytes 313344 | tf_op jit(solution)/shard_map/all_gather | solution.py:94
  329.1 9.4 %fusion.288 = (f32[12,4,192]{2,1,0:T(4,128)S(1)}, f32[12,4,192,192]{2,3,1,0:T(8,128)}) fusion(f32[4,192,192]{1,2,0:T(8,128)S(1)} %copy.171, pred[192]{0:T(512)(128)(4,1)S(1)} %copy-done.33, bf16[192,12,4,4,32]{0,4,3,2,1:T(8,128)(2,1)} %convolution_convert_fusion.3), kind=kOutput, calls=%fused_computation.400 | convolution fusion | flops 122093760 | bytes 9277632 | tf_op jit(solution)/shard_map/sub | solution.py:38
  338.6 5.5 %fusion.110 = bf16[192,12,128]{2,0,1:T(8,128)(2,1)S(1)} fusion(bf16[192,12,128]{2,0,1:T(8,128)(2,1)S(1)} %get-tuple-element.23, f32[12,4,192,192]{2,3,1,0:T(8,128)} %get-tuple-element.25, f32[12,4,192]{2,1,0:T(4,128)S(1)} %get-tuple-element.24, bf16[192,12,4,4,32]{0,4,3,2,1:T(8,128)(2,1)} %convolution_convert_fusion.3, ...), kind=kOutput, calls=%fused_computation.179 | convolution fusion | flops 194936832 | bytes 12271616 | tf_op jit(solution)/shard_map/abhd,hdc->abc/dot_general | solution.py:44
  351.9 31.7 %all_gather.28 = bf16[8,192,192]{1,0,2:T(8,128)(2,1)S(1)} all-gather(bf16[8,192,12]{1,0,2:T(8,128)(2,1)S(1)} %fusion.140), channel_id=1, replica_groups=mesh['data'=4,'dap'=16] {'dap'}, dimensions={2}, use_global_device_ids=true | all-gather | bytes 626688 | tf_op jit(solution)/shard_map/all_gather | solution.py:86
  384.9 9.8 %fusion.285 = (f32[8,8,192]{2,1,0:T(8,128)S(1)}, f32[8,8,192,192]{2,3,1,0:T(8,128)}) fusion(f32[8,192,192]{1,2,0:T(8,128)} %copy.166, pred[8,192]{1,0:T(8,128)(4,1)S(1)} %copy-done.17, bf16[8,192,4,8,32]{1,4,3,2,0:T(8,128)(2,1)} %convolution_convert_fusion), kind=kOutput, calls=%fused_computation.399 | convolution fusion | flops 162791616 | bytes 13157888 | tf_op jit(solution)/shard_map/sub | solution.py:38
  394.8 8.0 %fusion.84 = bf16[8,192,256]{2,1,0:T(8,128)(2,1)} fusion(f32[8,192,256]{2,0,1:T(8,128)S(1)} %bitcast.618, f32[8,8,192,192]{2,3,1,0:T(8,128)} %get-tuple-element.19, f32[8,8,192]{2,1,0:T(8,128)S(1)} %get-tuple-element.18, bf16[8,192,4,8,32]{1,4,3,2,0:T(8,128)(2,1)} %convolution_convert_fusion, bf16[2,8,32,256]{3,2,1,0:T(8,128)(2,1)S(1)} %copy-done.24), kind=kOutput, calls=%fused_computation.138 | convolution fusion | flops 360185856 | bytes 17235968 | tf_op jit(solution)/shard_map/abhd,hdc->abc/dot_general | solution.py:44
  410.1 15.8 %all_gather.31 = bf16[4,192,192]{2,0,1:T(4,128)(2,1)S(1)} all-gather(bf16[4,12,192]{2,0,1:T(4,128)(2,1)S(1)} %fusion.144), channel_id=1, replica_groups=mesh['data'=4,'dap'=16] {'dap'}, dimensions={1}, use_global_device_ids=true | all-gather | bytes 313344 | tf_op jit(solution)/shard_map/all_gather | solution.py:98
  428.7 9.7 %fusion.289 = (f32[12,4,192]{2,1,0:T(4,128)S(1)}, f32[12,4,192,192]{2,3,1,0:T(8,128)}) fusion(f32[4,192,192]{1,2,0:T(8,128)} %copy.178, pred[192]{0:T(512)(128)(4,1)S(1)} %copy-done.34, bf16[12,192,4,4,32]{1,4,3,2,0:T(8,128)(2,1)} %convolution_convert_fusion.2), kind=kOutput, calls=%fused_computation.401 | convolution fusion | flops 122093760 | bytes 9474240 | tf_op jit(solution)/shard_map/sub | solution.py:38
  438.4 6.3 %fusion.107 = bf16[12,192,128]{2,1,0:T(8,128)(2,1)} fusion(f32[12,192,128]{2,1,0:T(8,128)S(1)} %reshape.310, f32[12,4,192,192]{2,3,1,0:T(8,128)} %get-tuple-element.27, f32[12,4,192]{2,1,0:T(4,128)S(1)} %get-tuple-element.26, bf16[12,192,4,4,32]{1,4,3,2,0:T(8,128)(2,1)} %convolution_convert_fusion.2, bf16[2,4,32,128]{3,2,1,0:T(8,128)(2,1)S(1)} %copy-done.28), kind=kOutput, calls=%fused_computation.176 | convolution fusion | flops 194641920 | bytes 12861440 | tf_op jit(solution)/shard_map/abhd,hdc->abc/dot_general | solution.py:44
  (186 shorter events, 115.5 us)
Async XLA Ops:
  8.3 35.0 %copy-start.16 = (pred[8,192]{1,0:T(8,128)(4,1)}, pred[8,192]{1,0:T(8,128)(4,1)S(1)}, u32[]{:S(2)}) copy-start(pred[8,192]{1,0:T(8,128)(4,1)S(1)} %broadcast_compare_fusion) | copy-start | bytes 4612
  12.7 26.4 %copy-start = (bf16[8,192,256]{2,1,0:T(8,128)(2,1)S(1)}, bf16[8,192,256]{2,1,0:T(8,128)(2,1)}, u32[]{:S(2)}) copy-start(bf16[8,192,256]{2,1,0:T(8,128)(2,1)} %param.17) | copy-start | bytes 2359300
  43.3 9.2 %copy-start.23 = (bf16[2,8,32,256]{3,2,1,0:T(8,128)(2,1)S(1)}, bf16[2,8,32,256]{3,2,1,0:T(8,128)(2,1)}, u32[]{:S(2)}) copy-start(bf16[2,8,32,256]{3,2,1,0:T(8,128)(2,1)} %param.23) | copy-start | bytes 786436
  60.9 26.5 %copy-start.12 = (bf16[2,256,4,8,32]{1,4,3,2,0:T(8,128)(2,1)S(1)}, bf16[2,256,4,8,32]{1,4,3,2,0:T(8,128)(2,1)}, u32[]{:S(2)}) copy-start(bf16[2,256,4,8,32]{1,4,3,2,0:T(8,128)(2,1)} %param.24) | copy-start | bytes 3145732
  60.9 25.6 %all-to-all-start = ((bf16[8,192,256]{2,0,1:T(8,128)(2,1)}), bf16[8,192,256]{2,0,1:T(8,128)(2,1)S(1)}, u32[]{:S(2)}, u32[]{:S(2)}) async-start(bf16[8,192,256]{2,0,1:T(8,128)(2,1)} %copy.145), calls=%async_computation | async-start | bytes 1572864 | tf_op jit(solution)/shard_map/all_to_all | solution.py:73
  64.8 95.5 %all-gather.5.cloned.1.call-start = ((), (), s32[]{:S(2)}) async-start(), calls=%async_computation.4 | async-start | bytes 1671168 | tf_op jit(solution)/shard_map/all_gather | solution.py:76
  122.7 6.9 %copy-start.31 = (s32[192]{0:T(256)S(1)}, s32[192]{0:T(256)}, u32[]{:S(2)}) copy-start(s32[192]{0:T(256)} %param.20) | copy-start | bytes 2308
  122.7 7.1 %copy-start.1 = (bf16[128,12,256]{2,0,1:T(8,128)(2,1)S(1)}, bf16[128,12,256]{2,0,1:T(8,128)(2,1)}, u32[]{:S(2)}) copy-start(bf16[128,12,256]{2,0,1:T(8,128)(2,1)} %get-tuple-element.21) | copy-start | bytes 2359300
  125.3 33.3 %all-to-all-start.1 = ((bf16[128,12,256]{2,1,0:T(8,128)(2,1)}), bf16[128,12,256]{2,1,0:T(8,128)(2,1)S(1)}, u32[]{:S(2)}, u32[]{:S(2)}) async-start(bf16[128,12,256]{2,1,0:T(8,128)(2,1)} %copy.150), calls=%async_computation.1 | async-start | bytes 2097152 | tf_op jit(solution)/shard_map/all_to_all | solution.py:91
  129.1 172.7 %all-gather.7.cloned.1.call-start = ((), (), s32[]{:S(2)}) async-start(), calls=%async_computation.5 | async-start | bytes 1671168 | tf_op jit(solution)/shard_map/all_gather | solution.py:89
  129.6 88.9 %copy-start.32 = (pred[192]{0:T(512)(128)(4,1)}, pred[192]{0:T(512)(128)(4,1)S(1)}, u32[]{:S(2)}) copy-start(pred[192]{0:T(512)(128)(4,1)S(1)} %broadcast_compare_fusion.1) | copy-start | bytes 580
  131.0 39.8 %copy-start.15 = (bf16[128,12,2,32]{0,3,2,1:T(8,128)(2,1)}, bf16[128,12,2,32]{0,3,2,1:T(8,128)(2,1)S(1)}, u32[]{:S(2)}) copy-start(bf16[128,12,2,32]{0,3,2,1:T(8,128)(2,1)S(1)} %fusion.138) | copy-start | bytes 589828
  170.8 21.6 %copy-start.5 = (bf16[12,192,128]{2,1,0:T(8,128)(2,1)S(1)}, bf16[12,192,128]{2,1,0:T(8,128)(2,1)}, u32[]{:S(2)}) copy-start(bf16[12,192,128]{2,1,0:T(8,128)(2,1)} %param.18) | copy-start | bytes 1769476
  170.8 21.6 %copy-start.21 = (bf16[2,32,32,128]{3,2,1,0:T(8,128)(2,1)S(1)}, bf16[2,32,32,128]{3,2,1,0:T(8,128)(2,1)}, u32[]{:S(2)}) copy-start(bf16[2,32,32,128]{3,2,1,0:T(8,128)(2,1)} %param.27) | copy-start | bytes 1572868
  218.5 9.5 %copy-start.27 = (bf16[2,4,32,128]{3,2,1,0:T(8,128)(2,1)S(1)}, bf16[2,4,32,128]{3,2,1,0:T(8,128)(2,1)}, u32[]{:S(2)}) copy-start(bf16[2,4,32,128]{3,2,1,0:T(8,128)(2,1)} %param.30) | copy-start | bytes 196612
  233.5 6.7 %copy-start.11 = (f32[8,16,12]{0,1,2:T(8,128)S(1)}, f32[8,16,12]{0,1,2:T(8,128)}, u32[]{:S(2)}) copy-start(f32[8,16,12]{0,1,2:T(8,128)} %multiply_reduce_fusion.2) | copy-start | bytes 18436
  234.8 27.1 %all-to-all-start.2 = ((bf16[12,192,128]{2,0,1:T(8,128)(2,1)}), bf16[12,192,128]{2,0,1:T(8,128)(2,1)S(1)}, u32[]{:S(2)}, u32[]{:S(2)}) async-start(bf16[12,192,128]{2,0,1:T(8,128)(2,1)} %copy.159), calls=%async_computation.2 | async-start | bytes 1572864 | tf_op jit(solution)/shard_map/all_to_all | solution.py:81
  287.6 8.0 %copy-start.26 = (bf16[2,4,32,128]{3,2,1,0:T(8,128)(2,1)S(1)}, bf16[2,4,32,128]{3,2,1,0:T(8,128)(2,1)}, u32[]{:S(2)}) copy-start(bf16[2,4,32,128]{3,2,1,0:T(8,128)(2,1)} %param.33) | copy-start | bytes 196612
  344.0 6.9 %copy-start.30 = (bf16[2,128,8]{1,2,0:T(8,128)(2,1)S(1)}, bf16[2,128,8]{1,2,0:T(8,128)(2,1)}, u32[]{:S(2)}) copy-start(bf16[2,128,8]{1,2,0:T(8,128)(2,1)} %param.21) | copy-start | bytes 12292
  345.3 57.4 %all-to-all-start.3 = ((bf16[192,12,128]{2,1,0:T(8,128)(2,1)}), bf16[192,12,128]{2,1,0:T(8,128)(2,1)S(1)}, u32[]{:S(2)}, u32[]{:S(2)}) async-start(bf16[192,12,128]{2,1,0:T(8,128)(2,1)} %copy.173), calls=%async_computation.3 | async-start | bytes 1572864 | tf_op jit(solution)/shard_map/all_to_all | solution.py:96
  350.9 34.0 %copy-start.17 = (pred[8,192]{1,0:T(8,128)(4,1)S(1)}, pred[8,192]{1,0:T(8,128)(4,1)}, u32[]{:S(2)}) copy-start(pred[8,192]{1,0:T(8,128)(4,1)} %copy-done.16) | copy-start | bytes 4612
  384.9 9.8 %copy-start.6 = (f32[8,16,12,256]{3,0,2,1:T(8,128)S(1)}, f32[8,16,12,256]{3,0,2,1:T(8,128)}, u32[]{:S(2)}) copy-start(f32[8,16,12,256]{3,0,2,1:T(8,128)} %copy.152) | copy-start | bytes 4718596
  384.9 9.8 %copy-start.24 = (bf16[2,8,32,256]{3,2,1,0:T(8,128)(2,1)S(1)}, bf16[2,8,32,256]{3,2,1,0:T(8,128)(2,1)}, u32[]{:S(2)}) copy-start(bf16[2,8,32,256]{3,2,1,0:T(8,128)(2,1)} %param.23) | copy-start | bytes 786436
  428.7 9.7 %copy-start.28 = (bf16[2,4,32,128]{3,2,1,0:T(8,128)(2,1)S(1)}, bf16[2,4,32,128]{3,2,1,0:T(8,128)(2,1)}, u32[]{:S(2)}) copy-start(bf16[2,4,32,128]{3,2,1,0:T(8,128)(2,1)} %param.30) | copy-start | bytes 196612
  (17 other events, 55.3 us)
Sparse Core Ops, SparseCore 0:
  108.6 41.3 all-gather.4
  151.6 31.5 all-gather.6
where the time goes:
time: 461 us; the launch traced here: 452 us
  matrix products  157 us (34%)
  blocking collectives  122 us (26%)
  waiting for transfers between devices  64.4 us (14%)
  local copies, waits for them, and re-layouts  44.9 us (10%)
  other arithmetic  30 us (7%)
  starting transfers between devices  18.6 us (4%)
  between operations  15.1 us (3%)
    sub x6, matrix products, gated_attention(): attn_probs = jax.nn.softmax(logits, axis=-1).astype(jnp.bfloat16)  55.6 us
    dot_general x8, matrix products, gated_attention(): jnp.einsum('abhd,hdc->abc', gated, w_out, preferred_element_type=jnp.floa...  47.9 us
    all_gather x1, blocking collectives, local_step(): lax.all_gather(pair_bias(layer_norm(pair_blk), w_row_bias[1], 'ijc,ch->hi...  31.7 us
    all_to_all x1, waiting for transfers between devices, local_step(): value_a7 = lax.all_to_all(value_a7, 'dap', 0, 1, tiled=True)  26.9 us
    all_gather x1, blocking collectives, local_step(): lax.all_gather(pair_bias(layer_norm(pair_blk), w_row_bias[0], 'ijc,ch->hi...  24.8 us
    dot_general x8, matrix products, gated_attention(): jnp.einsum('abc,cfhd->abfhd', x_ln, w_in, preferred_element_type=jnp.floa...  21.8 us
    convert_element_type x1, local copies, waits for them, and re-layouts, opm_update(): jnp.einsum('sip,sjq->ijpq', left, right, preferred_element_type=jnp.float32)  21.6 us
    all_to_all x1, waiting for transfers between devices, local_step(): value_a7 = lax.all_to_all(value_a7, 'dap', 1, 0, tiled=True)  21.3 us
  transfers between devices with their start and end apart: 6, of which 3 were waited for; matrix products, arithmetic and copies ran while one was open for 29% of the time, Pallas kernels for 0%

commit v1 on v0

v1 whole, which is shorter than its diff:
```python
import functools

import jax
import jax.numpy as jnp
from jax import lax
from jax.experimental import pallas as pl
from jax.experimental.pallas import tpu as pltpu
from jax.sharding import PartitionSpec as P

F32 = jnp.float32
BF16 = jnp.bfloat16
LOG2E = 1.4426950408889634
NEG = -1e9 * LOG2E
HEAD = 32
INTERPRET = False


def dot(lhs, rhs, lc, rc):
    return lax.dot_general(lhs, rhs, (((lc,), (rc,)), ((), ())), preferred_element_type=F32)


def layer_norm(x):
    mean = jnp.mean(x, axis=-1, keepdims=True)
    cen = x - mean
    var = jnp.mean(cen * cen, axis=-1, keepdims=True)
    return (cen * lax.rsqrt(var + 1e-5)).astype(BF16)


def attention(x, wt, wk, wo, bias, mask2d, kcol):
    length = x.shape[0]
    width = wk.shape[1]
    xl = layer_norm(x)
    t = dot(wt, xl, 1, 1).astype(BF16)
    k = dot(xl, wk, 1, 0)
    if kcol is not None:
        k = k * kcol
    k = k.astype(BF16)
    outs = []
    for h in range(width // HEAD):
        grp, r = h // 4, h % 4
        parts = [t[HEAD * h:HEAD * h + HEAD]]
        if r > 0:
            parts.insert(0, jnp.zeros((HEAD * r, length), BF16))
        if r < 3:
            parts.append(jnp.zeros((HEAD * (3 - r), length), BF16))
        qh = jnp.concatenate(parts, axis=0)
        s = dot(k[:, 128 * grp:128 * grp + 128], qh, 1, 0) * (HEAD ** -0.5 * LOG2E)
        if bias is not None:
            s = s + bias[h]
        if mask2d is not None:
            s = jnp.where(mask2d > 0, s, NEG)
        top = jnp.max(s, axis=0, keepdims=True)
        e = jnp.exp2(s - top)
        den = jnp.sum(e, axis=0, keepdims=True)
        o = dot(t[width + HEAD * h:width + HEAD * h + HEAD], e.astype(BF16), 1, 0)
        gate = jax.nn.sigmoid(t[2 * width + HEAD * h:2 * width + HEAD * h + HEAD].astype(F32))
        outs.append((o * (1.0 / den) * gate).astype(BF16))
    return dot(jnp.concatenate(outs, axis=0), wo, 0, 0)


def residual(x, update):
    return (x + update).astype(BF16)


def spread(row, length):
    return jnp.broadcast_to(row, (length, length)).T


def stage(stg, pair, first, second, ndev):
    rows = first.shape[0] // ndev
    off = pl.multiple_of(2 * rows * pair, 8)
    for d in range(ndev):
        both = jnp.concatenate([first[rows * d:rows * d + rows], second[rows * d:rows * d + rows]], axis=0)
        stg[d, pl.ds(off, 2 * rows), :] = both.astype(BF16)


def fill(work, ref):
    for t in range(work.shape[0]):
        work[t] = ref[..., 128 * t:128 * t + 128].astype(F32).reshape(work.shape[1:])


def take(work, start, count, stride):
    return jnp.concatenate([work.at[t][pl.ds(start, count, stride=stride), :] for t in range(work.shape[0])], axis=1)


def bias_pieces(load, count, wb, piece):
    def body(b, _):
        zl = layer_norm(load(b))
        piece[b] = dot(wb[...], zl, 1, 1).astype(BF16)
        return 0
    lax.fori_loop(0, count, body, 0)


def spread_bias(gath, gf, bias, transpose, mask_row):
    length, heads = gath.shape[0], gath.shape[1]
    gf[...] = gath[...].astype(F32)
    keep = None if mask_row is None else spread(mask_row, length)
    for h in range(heads):
        value = gf[:, h, :]
        if transpose:
            value = value.T
        value = value * LOG2E
        if keep is not None:
            value = jnp.where(keep > 0, value, NEG)
        bias[h] = value


def run(body, outs, scratch, *args):
    return pl.pallas_call(
        body,
        out_shape=[jax.ShapeDtypeStruct(s, d) for s, d in outs],
        in_specs=[pl.BlockSpec(memory_space=pltpu.VMEM)] * len(args),
        out_specs=[pl.BlockSpec(memory_space=pltpu.VMEM)] * len(outs),
        scratch_shapes=[pltpu.VMEM(s, d) for s, d in scratch],
        interpret=INTERPRET,
        compiler_params=pltpu.CompilerParams(vmem_limit_bytes=56 * 2**20),
    )(*args)


def solution(mesh):
    nd = mesh.shape['dap']

    def local_step(m, z, msa_mask, res_mask, w_row_bias, w_row_in, w_row_out, w_col_in, w_col_out, w_opm_in, w_opm_out, w_ts_bias, w_ts_in, w_ts_out, w_te_bias, w_te_in, w_te_out):
        me = lax.axis_index('dap')
        sl, nr, cm = m.shape
        rl, _, cz = z.shape
        ns = sl * nd
        hm, ht = w_row_bias.shape[2], w_ts_bias.shape[2]
        wm, wz = hm * HEAD, ht * HEAD
        od = w_opm_in.shape[3]

        maskf = msa_mask.astype(F32)
        mask_seq = lax.dynamic_slice_in_dim(maskf, me * sl, sl, 0)
        mask_col = lax.dynamic_slice_in_dim(maskf, me * rl, rl, 1).T
        mask_b = msa_mask.astype(BF16)
        mask_r = res_mask.astype(F32)[None, :]

        def split(w, width):
            c = w.shape[1]
            w = w.reshape(2, c, 4, width)
            wt = jnp.stack([w[:, :, 0], w[:, :, 2], w[:, :, 3]], axis=1)
            return wt.transpose(0, 1, 3, 2).reshape(2, 3 * width, c), w[:, :, 1]

        row_t, row_k = split(w_row_in, wm)
        col_t, col_k = split(w_col_in, wm)
        ts_t, ts_k = split(w_ts_in, wz)
        te_t, te_k = split(w_te_in, wz)
        row_o = w_row_out.reshape(2, wm, cm)
        col_o = w_col_out.reshape(2, wm, cm)
        ts_o = w_ts_out.reshape(2, wz, cz)
        te_o = w_te_out.reshape(2, wz, cz)
        row_b = w_row_bias.transpose(0, 2, 1)
        ts_b = w_ts_bias.transpose(0, 2, 1)
        te_b = w_te_bias.transpose(0, 2, 1)
        opm_i = w_opm_in.reshape(2, cm, 2 * od).transpose(0, 2, 1)
        opm_o = jnp.stack([w_opm_out[0].transpose(2, 1, 0), w_opm_out[1].transpose(2, 0, 1)]).reshape(2, cz, od * od)

        gather = lambda v: lax.all_gather(v, 'dap', axis=0, tiled=True)
        swap = lambda v: lax.all_to_all(v, 'dap', 0, 0, tiled=True)

        def bias_kernel(z_ref, wb, piece):
            bias_pieces(lambda b: z_ref[b].astype(F32), rl, wb, piece)

        def bias_call(zz, wb):
            return run(bias_kernel, [((rl, wb.shape[0], nr), BF16)], [], zz, wb)[0]

        def row_kernel(transpose, staged, m_ref, g_ref, mask_ref, wt, wk, wo, out_ref, gf, bias, work):
            spread_bias(g_ref, gf, bias, transpose, None)
            if not staged:
                fill(work, m_ref)

            def one(s):
                x = m_ref[s].astype(F32) if staged else take(work, s, nr, sl)
                keep = spread(mask_ref[pl.ds(s, 1), :], nr)
                return residual(x, attention(x, wt[...], wk[...], wo[...], bias, keep, None))

            def body(t, _):
                pair = [one(2 * t), one(2 * t + 1)]
                if staged:
                    stage(out_ref, t, pair[0].astype(F32), pair[1].astype(F32), nd)
                else:
                    out_ref[2 * t], out_ref[2 * t + 1] = pair
                return 0
            lax.fori_loop(0, sl // 2, body, 0)

        def row_call(mm, g, b, transpose, staged):
            rows = sl * rl
            out = (nd, rows, cm) if staged else (sl, nr, cm)
            work = (cm // 128, nd * rows, 128)
            return run(functools.partial(row_kernel, transpose, staged), [(out, BF16)],
                       [((nr, hm, nr), F32), ((hm, nr, nr), F32), (work, F32)],
                       mm, g, mask_seq, row_t[b], row_k[b], row_o[b])[0]

        def col_kernel(b, r_ref, mask_ref, wt, wk, wo, wi, new_ref, loc_ref, gat_ref, *scratch):
            work, = scratch
            if b == 0:
                fill(work, r_ref)

            def one(i):
                x = take(work, i, ns, rl) if b == 0 else r_ref[i].astype(F32)
                row = mask_ref[pl.ds(i, 1), :]
                new = residual(x, attention(x, wt[...], wk[...], wo[...], None, spread(row, ns), None))
                newf = new.astype(F32)
                if b == 0:
                    new_ref[i] = new
                ac = (dot(wi[...], layer_norm(newf), 1, 1) * row).astype(BF16)
                a, c = ac[:od], ac[od:]
                loc_ref[i] = a if b == 0 else c
                gat_ref[i] = c if b == 0 else a
                return newf

            def body(t, _):
                first, second = one(2 * t), one(2 * t + 1)
                if b == 1:
                    stage(new_ref, t, first, second, nd)
                return 0
            lax.fori_loop(0, rl // 2, body, 0)

        def col_call(r, b):
            rows = sl * rl
            out = (rl, ns, cm) if b == 0 else (nd, rows, cm)
            work = (cm // 128, nd * rows, 128)
            return run(functools.partial(col_kernel, b), [(out, BF16), ((rl, od, ns), BF16), ((rl, od, ns), BF16)],
                       [(work, F32)], r, mask_col, col_t[b], col_k[b], col_o[b], opm_i[b])

        def opm_kernel(z_ref, loc_ref, gat_ref, mc_ref, mask_ref, w_ref, wb, out_ref, piece, gf, xs):
            gf[...] = gat_ref[...].astype(F32).reshape(gf.shape)
            loc = loc_ref[...].reshape(rl * od, ns)
            norm = dot(mc_ref[...].astype(BF16), mask_ref[...], 1, 0)

            def grow(g, _):
                col = gf[pl.ds(g, nr, stride=od), :].astype(BF16)
                x = dot(loc, col, 1, 1).astype(BF16)
                off = pl.multiple_of(g * od, od)
                for i in range(rl):
                    xs[i, pl.ds(off, od), :] = x[od * i:od * i + od]
                return 0
            lax.fori_loop(0, od, grow, 0)
            for i in range(rl):
                upd = dot(w_ref[...], xs[i], 1, 0) / (1e-3 + norm[i:i + 1])
                new = residual(z_ref[i].astype(F32), upd.T)
                out_ref[i] = new
                piece[i] = dot(wb[...], layer_norm(new.astype(F32)), 1, 1).astype(BF16)

        def opm_call(zz, loc, gat, b, wb):
            return run(opm_kernel, [((rl, nr, cz), BF16), ((rl, ht, nr), BF16)],
                       [((nr * od, ns), F32), ((rl, od * od, nr), BF16)],
                       zz, loc, gat, mask_col, mask_b, opm_o[b], wb)

        def tri_kernel(staged, z_ref, g_ref, mask_ref, wt, wk, wo, out_ref, gf, bias, work, kc):
            spread_bias(g_ref, gf, bias, True, mask_ref[...])
            kc[...] = jnp.broadcast_to(mask_ref[...], (wz, nr)).T

            def one(b):
                x = z_ref[b].astype(F32)
                return residual(x, attention(x, wt[...], wk[...], wo[...], bias, None, kc[...]))

            def body(t, _):
                pair = [one(2 * t), one(2 * t + 1)]
                if staged:
                    stage(out_ref, t, pair[0].astype(F32), pair[1].astype(F32), nd)
                else:
                    out_ref[2 * t], out_ref[2 * t + 1] = pair
                return 0
            lax.fori_loop(0, rl // 2, body, 0)

        def tri_call(zz, g, wt, wk, wo, staged):
            out = (nd, rl * rl, cz) if staged else (rl, nr, cz)
            return run(functools.partial(tri_kernel, staged), [(out, BF16)],
                       [((nr, ht, nr), F32), ((ht, nr, nr), F32), ((nd, rl * rl, cz), F32), ((nr, wz), F32)],
                       zz, g, mask_r, wt, wk, wo)[0]

        def turn_kernel(r_ref, wb, out_ref, piece, work):
            work[...] = r_ref[...].astype(F32).reshape(work.shape)

            def body(b, _):
                x = work[pl.ds(b, nr, stride=rl), :]
                out_ref[b] = x.astype(BF16)
                piece[b] = dot(wb[...], layer_norm(x), 1, 1).astype(BF16)
                return 0
            lax.fori_loop(0, rl, body, 0)

        def turn_call(r, wb):
            return run(turn_kernel, [((rl, nr, cz), BF16), ((rl, ht, nr), BF16)], [((nr * rl, cz), F32)], r, wb)

        g = gather(bias_call(z, row_b[0]))
        r = swap(row_call(m, g, 0, True, True))
        m, loc, gat = col_call(r, 0)
        r2, loc2, gat2 = col_call(m, 1)
        z, piece = opm_call(z, loc, gather(gat), 0, ts_b[0])
        rz = swap(tri_call(z, gather(piece), ts_t[0], ts_k[0], ts_o[0], True))
        z, piece = turn_call(rz, te_b[0])
        z = tri_call(z, gather(piece), te_t[0], te_k[0], te_o[0], False)
        g = gather(bias_call(z, row_b[1]))
        z, piece = opm_call(z, loc2, gather(gat2), 1, te_b[1])
        m = row_call(swap(r2), g, 1, False, False)
        rz = swap(tri_call(z, gather(piece), te_t[1], te_k[1], te_o[1], True))
        z, piece = turn_call(rz, ts_b[1])
        z = tri_call(z, gather(piece), ts_t[1], ts_k[1], ts_o[1], False)
        return m, z

    in_specs = (P(('data', 'dap')), P(('data', 'dap')), P('data'), P('data')) + (P(),) * 13
    out_specs = (P(('data', 'dap')), P(('data', 'dap')))
    return jax.shard_map(local_step, mesh=mesh, in_specs=in_specs, out_specs=out_specs, check_vma=False)
```

time: 461 us -> 444 us (0.963); the launches traced: 452 us -> 443 us
  Pallas kernels: 0 us -> 232 us
  matrix products: 157 us -> 0 us
  waiting for transfers between devices: 64.4 us -> 18.2 us
  other arithmetic: 30 us -> 1.46 us
  local copies, waits for them, and re-layouts: 44.9 us -> 22.2 us
  blocking collectives: 122 us -> 141 us
    pallas_call x0 -> x14, Pallas kernels: none -> 232 us  [run(): pl.pallas_call(body, out_shape=[jax.ShapeDtypeStruct(s, d) for s, d in ou...]
    dot_general x30 -> x0, matrix products: 102 us -> none  [the longest x8 47.9 us: gated_attention(): jnp.einsum('abhd,hdc->abc', gated, w_out, preferred_element_type=jnp.floa...]
    sub x6 -> x0, matrix products: 55.6 us -> none  [gated_attention(): attn_probs = jax.nn.softmax(logits, axis=-1).astype(jnp.bfloat16)]
    all_to_all x4 -> x3, waiting for transfers between devices: 64.3 us -> 17.1 us  [local_step(): swap = lambda v: lax.all_to_all(v, 'dap', 0, 0, tiled=True)]
    convert_element_type x25 -> x0, local copies, waits for them, and re-layouts: 39.5 us -> none  [the longest x1 21.6 us: opm_update(): jnp.einsum('sip,sjq->ijpq', left, right, preferred_element_type=jnp.float32)]
    all_to_all x0 -> x1, blocking collectives: none -> 24.3 us  [local_step(): swap = lambda v: lax.all_to_all(v, 'dap', 0, 0, tiled=True)]
    sub x2 -> x0, other arithmetic: 13.4 us -> none  [gated_attention(): attn_probs = jax.nn.softmax(logits, axis=-1).astype(jnp.bfloat16)]
    reduce_sum x17 -> x0, other arithmetic: 13.1 us -> none  [the longest x11 9.76 us: layer_norm(): row_var = jnp.mean(centered * centered, axis=-1, keepdims=True)]
  transfers between devices with their start and end apart: 6 -> 5, of which waited for: 3 -> 2; matrix products, arithmetic and copies ran while one was open for 29% -> 3% of each run, Pallas kernels for 0% -> 35%
where the time goes in v1:
time: 444 us; the launch traced here: 443 us
  Pallas kernels  232 us (52%)
  blocking collectives  141 us (32%)
  local copies, waits for them, and re-layouts  22.2 us (5%)
  waiting for transfers between devices  18.2 us (4%)
  between operations  14.3 us (3%)
  starting transfers between devices  14 us (3%)
    pallas_call x14, Pallas kernels, run(): pl.pallas_call(body, out_shape=[jax.ShapeDtypeStruct(s, d) for s, d in ou...  232 us
    all_gather x6, blocking collectives, local_step(): gather = lambda v: lax.all_gather(v, 'dap', axis=0, tiled=True)  117 us
    all_to_all x1, blocking collectives, local_step(): swap = lambda v: lax.all_to_all(v, 'dap', 0, 0, tiled=True)  24.3 us
    all_to_all x3, waiting for transfers between devices, local_step(): swap = lambda v: lax.all_to_all(v, 'dap', 0, 0, tiled=True)  17.1 us
    all_to_all x3, starting transfers between devices, local_step(): swap = lambda v: lax.all_to_all(v, 'dap', 0, 0, tiled=True)  13.7 us
  transfers between devices with their start and end apart: 5, of which 2 were waited for; matrix products, arithmetic and copies ran while one was open for 3% of the time, Pallas kernels for 35%

profile of v1, /device:TPU:21, one launch (start us, length us, event | category | flops | bytes accessed | tf_op | source)
XLA Modules:
  0.0 443.2 jit_solution(11224312195030157681)
XLA Ops:
  10.0 6.1 %shard_map.176 = bf16[12,8,192]{2,1,0:T(8,128)(2,1)} custom-call(bf16[12,192,128]{2,1,0:T(8,128)(2,1)} %z_ref.3, bf16[8,128]{1,0:T(8,128)(2,1)} %get-tuple-element.71.wb), custom_call_target="tpu_custom_call" | custom-call | tf_op jit(solution)/shard_map/pallas_call | solution.py:109
  16.1 24.8 %all_gather.24.g_ref = bf16[192,8,192]{2,1,0:T(8,128)(2,1)} all-gather(bf16[12,8,192]{2,1,0:T(8,128)(2,1)} %shard_map.176), channel_id=1, replica_groups=mesh['data'=4,'dap'=16] {'dap'}, dimensions={0}, use_global_device_ids=true | all-gather | bytes 626688 | tf_op jit(solution)/shard_map/all_gather | solution.py:158
  44.2 20.7 %shard_map.177 = bf16[16,96,256]{2,1,0:T(8,128)(2,1)} custom-call(bf16[8,192,256]{2,1,0:T(8,128)(2,1)} %m_ref.1, bf16[192,8,192]{2,1,0:T(8,128)(2,1)} %all_gather.24.g_ref, f32[8,192]{1,0:T(8,128)} %copy.61.mask_ref, bf16[768,256]{1,0:T(8,128)(2,1)} %bitcast.114, bf16[256,256]{1,0:T(8,128)(2,1)} %bitcast.124, bf16[256,256]{1,0:T(8,128)(2,1)} %bitcast.128), custom_call_target="tpu_custom_call" | custom-call | tf_op jit(solution)/shard_map/pallas_call | solution.py:109
  73.3 17.1 %all-to-all-done.r_ref = bf16[16,96,256]{2,1,0:T(8,128)(2,1)S(1)} async-done(((bf16[16,96,256]{2,1,0:T(8,128)(2,1)}), bf16[16,96,256]{2,1,0:T(8,128)(2,1)S(1)}, u32[]{:S(2)}, u32[]{:S(2)}) %all-to-all-start) | async-done | bytes 786464 | tf_op jit(solution)/shard_map/all_to_all | solution.py:159
  91.3 27.0 %shard_map.178 = (bf16[12,128,256]{2,1,0:T(8,128)(2,1)}, bf16[12,32,128]{2,1,0:T(8,128)(2,1)}, bf16[12,32,128]{2,1,0:T(8,128)(2,1)}) custom-call(bf16[16,96,256]{2,1,0:T(8,128)(2,1)} %copy-done, f32[12,128]{1,0:T(8,128)} %dynamic-slice_bitcast_fusion.mask_ref.mc_ref, bf16[768,256]{1,0:T(8,128)(2,1)} %bitcast.112, bf16[256,256]{1,0:T(8,128)(2,1)} %bitcast.121, ...), custom_call_target="tpu_custom_call" | custom-call | tf_op jit(solution)/shard_map/pallas_call | solution.py:109
  123.7 26.8 %shard_map.179 = (bf16[16,96,256]{2,1,0:T(8,128)(2,1)}, bf16[12,32,128]{2,1,0:T(8,128)(2,1)}, bf16[12,32,128]{2,1,0:T(8,128)(2,1)}) custom-call(bf16[12,128,256]{2,1,0:T(8,128)(2,1)} %get-tuple-element.16.r_ref, f32[12,128]{1,0:T(8,128)} %dynamic-slice_bitcast_fusion.mask_ref.mc_ref, bf16[768,256]{1,0:T(8,128)(2,1)} %bitcast.111, ...), custom_call_target="tpu_custom_call" | custom-call | tf_op jit(solution)/shard_map/pallas_call | solution.py:109
  152.2 19.3 %shard_map.180 = (bf16[12,192,128]{2,1,0:T(8,128)(2,1)}, bf16[12,4,192]{2,1,0:T(4,128)(2,1)}) custom-call(bf16[12,192,128]{2,1,0:T(8,128)(2,1)} %z_ref.3, bf16[12,32,128]{2,1,0:T(8,128)(2,1)} %get-tuple-element.18.loc_ref, bf16[192,32,128]{2,1,0:T(8,128)(2,1)} %all-gather.3.cloned.1.call-done.gat_ref, f32[12,128]{1,0:T(8,128)} %dynamic-slice_bitcast_fusion.mask_ref.mc_ref, ...), custom_call_target="tpu_custom_call" | custom-call | tf_op jit(solution)/shard_map/pallas_call | solution.py:109
  171.4 17.2 %all_gather.26.g_ref = bf16[192,4,192]{2,1,0:T(4,128)(2,1)} all-gather(bf16[12,4,192]{2,1,0:T(4,128)(2,1)} %get-tuple-element.21), channel_id=1, replica_groups=mesh['data'=4,'dap'=16] {'dap'}, dimensions={0}, use_global_device_ids=true | all-gather | bytes 313344 | tf_op jit(solution)/shard_map/all_gather | solution.py:158
  188.7 18.3 %shard_map.181 = bf16[16,144,128]{2,1,0:T(8,128)(2,1)} custom-call(bf16[12,192,128]{2,1,0:T(8,128)(2,1)} %get-tuple-element.20.z_ref, bf16[192,4,192]{2,1,0:T(4,128)(2,1)} %all_gather.26.g_ref, f32[1,192]{1,0:T(1,128)} %bitcast.146, bf16[384,128]{1,0:T(8,128)(2,1)} %bitcast.131, bf16[128,128]{1,0:T(8,128)(2,1)} %bitcast.137, bf16[128,128]{1,0:T(8,128)(2,1)} %bitcast.142), custom_call_target="tpu_custom_call" | custom-call | tf_op jit(solution)/shard_map/pallas_call | solution.py:109
  207.0 24.3 %all_to_all.20.r_ref = bf16[16,144,128]{2,1,0:T(8,128)(2,1)} all-to-all(bf16[16,144,128]{2,1,0:T(8,128)(2,1)} %shard_map.181), channel_id=1, replica_groups=mesh['data'=4,'dap'=16] {'dap'}, dimensions={0} | all-to-all | bytes 1179648 | tf_op jit(solution)/shard_map/all_to_all | solution.py:159
  231.2 3.9 all-to-all-start.1
  239.4 6.2 %shard_map.182 = (bf16[12,192,128]{2,1,0:T(8,128)(2,1)}, bf16[12,4,192]{2,1,0:T(4,128)(2,1)}) custom-call(bf16[16,144,128]{2,1,0:T(8,128)(2,1)} %all_to_all.20.r_ref, bf16[4,128]{1,0:T(4,128)(2,1)} %get-tuple-element.75.wb), custom_call_target="tpu_custom_call" | custom-call | tf_op jit(solution)/shard_map/pallas_call | solution.py:109
  245.6 21.5 %all_gather.27.g_ref = bf16[192,4,192]{2,1,0:T(4,128)(2,1)} all-gather(bf16[12,4,192]{2,1,0:T(4,128)(2,1)} %get-tuple-element.23), channel_id=1, replica_groups=mesh['data'=4,'dap'=16] {'dap'}, dimensions={0}, use_global_device_ids=true | all-gather | bytes 313344 | tf_op jit(solution)/shard_map/all_gather | solution.py:158
  267.1 18.3 %shard_map.183.z_ref = bf16[12,192,128]{2,1,0:T(8,128)(2,1)} custom-call(bf16[12,192,128]{2,1,0:T(8,128)(2,1)} %get-tuple-element.22.z_ref, bf16[192,4,192]{2,1,0:T(4,128)(2,1)} %all_gather.27.g_ref, f32[1,192]{1,0:T(1,128)} %bitcast.147, bf16[384,128]{1,0:T(8,128)(2,1)} %bitcast.132, bf16[128,128]{1,0:T(8,128)(2,1)} %bitcast.140, bf16[128,128]{1,0:T(8,128)(2,1)} %bitcast.144), custom_call_target="tpu_custom_call" | custom-call | tf_op jit(solution)/shard_map/pallas_call | solution.py:109
  285.4 19.3 %shard_map.186 = (bf16[12,192,128]{2,1,0:T(8,128)(2,1)}, bf16[12,4,192]{2,1,0:T(4,128)(2,1)}) custom-call(bf16[12,192,128]{2,1,0:T(8,128)(2,1)} %shard_map.183.z_ref, bf16[12,32,128]{2,1,0:T(8,128)(2,1)} %get-tuple-element.24.loc_ref, bf16[192,32,128]{2,1,0:T(8,128)(2,1)} %all-gather.5.cloned.1.call-done.gat_ref, ...), custom_call_target="tpu_custom_call" | custom-call | tf_op jit(solution)/shard_map/pallas_call | solution.py:109
  304.6 16.0 %all_gather.30.g_ref = bf16[192,4,192]{2,1,0:T(4,128)(2,1)} all-gather(bf16[12,4,192]{2,1,0:T(4,128)(2,1)} %get-tuple-element.27), channel_id=1, replica_groups=mesh['data'=4,'dap'=16] {'dap'}, dimensions={0}, use_global_device_ids=true | all-gather | bytes 313344 | tf_op jit(solution)/shard_map/all_gather | solution.py:158
  320.6 18.3 %shard_map.187 = bf16[16,144,128]{2,1,0:T(8,128)(2,1)} custom-call(bf16[12,192,128]{2,1,0:T(8,128)(2,1)} %get-tuple-element.26.z_ref, bf16[192,4,192]{2,1,0:T(4,128)(2,1)} %all_gather.30.g_ref, f32[1,192]{1,0:T(1,128)} %bitcast.148, bf16[384,128]{1,0:T(8,128)(2,1)} %bitcast.130, bf16[128,128]{1,0:T(8,128)(2,1)} %bitcast.138, bf16[128,128]{1,0:T(8,128)(2,1)} %bitcast.143), custom_call_target="tpu_custom_call" | custom-call | tf_op jit(solution)/shard_map/pallas_call | solution.py:109
  338.9 6.1 %all-to-all-start.3 = ((bf16[16,144,128]{2,1,0:T(8,128)(2,1)}), bf16[16,144,128]{2,1,0:T(8,128)(2,1)S(1)}, u32[]{:S(2)}, u32[]{:S(2)}) async-start(bf16[16,144,128]{2,1,0:T(8,128)(2,1)} %shard_map.187), calls=%async_computation.3 | async-start | bytes 1179648 | tf_op jit(solution)/shard_map/all_to_all | solution.py:159
  346.4 6.1 %shard_map.184 = bf16[12,8,192]{2,1,0:T(8,128)(2,1)} custom-call(bf16[12,192,128]{2,1,0:T(8,128)(2,1)} %shard_map.183.z_ref, bf16[8,128]{1,0:T(8,128)(2,1)} %get-tuple-element.70.wb), custom_call_target="tpu_custom_call" | custom-call | tf_op jit(solution)/shard_map/pallas_call | solution.py:109
  352.6 21.6 %all_gather.28.g_ref = bf16[192,8,192]{2,1,0:T(8,128)(2,1)} all-gather(bf16[12,8,192]{2,1,0:T(8,128)(2,1)} %shard_map.184), channel_id=1, replica_groups=mesh['data'=4,'dap'=16] {'dap'}, dimensions={0}, use_global_device_ids=true | all-gather | bytes 626688 | tf_op jit(solution)/shard_map/all_gather | solution.py:158
  374.2 21.3 %shard_map.185 = bf16[8,192,256]{2,1,0:T(8,128)(2,1)} custom-call(bf16[16,96,256]{2,1,0:T(8,128)(2,1)} %copy-done.1, bf16[192,8,192]{2,1,0:T(8,128)(2,1)} %all_gather.28.g_ref, f32[8,192]{1,0:T(8,128)} %copy.61.mask_ref, bf16[768,256]{1,0:T(8,128)(2,1)} %bitcast.113, bf16[256,256]{1,0:T(8,128)(2,1)} %bitcast.123, bf16[256,256]{1,0:T(8,128)(2,1)} %bitcast.125), custom_call_target="tpu_custom_call" | custom-call | tf_op jit(solution)/shard_map/pallas_call | solution.py:109
  396.3 6.2 %shard_map.188 = (bf16[12,192,128]{2,1,0:T(8,128)(2,1)}, bf16[12,4,192]{2,1,0:T(4,128)(2,1)}) custom-call(bf16[16,144,128]{2,1,0:T(8,128)(2,1)} %copy-done.2, bf16[4,128]{1,0:T(4,128)(2,1)} %get-tuple-element.72.wb), custom_call_target="tpu_custom_call" | custom-call | tf_op jit(solution)/shard_map/pallas_call | solution.py:109
  402.5 15.5 %all_gather.31.g_ref = bf16[192,4,192]{2,1,0:T(4,128)(2,1)} all-gather(bf16[12,4,192]{2,1,0:T(4,128)(2,1)} %get-tuple-element.29), channel_id=1, replica_groups=mesh['data'=4,'dap'=16] {'dap'}, dimensions={0}, use_global_device_ids=true | all-gather | bytes 313344 | tf_op jit(solution)/shard_map/all_gather | solution.py:158
  418.0 18.3 %shard_map.189 = bf16[12,192,128]{2,1,0:T(8,128)(2,1)} custom-call(bf16[12,192,128]{2,1,0:T(8,128)(2,1)} %get-tuple-element.28.z_ref, bf16[192,4,192]{2,1,0:T(4,128)(2,1)} %all_gather.31.g_ref, f32[1,192]{1,0:T(1,128)} %bitcast.149, bf16[384,128]{1,0:T(8,128)(2,1)} %bitcast.129, bf16[128,128]{1,0:T(8,128)(2,1)} %bitcast.139, bf16[128,128]{1,0:T(8,128)(2,1)} %bitcast.141), custom_call_target="tpu_custom_call" | custom-call | tf_op jit(solution)/shard_map/pallas_call | solution.py:109
  (86 shorter events, 28.7 us)
Async XLA Ops:
  7.2 2.2 copy-start.13
  7.2 33.7 %copy-start.5 = (s32[128,192]{0,1:T(8,128)S(1)}, s32[128,192]{0,1:T(8,128)}, u32[]{:S(2)}) copy-start(s32[128,192]{0,1:T(8,128)} %param.19) | copy-start | bytes 294916
  41.7 1.8 copy-start.8
  44.2 24.6 %copy-start.3 = (bf16[2,256,4,8,32]{1,4,3,2,0:T(8,128)(2,1)S(1)}, bf16[2,256,4,8,32]{1,4,3,2,0:T(8,128)(2,1)}, u32[]{:S(2)}) copy-start(bf16[2,256,4,8,32]{1,4,3,2,0:T(8,128)(2,1)} %param.24) | copy-start | bytes 3145732
  64.9 25.5 %all-to-all-start = ((bf16[16,96,256]{2,1,0:T(8,128)(2,1)}), bf16[16,96,256]{2,1,0:T(8,128)(2,1)S(1)}, u32[]{:S(2)}, u32[]{:S(2)}) async-start(bf16[16,96,256]{2,1,0:T(8,128)(2,1)} %shard_map.177), calls=%async_computation | async-start | bytes 1572864 | tf_op jit(solution)/shard_map/all_to_all | solution.py:159
  68.7 83.4 %all-gather.3.cloned.1.call-start = ((), (), s32[]{:S(2)}) async-start(), calls=%async_computation.4 | async-start | bytes 1671168 | tf_op jit(solution)/shard_map/all_gather | solution.py:158
  70.2 0.8 copy-start.10
  70.2 1.5 copy-start.9
  72.4 47.8 %copy-start.4 = (bf16[2,32,32,128]{3,2,1,0:T(8,128)(2,1)S(1)}, bf16[2,32,32,128]{3,2,1,0:T(8,128)(2,1)}, u32[]{:S(2)}) copy-start(bf16[2,32,32,128]{3,2,1,0:T(8,128)(2,1)} %param.27) | copy-start | bytes 1572868
  90.4 0.9 copy-start
  118.3 2.8 copy-start.16
  118.3 3.4 copy-start.6
  118.3 4.2 copy-start.14
  118.3 4.7 %copy-start.11 = (bf16[2,4,32,128]{3,2,1,0:T(8,128)(2,1)S(1)}, bf16[2,4,32,128]{3,2,1,0:T(8,128)(2,1)}, u32[]{:S(2)}) copy-start(bf16[2,4,32,128]{3,2,1,0:T(8,128)(2,1)} %param.30) | copy-start | bytes 196612
  118.4 167.0 %all-gather.5.cloned.1.call-start = ((), (), s32[]{:S(2)}) async-start(), calls=%async_computation.5 | async-start | bytes 1671168 | tf_op jit(solution)/shard_map/all_gather | solution.py:158
  207.0 28.2 %copy-start.7 = (bf16[2,128,4,4,32]{1,4,3,2,0:T(8,128)(2,1)S(1)}, bf16[2,128,4,4,32]{1,4,3,2,0:T(8,128)(2,1)}, u32[]{:S(2)}) copy-start(bf16[2,128,4,4,32]{1,4,3,2,0:T(8,128)(2,1)} %param.32) | copy-start | bytes 786436
  231.2 6.3 %copy-start.15 = (bf16[2,128,4]{1,2,0:T(4,128)(2,1)S(1)}, bf16[2,128,4]{1,2,0:T(4,128)(2,1)}, u32[]{:S(2)}) copy-start(bf16[2,128,4]{1,2,0:T(4,128)(2,1)} %param.31) | copy-start | bytes 6148
  231.2 6.8 %copy-start.12 = (bf16[2,4,32,128]{3,2,1,0:T(8,128)(2,1)S(1)}, bf16[2,4,32,128]{3,2,1,0:T(8,128)(2,1)}, u32[]{:S(2)}) copy-start(bf16[2,4,32,128]{3,2,1,0:T(8,128)(2,1)} %param.33) | copy-start | bytes 196612
  231.2 107.7 %all-to-all-start.1 = ((bf16[16,96,256]{2,1,0:T(8,128)(2,1)}), bf16[16,96,256]{2,1,0:T(8,128)(2,1)S(1)}, u32[]{:S(2)}, u32[]{:S(2)}) async-start(bf16[16,96,256]{2,1,0:T(8,128)(2,1)} %get-tuple-element.17), calls=%async_computation.1 | async-start | bytes 1572864 | tf_op jit(solution)/shard_map/all_to_all | solution.py:159
  338.9 35.3 %copy-start.1 = (bf16[16,96,256]{2,1,0:T(8,128)(2,1)}, bf16[16,96,256]{2,1,0:T(8,128)(2,1)S(1)}, u32[]{:S(2)}) copy-start(bf16[16,96,256]{2,1,0:T(8,128)(2,1)S(1)} %all-to-all-done.1.m_ref) | copy-start | bytes 2359300
  338.9 56.6 %all-to-all-start.3 = ((bf16[16,144,128]{2,1,0:T(8,128)(2,1)}), bf16[16,144,128]{2,1,0:T(8,128)(2,1)S(1)}, u32[]{:S(2)}, u32[]{:S(2)}) async-start(bf16[16,144,128]{2,1,0:T(8,128)(2,1)} %shard_map.187), calls=%async_computation.3 | async-start | bytes 1179648 | tf_op jit(solution)/shard_map/all_to_all | solution.py:159
  395.5 0.8 copy-start.2
Sparse Core Ops, SparseCore 0:
  118.5 33.5 all-gather.2
  153.8 34.3 all-gather.4

commit v2 on v1

v2 whole, which is shorter than its diff:
```python
import functools

import jax
import jax.numpy as jnp
from jax import lax
from jax.experimental import pallas as pl
from jax.experimental.pallas import tpu as pltpu
from jax.sharding import PartitionSpec as P

F32 = jnp.float32
BF16 = jnp.bfloat16
LOG2E = 1.4426950408889634
NEG = -1e9 * LOG2E
HEAD = 32
INTERPRET = False


def dot(lhs, rhs, lc, rc):
    return lax.dot_general(lhs, rhs, (((lc,), (rc,)), ((), ())), preferred_element_type=F32)


def layer_norm(x):
    mean = jnp.mean(x, axis=-1, keepdims=True)
    cen = x - mean
    var = jnp.mean(cen * cen, axis=-1, keepdims=True)
    return (cen * lax.rsqrt(var + 1e-5)).astype(BF16)


def project(xs, wt, wk, t_ref, k_ref, first, kcol):
    xl = [layer_norm(x) for x in xs]
    ts = [dot(wt[...], v, 1, 1) for v in xl]
    ks = [dot(v, wk[...], 1, 0) for v in xl]
    for n, v in enumerate(ts):
        t_ref[first + n] = v.astype(BF16)
    for n, v in enumerate(ks):
        if kcol is not None:
            v = v * kcol
        k_ref[first + n] = v.astype(BF16)


def diagonal(t, base, length):
    cols = []
    for r in range(4):
        parts = [t[base + HEAD * r:base + HEAD * r + HEAD]]
        if r > 0:
            parts.insert(0, jnp.zeros((HEAD * r, length), BF16))
        if r < 3:
            parts.append(jnp.zeros((HEAD * (3 - r), length), BF16))
        cols.append(jnp.concatenate(parts, axis=0))
    return jnp.concatenate(cols, axis=1)


def core(t_ref, k_ref, o_ref, rows, groups, bias, keeps):
    length = k_ref.shape[1]
    width = 128 * groups
    units = [(n, b, g) for n, b in enumerate(rows) for g in range(groups)]
    scores = []
    for n, b, g in units:
        t = t_ref[b, 128 * g:128 * g + 128, :]
        scores.append(dot(k_ref[b, :, 128 * g:128 * g + 128], diagonal(t, 0, length), 1, 0))
    probs = []
    dens = []
    for (n, b, g), s in zip(units, scores):
        s = s * (HEAD ** -0.5 * LOG2E)
        if bias is not None:
            s = s + bias[g]
        if keeps is not None:
            s = jnp.where(keeps[n] > 0, s, NEG)
        e = jnp.exp2(s - jnp.max(s, axis=0, keepdims=True))
        dens.append(jnp.sum(e, axis=0, keepdims=True))
        probs.append(e.astype(BF16))
    outs = [dot(t_ref[b, width + 128 * g:width + 128 * g + 128, :], p, 1, 0) for (n, b, g), p in zip(units, probs)]
    for (n, b, g), o, den in zip(units, outs, dens):
        inv = 1.0 / den
        gate = jax.nn.sigmoid(t_ref[b, 2 * width + 128 * g:2 * width + 128 * g + 128, :].astype(F32))
        parts = []
        for r in range(4):
            lanes = slice(length * r, length * r + length)
            parts.append(o[HEAD * r:HEAD * r + HEAD, lanes] * inv[:, lanes])
        o_ref[b, 128 * g:128 * g + 128, :] = (jnp.concatenate(parts, axis=0) * gate).astype(BF16)


def residual(x, update):
    return (x + update).astype(BF16)


def spread(row, lanes):
    return jnp.broadcast_to(row, (lanes, row.shape[1])).T


def widen(block, lanes):
    return jnp.concatenate([block] * (lanes // 128), axis=1)


def stage(stg, pair, first, second, ndev):
    rows = first.shape[0] // ndev
    off = pl.multiple_of(2 * rows * pair, 8)
    for d in range(ndev):
        both = jnp.concatenate([first[rows * d:rows * d + rows], second[rows * d:rows * d + rows]], axis=0)
        stg[d, pl.ds(off, 2 * rows), :] = both.astype(BF16)


def fill(work, ref):
    for t in range(work.shape[0]):
        work[t] = ref[..., 128 * t:128 * t + 128].astype(F32).reshape(work.shape[1:])


def take(work, start, count, stride):
    return jnp.concatenate([work.at[t][pl.ds(start, count, stride=stride), :] for t in range(work.shape[0])], axis=1)


def bias_pieces(load, count, wb, piece):
    def body(t, _):
        zl = [layer_norm(load(4 * t + n)) for n in range(4)]
        ps = [dot(wb[...], v, 1, 1) for v in zl]
        for n, v in enumerate(ps):
            piece[4 * t + n] = v.astype(BF16)
        return 0
    lax.fori_loop(0, count // 4, body, 0)


def spread_bias(gath, gf, bias, transpose, mask_row):
    length, heads = gath.shape[0], gath.shape[1]
    gf[...] = gath[...].astype(F32)
    keep = None if mask_row is None else widen(spread(mask_row, 128), 4 * length)
    for g in range(heads // 4):
        parts = []
        for r in range(4):
            value = gf[:, 4 * g + r, :]
            parts.append(value.T if transpose else value)
        value = jnp.concatenate(parts, axis=1) * LOG2E
        if keep is not None:
            value = jnp.where(keep > 0, value, NEG)
        bias[g] = value


def run(body, outs, scratch, *args):
    return pl.pallas_call(
        body,
        out_shape=[jax.ShapeDtypeStruct(s, d) for s, d in outs],
        in_specs=[pl.BlockSpec(memory_space=pltpu.VMEM)] * len(args),
        out_specs=[pl.BlockSpec(memory_space=pltpu.VMEM)] * len(outs),
        scratch_shapes=[pltpu.VMEM(s, d) for s, d in scratch],
        interpret=INTERPRET,
        compiler_params=pltpu.CompilerParams(vmem_limit_bytes=56 * 2**20),
    )(*args)


def solution(mesh):
    nd = mesh.shape['dap']

    def local_step(m, z, msa_mask, res_mask, w_row_bias, w_row_in, w_row_out, w_col_in, w_col_out, w_opm_in, w_opm_out, w_ts_bias, w_ts_in, w_ts_out, w_te_bias, w_te_in, w_te_out):
        me = lax.axis_index('dap')
        sl, nr, cm = m.shape
        rl, _, cz = z.shape
        ns = sl * nd
        hm, ht = w_row_bias.shape[2], w_ts_bias.shape[2]
        wm, wz = hm * HEAD, ht * HEAD
        od = w_opm_in.shape[3]

        maskf = msa_mask.astype(F32)
        mask_seq = lax.dynamic_slice_in_dim(maskf, me * sl, sl, 0)
        mask_col = lax.dynamic_slice_in_dim(maskf, me * rl, rl, 1).T
        mask_b = msa_mask.astype(BF16)
        mask_r = res_mask.astype(F32)[None, :]

        def split(w, width):
            c = w.shape[1]
            w = w.reshape(2, c, 4, width)
            wt = jnp.stack([w[:, :, 0], w[:, :, 2], w[:, :, 3]], axis=1)
            return wt.transpose(0, 1, 3, 2).reshape(2, 3 * width, c), w[:, :, 1]

        row_t, row_k = split(w_row_in, wm)
        col_t, col_k = split(w_col_in, wm)
        ts_t, ts_k = split(w_ts_in, wz)
        te_t, te_k = split(w_te_in, wz)
        row_o = w_row_out.reshape(2, wm, cm)
        col_o = w_col_out.reshape(2, wm, cm)
        ts_o = w_ts_out.reshape(2, wz, cz)
        te_o = w_te_out.reshape(2, wz, cz)
        row_b = w_row_bias.transpose(0, 2, 1)
        ts_b = w_ts_bias.transpose(0, 2, 1)
        te_b = w_te_bias.transpose(0, 2, 1)
        opm_i = w_opm_in.reshape(2, cm, 2 * od).transpose(0, 2, 1)
        opm_o = jnp.stack([w_opm_out[0].transpose(2, 1, 0), w_opm_out[1].transpose(2, 0, 1)]).reshape(2, cz, od * od)

        gather = lambda v: lax.all_gather(v, 'dap', axis=0, tiled=True)
        swap = lambda v: lax.all_to_all(v, 'dap', 0, 0, tiled=True)

        def bias_kernel(z_ref, wb, piece):
            bias_pieces(lambda b: z_ref[b].astype(F32), rl, wb, piece)

        def bias_call(zz, wb):
            return run(bias_kernel, [((rl, wb.shape[0], nr), BF16)], [], zz, wb)[0]

        def row_kernel(transpose, staged, m_ref, g_ref, mask_ref, wt, wk, wo, out_ref, gf, bias, work, t_ref, k_ref, o_ref):
            if not staged:
                fill(work, m_ref)

            def load(s):
                return m_ref[s].astype(F32) if staged else take(work, s, nr, sl)

            def first(t, _):
                project([load(2 * t), load(2 * t + 1)], wt, wk, t_ref, k_ref, 2 * t, None)
                return 0
            lax.fori_loop(0, sl // 2, first, 0)
            spread_bias(g_ref, gf, bias, transpose, None)

            def second(s, _):
                keep = widen(spread(mask_ref[pl.ds(s, 1), :], 128), 4 * nr)
                core(t_ref, k_ref, o_ref, [s], hm // 4, bias, [keep])
                return 0
            lax.fori_loop(0, sl, second, 0)

            def third(t, _):
                ups = [dot(o_ref[2 * t + n], wo[...], 0, 0) for n in range(2)]
                pair = [residual(load(2 * t + n), ups[n]) for n in range(2)]
                if staged:
                    stage(out_ref, t, pair[0].astype(F32), pair[1].astype(F32), nd)
                else:
                    out_ref[2 * t], out_ref[2 * t + 1] = pair
                return 0
            lax.fori_loop(0, sl // 2, third, 0)

        def row_call(mm, g, b, transpose, staged):
            rows = sl * rl
            out = (nd, rows, cm) if staged else (sl, nr, cm)
            work = (cm // 128, nd * rows, 128)
            return run(functools.partial(row_kernel, transpose, staged), [(out, BF16)],
                       [((nr, hm, nr), F32), ((hm // 4, nr, 4 * nr), F32), (work, F32),
                        ((sl, 3 * wm, nr), BF16), ((sl, nr, wm), BF16), ((sl, wm, nr), BF16)],
                       mm, g, mask_seq, row_t[b], row_k[b], row_o[b])[0]

        def col_kernel(b, r_ref, mask_ref, wt, wk, wo, wi, new_ref, loc_ref, gat_ref, work, t_ref, k_ref, o_ref):
            if b == 0:
                fill(work, r_ref)

            def load(i):
                return take(work, i, ns, rl) if b == 0 else r_ref[i].astype(F32)

            def first(t, _):
                project([load(4 * t + n) for n in range(4)], wt, wk, t_ref, k_ref, 4 * t, None)
                return 0
            lax.fori_loop(0, rl // 4, first, 0)

            def second(t, _):
                rows = [2 * t, 2 * t + 1]
                keeps = [widen(spread(mask_ref[pl.ds(i, 1), :], 128), 4 * ns) for i in rows]
                core(t_ref, k_ref, o_ref, rows, hm // 4, None, keeps)
                return 0
            lax.fori_loop(0, rl // 2, second, 0)

            def third(t, _):
                rows = [4 * t + n for n in range(4)]
                ups = [dot(o_ref[i], wo[...], 0, 0) for i in rows]
                new = [residual(load(i), u) for i, u in zip(rows, ups)]
                newf = [v.astype(F32) for v in new]
                if b == 0:
                    for i, v in zip(rows, new):
                        new_ref[i] = v
                else:
                    stage(new_ref, 2 * t, newf[0], newf[1], nd)
                    stage(new_ref, 2 * t + 1, newf[2], newf[3], nd)
                ln = [layer_norm(v) for v in newf]
                acs = [dot(wi[...], v, 1, 1) for v in ln]
                for i, v in zip(rows, acs):
                    ac = (v * mask_ref[pl.ds(i, 1), :]).astype(BF16)
                    a, c = ac[:od], ac[od:]
                    loc_ref[i] = a if b == 0 else c
                    gat_ref[i] = c if b == 0 else a
                return 0
            lax.fori_loop(0, rl // 4, third, 0)

        def col_call(r, b):
            rows = sl * rl
            out = (rl, ns, cm) if b == 0 else (nd, rows, cm)
            work = (cm // 128, nd * rows, 128)
            return run(functools.partial(col_kernel, b), [(out, BF16), ((rl, od, ns), BF16), ((rl, od, ns), BF16)],
                       [(work, F32), ((rl, 3 * wm, ns), BF16), ((rl, ns, wm), BF16), ((rl, wm, ns), BF16)], r, mask_col, col_t[b], col_k[b], col_o[b], opm_i[b])

        def opm_kernel(z_ref, loc_ref, gat_ref, mc_ref, mask_ref, w_ref, wb, out_ref, piece, gf, xs, nrm):
            gf[...] = gat_ref[...].astype(F32).reshape(gf.shape)
            nrm[...] = dot(mc_ref[...].astype(BF16), mask_ref[...], 1, 0)

            def grow(t, _):
                loc = loc_ref[...].reshape(rl * od, ns)
                for n in range(4):
                    g = 4 * t + n
                    col = gf[pl.ds(g, nr, stride=od), :].astype(BF16)
                    x = dot(loc, col, 1, 1).astype(BF16)
                    off = pl.multiple_of(g * od, od)
                    for i in range(rl):
                        xs[i, pl.ds(off, od), :] = x[od * i:od * i + od]
                return 0
            lax.fori_loop(0, od // 4, grow, 0)

            def fold(t, _):
                rows = [4 * t + n for n in range(4)]
                ups = [dot(w_ref[...], xs[i], 1, 0) for i in rows]
                ups = [u / (1e-3 + nrm[pl.ds(i, 1), :]) for i, u in zip(rows, ups)]
                ups = [u.T for u in ups]
                new = [residual(z_ref[i].astype(F32), u) for i, u in zip(rows, ups)]
                for i, v in zip(rows, new):
                    out_ref[i] = v
                ln = [layer_norm(v.astype(F32)) for v in new]
                ps = [dot(wb[...], v, 1, 1) for v in ln]
                for i, v in zip(rows, ps):
                    piece[i] = v.astype(BF16)
                return 0
            lax.fori_loop(0, rl // 4, fold, 0)

        def opm_call(zz, loc, gat, b, wb):
            return run(opm_kernel, [((rl, nr, cz), BF16), ((rl, ht, nr), BF16)],
                       [((nr * od, ns), F32), ((rl, od * od, nr), BF16), ((rl, nr), F32)],
                       zz, loc, gat, mask_col, mask_b, opm_o[b], wb)

        def tri_kernel(staged, z_ref, g_ref, mask_ref, wt, wk, wo, out_ref, gf, bias, kc, t_ref, k_ref, o_ref):
            kc[...] = spread(mask_ref[...], wz)

            def first(t, _):
                project([z_ref[4 * t + n].astype(F32) for n in range(4)], wt, wk, t_ref, k_ref, 4 * t, kc[...])
                return 0
            lax.fori_loop(0, rl // 4, first, 0)
            spread_bias(g_ref, gf, bias, True, mask_ref[...])

            def second(t, _):
                core(t_ref, k_ref, o_ref, [2 * t, 2 * t + 1], ht // 4, bias, None)
                return 0
            lax.fori_loop(0, rl // 2, second, 0)

            def third(t, _):
                rows = [4 * t + n for n in range(4)]
                ups = [dot(o_ref[i], wo[...], 0, 0) for i in rows]
                new = [residual(z_ref[i].astype(F32), u) for i, u in zip(rows, ups)]
                if staged:
                    for n in range(2):
                        stage(out_ref, 2 * t + n, new[2 * n].astype(F32), new[2 * n + 1].astype(F32), nd)
                else:
                    for i, v in zip(rows, new):
                        out_ref[i] = v
                return 0
            lax.fori_loop(0, rl // 4, third, 0)

        def tri_call(zz, g, wt, wk, wo, staged):
            out = (nd, rl * rl, cz) if staged else (rl, nr, cz)
            return run(functools.partial(tri_kernel, staged), [(out, BF16)],
                       [((nr, ht, nr), F32), ((ht // 4, nr, 4 * nr), F32), ((nr, wz), F32),
                        ((rl, 3 * wz, nr), BF16), ((rl, nr, wz), BF16), ((rl, wz, nr), BF16)],
                       zz, g, mask_r, wt, wk, wo)[0]

        def turn_kernel(r_ref, wb, out_ref, piece, work):
            work[...] = r_ref[...].astype(F32).reshape(work.shape)

            for b in range(rl):
                out_ref[b] = work[pl.ds(b, nr, stride=rl), :].astype(BF16)
            bias_pieces(lambda b: out_ref[b].astype(F32), rl, wb, piece)

        def turn_call(r, wb):
            return run(turn_kernel, [((rl, nr, cz), BF16), ((rl, ht, nr), BF16)], [((nr * rl, cz), F32)], r, wb)

        g = gather(bias_call(z, row_b[0]))
        r = swap(row_call(m, g, 0, True, True))
        m, loc, gat = col_call(r, 0)
        r2, loc2, gat2 = col_call(m, 1)
        z, piece = opm_call(z, loc, gather(gat), 0, ts_b[0])
        rz = swap(tri_call(z, gather(piece), ts_t[0], ts_k[0], ts_o[0], True))
        z, piece = turn_call(rz, te_b[0])
        z = tri_call(z, gather(piece), te_t[0], te_k[0], te_o[0], False)
        g = gather(bias_call(z, row_b[1]))
        z, piece = opm_call(z, loc2, gather(gat2), 1, te_b[1])
        m = row_call(swap(r2), g, 1, False, False)
        rz = swap(tri_call(z, gather(piece), te_t[1], te_k[1], te_o[1], True))
        z, piece = turn_call(rz, ts_b[1])
        z = tri_call(z, gather(piece), ts_t[1], ts_k[1], ts_o[1], False)
        return m, z

    in_specs = (P(('data', 'dap')), P(('data', 'dap')), P('data'), P('data')) + (P(),) * 13
    out_specs = (P(('data', 'dap')), P(('data', 'dap')))
    return jax.shard_map(local_step, mesh=mesh, in_specs=in_specs, out_specs=out_specs, check_vma=False)
```

time: 444 us -> 355 us (0.80)
  Pallas kernels: 232 us -> 120 us
  waiting for transfers between devices: 18.2 us -> 34.9 us
  blocking collectives: 141 us -> 147 us
    pallas_call x14, Pallas kernels: 232 us -> 120 us  [run(): pl.pallas_call(body, out_shape=[jax.ShapeDtypeStruct(s, d) for s, d in ou...]
    all_gather x2, waiting for transfers between devices: 0.91 us -> 17.7 us  [local_step(): gather = lambda v: lax.all_gather(v, 'dap', axis=0, tiled=True)]
    all_gather x6, blocking collectives: 117 us -> 123 us  [local_step(): gather = lambda v: lax.all_gather(v, 'dap', axis=0, tiled=True)]
  transfers between devices with their start and end apart: 5 -> 5, of which waited for: 2 -> 2; matrix products, arithmetic and copies ran while one was open for 3% -> 4% of each run, Pallas kernels for 35% -> 22%
where the time goes in v2:
time: 355 us; the launch traced here: 354 us
  blocking collectives  147 us (41%)
  Pallas kernels  120 us (34%)
  waiting for transfers between devices  34.9 us (10%)
  local copies, waits for them, and re-layouts  22.2 us (6%)
  between operations  14.3 us (4%)
  starting transfers between devices  13.9 us (4%)
    all_gather x6, blocking collectives, local_step(): gather = lambda v: lax.all_gather(v, 'dap', axis=0, tiled=True)  123 us
    pallas_call x14, Pallas kernels, run(): pl.pallas_call(body, out_shape=[jax.ShapeDtypeStruct(s, d) for s, d in ou...  120 us
    all_to_all x1, blocking collectives, local_step(): swap = lambda v: lax.all_to_all(v, 'dap', 0, 0, tiled=True)  24.6 us
    all_gather x2, waiting for transfers between devices, local_step(): gather = lambda v: lax.all_gather(v, 'dap', axis=0, tiled=True)  17.7 us
    all_to_all x3, waiting for transfers between devices, local_step(): swap = lambda v: lax.all_to_all(v, 'dap', 0, 0, tiled=True)  17.1 us
    all_to_all x3, starting transfers between devices, local_step(): swap = lambda v: lax.all_to_all(v, 'dap', 0, 0, tiled=True)  13.7 us
    unnamed x44, local copies, waits for them, and re-layouts  8.5 us
  transfers between devices with their start and end apart: 5, of which 2 were waited for; matrix products, arithmetic and copies ran while one was open for 4% of the time, Pallas kernels for 22%

profile of v2, /device:TPU:21, one launch (start us, length us, event | category | flops | bytes accessed | tf_op | source)
XLA Modules:
  0.0 353.6 jit_solution(10185864105815401788)
XLA Ops:
  13.1 24.8 %all_gather.24.g_ref = bf16[192,8,192]{2,1,0:T(8,128)(2,1)} all-gather(bf16[12,8,192]{2,1,0:T(8,128)(2,1)} %shard_map.176), channel_id=1, replica_groups=mesh['data'=4,'dap'=16] {'dap'}, dimensions={0}, use_global_device_ids=true | all-gather | bytes 626688 | tf_op jit(solution)/shard_map/all_gather | solution.py:187
  41.1 13.6 %shard_map.177 = bf16[16,96,256]{2,1,0:T(8,128)(2,1)} custom-call(bf16[8,192,256]{2,1,0:T(8,128)(2,1)} %m_ref.1, bf16[192,8,192]{2,1,0:T(8,128)(2,1)} %all_gather.24.g_ref, f32[8,192]{1,0:T(8,128)} %copy.61.mask_ref, bf16[768,256]{1,0:T(8,128)(2,1)} %bitcast.114, bf16[256,256]{1,0:T(8,128)(2,1)} %bitcast.124, bf16[256,256]{1,0:T(8,128)(2,1)} %bitcast.128), custom_call_target="tpu_custom_call" | custom-call | tf_op jit(solution)/shard_map/pallas_call | solution.py:138
  54.7 3.8 %all-to-all-start = ((bf16[16,96,256]{2,1,0:T(8,128)(2,1)}), bf16[16,96,256]{2,1,0:T(8,128)(2,1)S(1)}, u32[]{:S(2)}, u32[]{:S(2)}) async-start(bf16[16,96,256]{2,1,0:T(8,128)(2,1)} %shard_map.177), calls=%async_computation | async-start | bytes 1572864 | tf_op jit(solution)/shard_map/all_to_all | solution.py:188
  63.0 17.1 %all-to-all-done.r_ref = bf16[16,96,256]{2,1,0:T(8,128)(2,1)S(1)} async-done(((bf16[16,96,256]{2,1,0:T(8,128)(2,1)}), bf16[16,96,256]{2,1,0:T(8,128)(2,1)S(1)}, u32[]{:S(2)}, u32[]{:S(2)}) %all-to-all-start) | async-done | bytes 786464 | tf_op jit(solution)/shard_map/all_to_all | solution.py:188
  81.1 10.2 %shard_map.178 = (bf16[12,128,256]{2,1,0:T(8,128)(2,1)}, bf16[12,32,128]{2,1,0:T(8,128)(2,1)}, bf16[12,32,128]{2,1,0:T(8,128)(2,1)}) custom-call(bf16[16,96,256]{2,1,0:T(8,128)(2,1)} %copy-done, f32[12,128]{1,0:T(8,128)} %dynamic-slice_bitcast_fusion.mask_ref.mc_ref, bf16[768,256]{1,0:T(8,128)(2,1)} %bitcast.112, bf16[256,256]{1,0:T(8,128)(2,1)} %bitcast.121, ...), custom_call_target="tpu_custom_call" | custom-call | tf_op jit(solution)/shard_map/pallas_call | solution.py:138
  96.5 10.1 %shard_map.179 = (bf16[16,96,256]{2,1,0:T(8,128)(2,1)}, bf16[12,32,128]{2,1,0:T(8,128)(2,1)}, bf16[12,32,128]{2,1,0:T(8,128)(2,1)}) custom-call(bf16[12,128,256]{2,1,0:T(8,128)(2,1)} %get-tuple-element.16.r_ref, f32[12,128]{1,0:T(8,128)} %dynamic-slice_bitcast_fusion.mask_ref.mc_ref, bf16[768,256]{1,0:T(8,128)(2,1)} %bitcast.111, ...), custom_call_target="tpu_custom_call" | custom-call | tf_op jit(solution)/shard_map/pallas_call | solution.py:138
  107.3 17.7 %all-gather.3.cloned.1.call-done.gat_ref = bf16[192,32,128]{2,1,0:T(8,128)(2,1)} async-done(((bf16[12,32,128]{2,1,0:T(8,128)(2,1)}), bf16[192,32,128]{2,1,0:T(8,128)(2,1)}) %all-gather.3.cloned.1.call-update) | async-done | bytes 1572880 | tf_op jit(solution)/shard_map/all_gather | solution.py:187
  125.0 9.4 %shard_map.180 = (bf16[12,192,128]{2,1,0:T(8,128)(2,1)}, bf16[12,4,192]{2,1,0:T(4,128)(2,1)}) custom-call(bf16[12,192,128]{2,1,0:T(8,128)(2,1)} %z_ref.3, bf16[12,32,128]{2,1,0:T(8,128)(2,1)} %get-tuple-element.18.loc_ref, bf16[192,32,128]{2,1,0:T(8,128)(2,1)} %all-gather.3.cloned.1.call-done.gat_ref, f32[12,128]{1,0:T(8,128)} %dynamic-slice_bitcast_fusion.mask_ref.mc_ref, ...), custom_call_target="tpu_custom_call" | custom-call | tf_op jit(solution)/shard_map/pallas_call | solution.py:138
  134.4 17.2 %all_gather.26.g_ref = bf16[192,4,192]{2,1,0:T(4,128)(2,1)} all-gather(bf16[12,4,192]{2,1,0:T(4,128)(2,1)} %get-tuple-element.21), channel_id=1, replica_groups=mesh['data'=4,'dap'=16] {'dap'}, dimensions={0}, use_global_device_ids=true | all-gather | bytes 313344 | tf_op jit(solution)/shard_map/all_gather | solution.py:187
  151.5 10.3 %shard_map.181 = bf16[16,144,128]{2,1,0:T(8,128)(2,1)} custom-call(bf16[12,192,128]{2,1,0:T(8,128)(2,1)} %get-tuple-element.20.z_ref, bf16[192,4,192]{2,1,0:T(4,128)(2,1)} %all_gather.26.g_ref, f32[1,192]{1,0:T(1,128)} %bitcast.146, bf16[384,128]{1,0:T(8,128)(2,1)} %bitcast.131, bf16[128,128]{1,0:T(8,128)(2,1)} %bitcast.137, bf16[128,128]{1,0:T(8,128)(2,1)} %bitcast.142), custom_call_target="tpu_custom_call" | custom-call | tf_op jit(solution)/shard_map/pallas_call | solution.py:138
  161.9 24.6 %all_to_all.20.r_ref = bf16[16,144,128]{2,1,0:T(8,128)(2,1)} all-to-all(bf16[16,144,128]{2,1,0:T(8,128)(2,1)} %shard_map.181), channel_id=1, replica_groups=mesh['data'=4,'dap'=16] {'dap'}, dimensions={0} | all-to-all | bytes 1179648 | tf_op jit(solution)/shard_map/all_to_all | solution.py:188
  186.4 3.9 %all-to-all-start.1 = ((bf16[16,96,256]{2,1,0:T(8,128)(2,1)}), bf16[16,96,256]{2,1,0:T(8,128)(2,1)S(1)}, u32[]{:S(2)}, u32[]{:S(2)}) async-start(bf16[16,96,256]{2,1,0:T(8,128)(2,1)} %get-tuple-element.17), calls=%async_computation.1 | async-start | bytes 1572864 | tf_op jit(solution)/shard_map/all_to_all | solution.py:188
  194.6 3.2 shard_map.182
  197.8 24.5 %all_gather.27.g_ref = bf16[192,4,192]{2,1,0:T(4,128)(2,1)} all-gather(bf16[12,4,192]{2,1,0:T(4,128)(2,1)} %get-tuple-element.23), channel_id=1, replica_groups=mesh['data'=4,'dap'=16] {'dap'}, dimensions={0}, use_global_device_ids=true | all-gather | bytes 313344 | tf_op jit(solution)/shard_map/all_gather | solution.py:187
  222.2 10.3 %shard_map.183.z_ref = bf16[12,192,128]{2,1,0:T(8,128)(2,1)} custom-call(bf16[12,192,128]{2,1,0:T(8,128)(2,1)} %get-tuple-element.22.z_ref, bf16[192,4,192]{2,1,0:T(4,128)(2,1)} %all_gather.27.g_ref, f32[1,192]{1,0:T(1,128)} %bitcast.147, bf16[384,128]{1,0:T(8,128)(2,1)} %bitcast.132, bf16[128,128]{1,0:T(8,128)(2,1)} %bitcast.140, bf16[128,128]{1,0:T(8,128)(2,1)} %bitcast.144), custom_call_target="tpu_custom_call" | custom-call | tf_op jit(solution)/shard_map/pallas_call | solution.py:138
  232.6 9.4 %shard_map.186 = (bf16[12,192,128]{2,1,0:T(8,128)(2,1)}, bf16[12,4,192]{2,1,0:T(4,128)(2,1)}) custom-call(bf16[12,192,128]{2,1,0:T(8,128)(2,1)} %shard_map.183.z_ref, bf16[12,32,128]{2,1,0:T(8,128)(2,1)} %get-tuple-element.24.loc_ref, bf16[192,32,128]{2,1,0:T(8,128)(2,1)} %all-gather.5.cloned.1.call-done.gat_ref, ...), custom_call_target="tpu_custom_call" | custom-call | tf_op jit(solution)/shard_map/pallas_call | solution.py:138
  241.9 16.0 %all_gather.30.g_ref = bf16[192,4,192]{2,1,0:T(4,128)(2,1)} all-gather(bf16[12,4,192]{2,1,0:T(4,128)(2,1)} %get-tuple-element.27), channel_id=1, replica_groups=mesh['data'=4,'dap'=16] {'dap'}, dimensions={0}, use_global_device_ids=true | all-gather | bytes 313344 | tf_op jit(solution)/shard_map/all_gather | solution.py:187
  257.9 10.3 %shard_map.187 = bf16[16,144,128]{2,1,0:T(8,128)(2,1)} custom-call(bf16[12,192,128]{2,1,0:T(8,128)(2,1)} %get-tuple-element.26.z_ref, bf16[192,4,192]{2,1,0:T(4,128)(2,1)} %all_gather.30.g_ref, f32[1,192]{1,0:T(1,128)} %bitcast.148, bf16[384,128]{1,0:T(8,128)(2,1)} %bitcast.130, bf16[128,128]{1,0:T(8,128)(2,1)} %bitcast.138, bf16[128,128]{1,0:T(8,128)(2,1)} %bitcast.143), custom_call_target="tpu_custom_call" | custom-call | tf_op jit(solution)/shard_map/pallas_call | solution.py:138
  268.2 6.1 %all-to-all-start.3 = ((bf16[16,144,128]{2,1,0:T(8,128)(2,1)}), bf16[16,144,128]{2,1,0:T(8,128)(2,1)S(1)}, u32[]{:S(2)}, u32[]{:S(2)}) async-start(bf16[16,144,128]{2,1,0:T(8,128)(2,1)} %shard_map.187), calls=%async_computation.3 | async-start | bytes 1179648 | tf_op jit(solution)/shard_map/all_to_all | solution.py:188
  278.8 24.7 %all_gather.28.g_ref = bf16[192,8,192]{2,1,0:T(8,128)(2,1)} all-gather(bf16[12,8,192]{2,1,0:T(8,128)(2,1)} %shard_map.184), channel_id=1, replica_groups=mesh['data'=4,'dap'=16] {'dap'}, dimensions={0}, use_global_device_ids=true | all-gather | bytes 626688 | tf_op jit(solution)/shard_map/all_gather | solution.py:187
  303.5 13.3 %shard_map.185 = bf16[8,192,256]{2,1,0:T(8,128)(2,1)} custom-call(bf16[16,96,256]{2,1,0:T(8,128)(2,1)} %copy-done.1, bf16[192,8,192]{2,1,0:T(8,128)(2,1)} %all_gather.28.g_ref, f32[8,192]{1,0:T(8,128)} %copy.61.mask_ref, bf16[768,256]{1,0:T(8,128)(2,1)} %bitcast.113, bf16[256,256]{1,0:T(8,128)(2,1)} %bitcast.123, bf16[256,256]{1,0:T(8,128)(2,1)} %bitcast.125), custom_call_target="tpu_custom_call" | custom-call | tf_op jit(solution)/shard_map/pallas_call | solution.py:138
  317.7 3.2 shard_map.188
  320.9 15.6 %all_gather.31.g_ref = bf16[192,4,192]{2,1,0:T(4,128)(2,1)} all-gather(bf16[12,4,192]{2,1,0:T(4,128)(2,1)} %get-tuple-element.29), channel_id=1, replica_groups=mesh['data'=4,'dap'=16] {'dap'}, dimensions={0}, use_global_device_ids=true | all-gather | bytes 313344 | tf_op jit(solution)/shard_map/all_gather | solution.py:187
  336.5 10.3 %shard_map.189 = bf16[12,192,128]{2,1,0:T(8,128)(2,1)} custom-call(bf16[12,192,128]{2,1,0:T(8,128)(2,1)} %get-tuple-element.28.z_ref, bf16[192,4,192]{2,1,0:T(4,128)(2,1)} %all_gather.31.g_ref, f32[1,192]{1,0:T(1,128)} %bitcast.149, bf16[384,128]{1,0:T(8,128)(2,1)} %bitcast.129, bf16[128,128]{1,0:T(8,128)(2,1)} %bitcast.139, bf16[128,128]{1,0:T(8,128)(2,1)} %bitcast.141), custom_call_target="tpu_custom_call" | custom-call | tf_op jit(solution)/shard_map/pallas_call | solution.py:138
  (86 shorter events, 30.0 us)
Async XLA Ops:
  7.2 2.2 copy-start.13
  7.2 30.7 %copy-start.5 = (s32[128,192]{0,1:T(8,128)S(1)}, s32[128,192]{0,1:T(8,128)}, u32[]{:S(2)}) copy-start(s32[128,192]{0,1:T(8,128)} %param.19) | copy-start | bytes 294916
  38.6 1.8 copy-start.8
  41.1 17.4 %copy-start.3 = (bf16[2,256,4,8,32]{1,4,3,2,0:T(8,128)(2,1)S(1)}, bf16[2,256,4,8,32]{1,4,3,2,0:T(8,128)(2,1)}, u32[]{:S(2)}) copy-start(bf16[2,256,4,8,32]{1,4,3,2,0:T(8,128)(2,1)} %param.24) | copy-start | bytes 3145732
  54.7 25.5 %all-to-all-start = ((bf16[16,96,256]{2,1,0:T(8,128)(2,1)}), bf16[16,96,256]{2,1,0:T(8,128)(2,1)S(1)}, u32[]{:S(2)}, u32[]{:S(2)}) async-start(bf16[16,96,256]{2,1,0:T(8,128)(2,1)} %shard_map.177), calls=%async_computation | async-start | bytes 1572864 | tf_op jit(solution)/shard_map/all_to_all | solution.py:188
  58.5 66.5 %all-gather.3.cloned.1.call-start = ((), (), s32[]{:S(2)}) async-start(), calls=%async_computation.4 | async-start | bytes 1671168 | tf_op jit(solution)/shard_map/all_gather | solution.py:187
  59.9 0.8 copy-start.10
  59.9 1.5 copy-start.9
  62.1 30.8 %copy-start.4 = (bf16[2,32,32,128]{3,2,1,0:T(8,128)(2,1)S(1)}, bf16[2,32,32,128]{3,2,1,0:T(8,128)(2,1)}, u32[]{:S(2)}) copy-start(bf16[2,32,32,128]{3,2,1,0:T(8,128)(2,1)} %param.27) | copy-start | bytes 1572868
  80.2 0.9 copy-start
  91.2 2.6 copy-start.16
  91.2 3.2 copy-start.6
  91.3 4.0 %copy-start.14 = (bf16[2,128,4]{1,2,0:T(4,128)(2,1)S(1)}, bf16[2,128,4]{1,2,0:T(4,128)(2,1)}, u32[]{:S(2)}) copy-start(bf16[2,128,4]{1,2,0:T(4,128)(2,1)} %param.28) | copy-start | bytes 6148
  91.3 4.6 %copy-start.11 = (bf16[2,4,32,128]{3,2,1,0:T(8,128)(2,1)S(1)}, bf16[2,4,32,128]{3,2,1,0:T(8,128)(2,1)}, u32[]{:S(2)}) copy-start(bf16[2,4,32,128]{3,2,1,0:T(8,128)(2,1)} %param.30) | copy-start | bytes 196612
  91.3 141.2 %all-gather.5.cloned.1.call-start = ((), (), s32[]{:S(2)}) async-start(), calls=%async_computation.5 | async-start | bytes 1671168 | tf_op jit(solution)/shard_map/all_gather | solution.py:187
  161.9 28.5 %copy-start.7 = (bf16[2,128,4,4,32]{1,4,3,2,0:T(8,128)(2,1)S(1)}, bf16[2,128,4,4,32]{1,4,3,2,0:T(8,128)(2,1)}, u32[]{:S(2)}) copy-start(bf16[2,128,4,4,32]{1,4,3,2,0:T(8,128)(2,1)} %param.32) | copy-start | bytes 786436
  186.4 6.3 %copy-start.15 = (bf16[2,128,4]{1,2,0:T(4,128)(2,1)S(1)}, bf16[2,128,4]{1,2,0:T(4,128)(2,1)}, u32[]{:S(2)}) copy-start(bf16[2,128,4]{1,2,0:T(4,128)(2,1)} %param.31) | copy-start | bytes 6148
  186.4 6.8 %copy-start.12 = (bf16[2,4,32,128]{3,2,1,0:T(8,128)(2,1)S(1)}, bf16[2,4,32,128]{3,2,1,0:T(8,128)(2,1)}, u32[]{:S(2)}) copy-start(bf16[2,4,32,128]{3,2,1,0:T(8,128)(2,1)} %param.33) | copy-start | bytes 196612
  186.4 81.8 %all-to-all-start.1 = ((bf16[16,96,256]{2,1,0:T(8,128)(2,1)}), bf16[16,96,256]{2,1,0:T(8,128)(2,1)S(1)}, u32[]{:S(2)}, u32[]{:S(2)}) async-start(bf16[16,96,256]{2,1,0:T(8,128)(2,1)} %get-tuple-element.17), calls=%async_computation.1 | async-start | bytes 1572864 | tf_op jit(solution)/shard_map/all_to_all | solution.py:188
  268.2 35.3 %copy-start.1 = (bf16[16,96,256]{2,1,0:T(8,128)(2,1)}, bf16[16,96,256]{2,1,0:T(8,128)(2,1)S(1)}, u32[]{:S(2)}) copy-start(bf16[16,96,256]{2,1,0:T(8,128)(2,1)S(1)} %all-to-all-done.1.m_ref) | copy-start | bytes 2359300
  268.2 48.7 %all-to-all-start.3 = ((bf16[16,144,128]{2,1,0:T(8,128)(2,1)}), bf16[16,144,128]{2,1,0:T(8,128)(2,1)S(1)}, u32[]{:S(2)}, u32[]{:S(2)}) async-start(bf16[16,144,128]{2,1,0:T(8,128)(2,1)} %shard_map.187), calls=%async_computation.3 | async-start | bytes 1179648 | tf_op jit(solution)/shard_map/all_to_all | solution.py:188
  316.9 0.8 copy-start.2
Sparse Core Ops, SparseCore 0:
  91.5 33.4 all-gather.2
  126.6 34.2 all-gather.4

commit v3 on v2

v3 whole, which is shorter than its diff:
```python
import functools

import jax
import jax.numpy as jnp
from jax import lax
from jax.experimental import pallas as pl
from jax.experimental.pallas import tpu as pltpu
from jax.sharding import PartitionSpec as P

F32 = jnp.float32
BF16 = jnp.bfloat16
LOG2E = 1.4426950408889634
NEG = -1e9 * LOG2E
HEAD = 32
MESH = pl.DeviceIdType.MESH


def dot(lhs, rhs, lc, rc):
    return lax.dot_general(lhs, rhs, (((lc,), (rc,)), ((), ())), preferred_element_type=F32)


def layer_norm(x):
    mean = jnp.mean(x, axis=-1, keepdims=True)
    cen = x - mean
    var = jnp.mean(cen * cen, axis=-1, keepdims=True)
    return (cen * lax.rsqrt(var + 1e-5)).astype(BF16)


def project(xs, wt, wk, t_ref, k_ref, first, kcol):
    xl = [layer_norm(x) for x in xs]
    ts = [dot(wt[...], v, 1, 1) for v in xl]
    ks = [dot(v, wk[...], 1, 0) for v in xl]
    for n, v in enumerate(ts):
        t_ref[first + n] = v.astype(BF16)
    for n, v in enumerate(ks):
        if kcol is not None:
            v = v * kcol
        k_ref[first + n] = v.astype(BF16)


def diagonal(t, base, length):
    cols = []
    for r in range(4):
        parts = [t[base + HEAD * r:base + HEAD * r + HEAD]]
        if r > 0:
            parts.insert(0, jnp.zeros((HEAD * r, length), BF16))
        if r < 3:
            parts.append(jnp.zeros((HEAD * (3 - r), length), BF16))
        cols.append(jnp.concatenate(parts, axis=0))
    return jnp.concatenate(cols, axis=1)


def core(t_ref, k_ref, o_ref, rows, groups, bias, keeps):
    length = k_ref.shape[1]
    width = 128 * groups
    units = [(n, b, g) for n, b in enumerate(rows) for g in range(groups)]
    scores = []
    for n, b, g in units:
        t = t_ref[b, 128 * g:128 * g + 128, :]
        scores.append(dot(k_ref[b, :, 128 * g:128 * g + 128], diagonal(t, 0, length), 1, 0))
    probs = []
    dens = []
    for (n, b, g), s in zip(units, scores):
        s = s * (HEAD ** -0.5 * LOG2E)
        if bias is not None:
            s = s + bias[g]
        if keeps is not None:
            s = jnp.where(keeps[n] > 0, s, NEG)
        e = jnp.exp2(s - jnp.max(s, axis=0, keepdims=True))
        dens.append(jnp.sum(e, axis=0, keepdims=True))
        probs.append(e.astype(BF16))
    outs = [dot(t_ref[b, width + 128 * g:width + 128 * g + 128, :], p, 1, 0) for (n, b, g), p in zip(units, probs)]
    for (n, b, g), o, den in zip(units, outs, dens):
        inv = 1.0 / den
        gate = jax.nn.sigmoid(t_ref[b, 2 * width + 128 * g:2 * width + 128 * g + 128, :].astype(F32))
        parts = []
        for r in range(4):
            lanes = slice(length * r, length * r + length)
            parts.append(o[HEAD * r:HEAD * r + HEAD, lanes] * inv[:, lanes])
        o_ref[b, 128 * g:128 * g + 128, :] = (jnp.concatenate(parts, axis=0) * gate).astype(BF16)


def residual(x, update):
    return (x + update).astype(BF16)


def spread(row, lanes):
    return jnp.broadcast_to(row, (lanes, row.shape[1])).T


def widen(block, lanes):
    return jnp.concatenate([block] * (lanes // 128), axis=1)


def stage(stg, pair, first, second, ndev):
    rows = first.shape[0] // ndev
    off = pl.multiple_of(2 * rows * pair, 8)
    for d in range(ndev):
        both = jnp.concatenate([first[rows * d:rows * d + rows], second[rows * d:rows * d + rows]], axis=0)
        stg[d, pl.ds(off, 2 * rows), :] = both.astype(BF16)


def fill(work, ref):
    for t in range(work.shape[0]):
        work[t] = ref[..., 128 * t:128 * t + 128].astype(F32).reshape(work.shape[1:])


def take(work, start, count, stride):
    return jnp.concatenate([work.at[t][pl.ds(start, count, stride=stride), :] for t in range(work.shape[0])], axis=1)


def spread_bias(gath, gf, bias, transpose, mask_row):
    length, heads = gath.shape[0], gath.shape[1]
    gf[...] = gath[...].astype(F32)
    keep = None if mask_row is None else widen(spread(mask_row, 128), 4 * length)
    for g in range(heads // 4):
        parts = []
        for r in range(4):
            value = gf[:, 4 * g + r, :]
            parts.append(value.T if transpose else value)
        value = jnp.concatenate(parts, axis=1) * LOG2E
        if keep is not None:
            value = jnp.where(keep > 0, value, NEG)
        bias[g] = value


def bias_pieces(load, count, wb, store):
    def body(t, _):
        zl = [layer_norm(load(4 * t + n)) for n in range(4)]
        ps = [dot(wb, v, 1, 1) for v in zl]
        for n, v in enumerate(ps):
            store(4 * t + n, v.astype(BF16))
        return 0
    lax.fori_loop(0, count // 4, body, 0)


class Comm:
    def __init__(self, nd, sems):
        self.nd = nd
        self.me = lax.axis_index('dap')
        self.partner = self.me + 1 - 2 * lax.rem(self.me, 2)
        self.ssem, self.rsem, self.fsem, self.gsem = sems

    def copy(self, src, dst, send, recv, dev):
        return pltpu.make_async_remote_copy(src_ref=src, dst_ref=dst, send_sem=send, recv_sem=recv,
                                            device_id={'dap': dev}, device_id_type=MESH)

    def barrier_signal(self):
        bar = pltpu.get_barrier_semaphore()

        def body(k, _):
            pl.semaphore_signal(bar, inc=1, device_id={'dap': lax.rem(self.me + k, self.nd)}, device_id_type=MESH)
            return 0
        lax.fori_loop(1, self.nd, body, 0)

    def barrier_wait(self):
        pl.semaphore_wait(pltpu.get_barrier_semaphore(), self.nd - 1)

    def await_bytes(self, ref, sem):
        pltpu.make_async_copy(ref, ref, sem).wait()

    def gather_start(self, buf, i):
        n = buf.shape[0] // self.nd
        own = buf.at[pl.ds(self.me * n, n)]

        def body(k, _):
            self.copy(own, own, self.ssem.at[i], self.gsem.at[i, k], lax.rem(self.me + 2 * k, self.nd)).start()
            return 0
        lax.fori_loop(1, self.nd // 2, body, 0)
        self.copy(own, own, self.ssem.at[i], self.gsem.at[i, 0], self.partner).start()

    def gather_finish(self, buf, i):
        n = buf.shape[0] // self.nd
        half = self.nd // 2

        def body(k, _):
            slot = buf.at[pl.ds(lax.rem(self.me + self.nd - 2 * k, self.nd) * n, n)]
            self.await_bytes(slot, self.gsem.at[i, k])
            self.copy(slot, slot, self.fsem.at[i], self.rsem.at[i], self.partner).start()
            return 0
        lax.fori_loop(1, half, body, 0)
        self.await_bytes(buf.at[pl.ds(0, n)], self.gsem.at[i, 0])
        rest = buf.at[pl.ds(0, (half - 1) * n)]
        self.await_bytes(rest, self.rsem.at[i])
        self.await_bytes(rest, self.fsem.at[i])
        self.await_bytes(buf.at[pl.ds(0, half * n)], self.ssem.at[i])

    def swap_start(self, send, recv, i, off, rows):
        part = pl.ds(off, rows)

        def body(k, _):
            d = lax.rem(self.me + k, self.nd)
            self.copy(send.at[d, part], recv.at[self.me, part], self.ssem.at[i], self.rsem.at[i], d).start()
            return 0
        lax.fori_loop(1, self.nd, body, 0)
        pltpu.make_async_copy(send.at[self.me, part], recv.at[self.me, part], self.rsem.at[i]).start()

    def swap_finish(self, send, recv, i):
        self.await_bytes(recv, self.rsem.at[i])
        self.await_bytes(send.at[pl.ds(0, self.nd - 1)], self.ssem.at[i])


def kernel(names, outs, nd, refs):
    r = dict(zip(names, refs))
    class N:
        pass
    v = N()
    v.__dict__.update(r)
    sl, nr, cm = v.m.shape
    rl, _, cz = v.z.shape
    ns = sl * nd
    wm, wz = v.row_k.shape[2], v.ts_k.shape[2]
    gm, gz = wm // 128, wz // 128
    od = v.opm_i.shape[1] // 2
    comm = Comm(nd, (v.ssem, v.rsem, v.fsem, v.gsem))
    me = comm.me
    rows_m = sl * rl

    def store_piece(buf):
        def store(i, val):
            buf[me * rl + i] = val
        return store

    def loop(n, body):
        def step(t, _):
            body(t)
            return 0
        lax.fori_loop(0, n, step, 0)

    def row_project(load, b):
        loop(sl // 2, lambda t: project([load(2 * t), load(2 * t + 1)], v.row_t[b], v.row_k[b], v.rt, v.rk, 2 * t, None))

    def row_attend(load, b, finish):
        def body(t):
            for n in range(2):
                keep = widen(spread(v.mask_seq[pl.ds(2 * t + n, 1), :], 128), 4 * nr)
                core(v.rt, v.rk, v.ro, [2 * t + n], gm, v.rbias, [keep])
            ups = [dot(v.ro[2 * t + n], v.row_o[b], 0, 0) for n in range(2)]
            finish(t, [residual(load(2 * t + n), ups[n]) for n in range(2)])
        loop(sl // 2, body)

    def col_project(load, b):
        loop(rl // 4, lambda t: project([load(4 * t + n) for n in range(4)], v.col_t[b], v.col_k[b], v.ct, v.ck, 4 * t, None))

    def col_attend(load, b, finish, loc, gat):
        def body(t):
            rows = [2 * t, 2 * t + 1]
            keeps = [widen(spread(v.mask_col[pl.ds(i, 1), :], 128), 4 * ns) for i in rows]
            core(v.ct, v.ck, v.co, rows, gm, None, keeps)
        loop(rl // 2, body)

        def out(t):
            rows = [4 * t + n for n in range(4)]
            ups = [dot(v.co[i], v.col_o[b], 0, 0) for i in rows]
            new = [residual(load(i), u) for i, u in zip(rows, ups)]
            newf = [x.astype(F32) for x in new]
            finish(t, new, newf)
            ln = [layer_norm(x) for x in newf]
            acs = [dot(v.opm_i[b], x, 1, 1) for x in ln]
            for i, x in zip(rows, acs):
                ac = (x * v.mask_col[pl.ds(i, 1), :]).astype(BF16)
                a, c = ac[:od], ac[od:]
                loc[i] = a if b == 0 else c
                gat[me * rl + i] = c if b == 0 else a
        loop(rl // 4, out)

    def opm(loc, gat, b, load, wb, piece):
        v.gcol[...] = gat[...].astype(F32).reshape(v.gcol.shape)
        v.nrm[...] = dot(v.mask_col[...].astype(BF16), v.mask_b[...], 1, 0)

        def grow(t):
            left = loc[...].reshape(rl * od, ns)
            for n in range(4):
                g = 4 * t + n
                col = v.gcol[pl.ds(g, nr, stride=od), :].astype(BF16)
                x = dot(left, col, 1, 1).astype(BF16)
                off = pl.multiple_of(g * od, od)
                for i in range(rl):
                    v.xs[i, pl.ds(off, od), :] = x[od * i:od * i + od]
        loop(od // 4, grow)

        def fold(t):
            rows = [4 * t + n for n in range(4)]
            ups = [dot(v.opm_o[b], v.xs[i], 1, 0) for i in rows]
            ups = [u / (1e-3 + v.nrm[pl.ds(i, 1), :]) for i, u in zip(rows, ups)]
            ups = [u.T for u in ups]
            new = [residual(load(i), u) for i, u in zip(rows, ups)]
            for i, x in zip(rows, new):
                v.zc[i] = x
            ln = [layer_norm(x.astype(F32)) for x in new]
            ps = [dot(wb, x, 1, 1) for x in ln]
            for i, x in zip(rows, ps):
                piece[me * rl + i] = x.astype(BF16)
        loop(rl // 4, fold)

    def zload(i):
        return v.zc[i].astype(F32)

    def tri_project(wt, wk):
        loop(rl // 4, lambda t: project([zload(4 * t + n) for n in range(4)], wt, wk, v.tt, v.tk, 4 * t, v.kc[...]))

    def tri_attend(wo, finish):
        def body(t):
            core(v.tt, v.tk, v.to, [2 * t, 2 * t + 1], gz, v.tbias, None)
            rows = [2 * t, 2 * t + 1]
            ups = [dot(v.to[i], wo, 0, 0) for i in rows]
            finish(t, [residual(zload(i), u) for i, u in zip(rows, ups)])
        loop(rl // 2, body)

    def send_pair(send, recv, i, rows):
        def finish(t, pair):
            stage(send, t, pair[0].astype(F32), pair[1].astype(F32), nd)
            comm.swap_start(send, recv, i, pl.multiple_of(2 * rows * t, 8), 2 * rows)
        return finish

    def keep_pair(out):
        def finish(t, pair):
            out[2 * t], out[2 * t + 1] = pair
        return finish

    def turn(recv):
        fill(v.zwork, recv)
        for b in range(rl):
            v.zc[b] = take(v.zwork, b, nr, rl).astype(BF16)

    comm.barrier_signal()
    bias_pieces(lambda i: v.z[i].astype(F32), rl, v.row_b[0], store_piece(v.g0))
    v.kc[...] = spread(v.mask_r[...], wz)
    comm.barrier_wait()
    comm.gather_start(v.g0, 0)
    mload = lambda s: v.m[s].astype(F32)
    row_project(mload, 0)
    comm.gather_finish(v.g0, 0)
    spread_bias(v.g0, v.gf, v.rbias, True, None)
    row_attend(mload, 0, send_pair(v.s0, v.r0, 8, rl))
    comm.swap_finish(v.s0, v.r0, 8)

    fill(v.mwork, v.r0)
    cload = lambda i: take(v.mwork, i, ns, rl)
    col_project(cload, 0)

    def keep_four(t, new, newf):
        for n, x in enumerate(new):
            v.mc[4 * t + n] = x
    col_attend(cload, 0, keep_four, v.loc0, v.g1)
    comm.gather_start(v.g1, 1)

    c2load = lambda i: v.mc[i].astype(F32)
    col_project(c2load, 1)

    def send_four(t, new, newf):
        for n in range(2):
            stage(v.s1, 2 * t + n, newf[2 * n], newf[2 * n + 1], nd)
    col_attend(c2load, 1, send_four, v.loc1, v.g2)
    comm.gather_finish(v.g1, 1)
    opm(v.loc0, v.g1, 0, lambda i: v.z[i].astype(F32), v.ts_b[0], v.g3)
    comm.gather_start(v.g3, 3)
    tri_project(v.ts_t[0], v.ts_k[0])
    comm.gather_finish(v.g3, 3)
    spread_bias(v.g3, v.gf2, v.tbias, True, v.mask_r[...])
    tri_attend(v.ts_o[0], send_pair(v.s2, v.r2, 9, rl))
    comm.gather_start(v.g2, 2)
    comm.swap_finish(v.s2, v.r2, 9)
    turn(v.r2)
    bias_pieces(zload, rl, v.te_b[0], store_piece(v.g4))
    comm.gather_start(v.g4, 4)
    comm.swap_start(v.s1, v.r1, 10, 0, rows_m)
    tri_project(v.te_t[0], v.te_k[0])
    comm.gather_finish(v.g4, 4)
    spread_bias(v.g4, v.gf2, v.tbias, True, v.mask_r[...])
    tri_attend(v.te_o[0], keep_pair(v.zc))

    bias_pieces(zload, rl, v.row_b[1], store_piece(v.g5))
    comm.gather_start(v.g5, 5)
    comm.gather_finish(v.g2, 2)
    opm(v.loc1, v.g2, 1, zload, v.te_b[1], v.g6)
    comm.gather_start(v.g6, 6)
    comm.swap_finish(v.s1, v.r1, 10)
    fill(v.mwork, v.r1)
    rload = lambda s: take(v.mwork, s, nr, sl)
    row_project(rload, 1)
    tri_project(v.te_t[1], v.te_k[1])
    comm.gather_finish(v.g5, 5)
    comm.gather_finish(v.g6, 6)
    spread_bias(v.g6, v.gf2, v.tbias, True, v.mask_r[...])
    tri_attend(v.te_o[1], send_pair(v.s3, v.r3, 11, rl))
    spread_bias(v.g5, v.gf, v.rbias, False, None)
    row_attend(rload, 1, keep_pair(v.m_out))
    comm.swap_finish(v.s3, v.r3, 11)
    turn(v.r3)
    bias_pieces(zload, rl, v.ts_b[1], store_piece(v.g7))
    comm.gather_start(v.g7, 7)
    tri_project(v.ts_t[1], v.ts_k[1])
    comm.gather_finish(v.g7, 7)
    spread_bias(v.g7, v.gf2, v.tbias, True, v.mask_r[...])
    tri_attend(v.ts_o[1], keep_pair(v.z_out))


def solution(mesh):
    nd = mesh.shape['dap']

    def local_step(m, z, msa_mask, res_mask, w_row_bias, w_row_in, w_row_out, w_col_in, w_col_out, w_opm_in, w_opm_out, w_ts_bias, w_ts_in, w_ts_out, w_te_bias, w_te_in, w_te_out):
        me = lax.axis_index('dap')
        sl, nr, cm = m.shape
        rl, _, cz = z.shape
        ns = sl * nd
        hm, ht = w_row_bias.shape[2], w_ts_bias.shape[2]
        wm, wz = hm * HEAD, ht * HEAD
        od = w_opm_in.shape[3]

        maskf = msa_mask.astype(F32)
        mask_seq = lax.dynamic_slice_in_dim(maskf, me * sl, sl, 0)
        mask_col = lax.dynamic_slice_in_dim(maskf, me * rl, rl, 1).T
        mask_b = msa_mask.astype(BF16)
        mask_r = res_mask.astype(F32)[None, :]

        def split(w, width):
            c = w.shape[1]
            w = w.reshape(2, c, 4, width)
            wt = jnp.stack([w[:, :, 0], w[:, :, 2], w[:, :, 3]], axis=1)
            return wt.transpose(0, 1, 3, 2).reshape(2, 3 * width, c), w[:, :, 1]

        row_t, row_k = split(w_row_in, wm)
        col_t, col_k = split(w_col_in, wm)
        ts_t, ts_k = split(w_ts_in, wz)
        te_t, te_k = split(w_te_in, wz)
        row_o = w_row_out.reshape(2, wm, cm)
        col_o = w_col_out.reshape(2, wm, cm)
        ts_o = w_ts_out.reshape(2, wz, cz)
        te_o = w_te_out.reshape(2, wz, cz)
        row_b = w_row_bias.transpose(0, 2, 1)
        ts_b = w_ts_bias.transpose(0, 2, 1)
        te_b = w_te_bias.transpose(0, 2, 1)
        opm_i = w_opm_in.reshape(2, cm, 2 * od).transpose(0, 2, 1)
        opm_o = jnp.stack([w_opm_out[0].transpose(2, 1, 0), w_opm_out[1].transpose(2, 0, 1)]).reshape(2, cz, od * od)

        ins = dict(m=m, z=z, mask_seq=mask_seq, mask_col=mask_col, mask_b=mask_b, mask_r=mask_r,
                   row_t=row_t, row_k=row_k, row_o=row_o, row_b=row_b, col_t=col_t, col_k=col_k, col_o=col_o,
                   ts_t=ts_t, ts_k=ts_k, ts_o=ts_o, ts_b=ts_b, te_t=te_t, te_k=te_k, te_o=te_o, te_b=te_b,
                   opm_i=opm_i, opm_o=opm_o)
        outs = dict(m_out=m, z_out=z)
        gm, gz = wm // 128, wz // 128
        xm, xz = (nd, sl * rl, cm), (nd, rl * rl, cz)
        grow, gtri, gopm = (nd * rl, hm, nr), (nd * rl, ht, nr), (nd * rl, od, ns)
        scratch = dict(
            s0=(xm, BF16), r0=(xm, BF16), s1=(xm, BF16), r1=(xm, BF16),
            s2=(xz, BF16), r2=(xz, BF16), s3=(xz, BF16), r3=(xz, BF16),
            g0=(grow, BF16), g5=(grow, BF16), g1=(gopm, BF16), g2=(gopm, BF16),
            g3=(gtri, BF16), g4=(gtri, BF16), g6=(gtri, BF16), g7=(gtri, BF16),
            gf=(grow, F32), gf2=(gtri, F32), rbias=((gm, nr, 4 * nr), F32), tbias=((gz, nr, 4 * nr), F32),
            mwork=((cm // 128, nd * sl * rl, 128), F32), zwork=((cz // 128, nr * rl, 128), F32),
            gcol=((nr * od, ns), F32), xs=((rl, od * od, nr), BF16), nrm=((rl, nr), F32), kc=((nr, wz), F32),
            rt=((sl, 3 * wm, nr), BF16), rk=((sl, nr, wm), BF16), ro=((sl, wm, nr), BF16),
            ct=((rl, 3 * wm, ns), BF16), ck=((rl, ns, wm), BF16), co=((rl, wm, ns), BF16),
            tt=((rl, 3 * wz, nr), BF16), tk=((rl, nr, wz), BF16), to=((rl, wz, nr), BF16),
            mc=((rl, ns, cm), BF16), zc=((rl, nr, cz), BF16), loc0=((rl, od, ns), BF16), loc1=((rl, od, ns), BF16))
        sems = dict(ssem=(12,), rsem=(12,), fsem=(8,), gsem=(8, nd // 2))
        names = list(ins) + list(outs) + list(scratch) + list(sems)
        return pl.pallas_call(
            lambda *refs: kernel(names, outs, nd, refs),
            out_shape=[jax.ShapeDtypeStruct(o.shape, o.dtype) for o in outs.values()],
            in_specs=[pl.BlockSpec(memory_space=pltpu.VMEM)] * len(ins),
            out_specs=[pl.BlockSpec(memory_space=pltpu.VMEM)] * len(outs),
            scratch_shapes=[pltpu.VMEM(*x) for x in scratch.values()] + [pltpu.SemaphoreType.DMA(x) for x in sems.values()],
            compiler_params=pltpu.CompilerParams(collective_id=0, has_side_effects=True, vmem_limit_bytes=67043328),
        )(*ins.values())

    in_specs = (P(('data', 'dap')), P(('data', 'dap')), P('data'), P('data')) + (P(),) * 13
    out_specs = (P(('data', 'dap')), P(('data', 'dap')))
    return jax.shard_map(local_step, mesh=mesh, in_specs=in_specs, out_specs=out_specs, check_vma=False)
```

time: 355 us -> 219 us (0.62)
  blocking collectives: 147 us -> 0 us
  Pallas kernels: 120 us -> 201 us
  waiting for transfers between devices: 34.9 us -> 0 us
  starting transfers between devices: 13.9 us -> 0 us
  between operations: 14.3 us -> 0.77 us
  local copies, waits for them, and re-layouts: 22.2 us -> 13.7 us
    all_gather x6 -> x0, blocking collectives: 123 us -> none  [local_step(): gather = lambda v: lax.all_gather(v, 'dap', axis=0, tiled=True)]
    pallas_call x14 -> x1, Pallas kernels: 120 us -> 201 us  [local_step(): pl.pallas_call(lambda *refs: kernel(names, outs, nd, refs), out_shape=[ja...]
    all_to_all x1 -> x0, blocking collectives: 24.6 us -> none  [local_step(): swap = lambda v: lax.all_to_all(v, 'dap', 0, 0, tiled=True)]
    all_gather x2 -> x0, waiting for transfers between devices: 17.7 us -> none  [local_step(): gather = lambda v: lax.all_gather(v, 'dap', axis=0, tiled=True)]
    all_to_all x3 -> x0, waiting for transfers between devices: 17.1 us -> none  [local_step(): swap = lambda v: lax.all_to_all(v, 'dap', 0, 0, tiled=True)]
    all_to_all x3 -> x0, starting transfers between devices: 13.7 us -> none  [local_step(): swap = lambda v: lax.all_to_all(v, 'dap', 0, 0, tiled=True)]
    slice x13 -> x5, local copies, waits for them, and re-layouts: 6.96 us -> 0.21 us  [the longest x4 0.17 us: split(): return (wt.transpose(0, 1, 3, 2).reshape(2, 3 * width, c), w[:, :, 1])]
    squeeze x6 -> x0, local copies, waits for them, and re-layouts: 4.08 us -> none  [the longest x2 1.7 us: opm_call(): opm_o[b]]
  transfers between devices with their start and end apart: 5 -> 0, of which waited for: 2 -> 0; matrix products, arithmetic and copies ran while one was open for 4% -> 0% of each run, Pallas kernels for 22% -> 0%
where the time goes in v3:
time: 219 us; the launch traced here: 218 us
  Pallas kernels  201 us (92%)
  local copies, waits for them, and re-layouts  13.7 us (6%)
  other arithmetic  2.55 us (1%)
    pallas_call x1, Pallas kernels, local_step(): pl.pallas_call(lambda *refs: kernel(names, outs, nd, refs), out_shape=[ja...  201 us
    unnamed x21, local copies, waits for them, and re-layouts  7.87 us

profile of v3, /device:TPU:21, one launch (start us, length us, event | category | flops | bytes accessed | tf_op | source)
XLA Modules:
  0.0 217.7 jit_solution(5929855498237457567)
XLA Ops:
  0.6 0.7 copy-done.6
  1.3 0.5 convert_element_type.11
  1.8 1.0 fusion.5
  2.8 0.6 dynamic-slice_bitcast_fusion.refs_3_
  3.5 0.7 copy.67.refs_2_
  4.2 0.7 copy.68.refs_4_
  4.9 0.7 copy.77
  5.7 0.7 copy.58
  6.4 0.3 copy-done.5
  6.8 0.7 copy.80
  7.5 0.7 copy.62
  8.3 0.1 copy.81
  8.4 0.1 copy.65
  8.5 0.1 copy.66
  8.7 0.8 pad_maximum_fusion.refs_22_
  9.7 0.8 copy.71
  10.5 0.1 maximum_bitcast_fusion
  10.6 0.9 copy.50
  11.6 0.6 copy-done.1
  12.2 0.8 copy.74
  13.1 0.9 copy.54
  14.1 200.6 %shard_map.176 = (bf16[8,192,256]{2,1,0:T(8,128)(2,1)}, bf16[12,192,128]{2,1,0:T(8,128)(2,1)}) custom-call(bf16[8,192,256]{2,1,0:T(8,128)(2,1)} %refs_0_.1, bf16[12,192,128]{2,1,0:T(8,128)(2,1)} %refs_1_.1, f32[8,192]{1,0:T(8,128)} %copy.67.refs_2_, f32[12,128]{1,0:T(8,128)} %dynamic-slice_bitcast_fusion.refs_3_, bf16[128,192]{1,0:T(8,128)(2,1)} %copy.68.refs_4_, ...), custom_call_target="tpu_custom_call" | custom-call | tf_op jit(solution)/shard_map/pallas_call | solution.py:459
  214.7 2.1 copy.84
  216.9 0.8 copy.85
  (20 shorter events, 0.5 us)
Async XLA Ops:
  0.6 0.7 copy-start.6
  2.8 2.1 copy-start.4
  5.7 1.0 copy-start.5
  6.7 1.5 copy-start.3
  8.4 1.2 copy-start
  10.6 1.5 copy-start.1
  214.7 2.1 copy-start.2

commit v4 on v3

--- a/solution.py
+++ b/solution.py
@@ -145,6 +145,10 @@
         return pltpu.make_async_remote_copy(src_ref=src, dst_ref=dst, send_sem=send, recv_sem=recv,
                                             device_id={'dap': dev}, device_id_type=MESH)
 
+    def near(self, k, unit):
+        off = ((k + 1) // 2) * (2 * lax.rem(k, 2) - 1)
+        return lax.rem(self.me + self.nd + unit * off, self.nd)
+
     def barrier_signal(self):
         bar = pltpu.get_barrier_semaphore()
 
@@ -164,7 +168,7 @@
         own = buf.at[pl.ds(self.me * n, n)]
 
         def body(k, _):
-            self.copy(own, own, self.ssem.at[i], self.gsem.at[i, k], lax.rem(self.me + 2 * k, self.nd)).start()
+            self.copy(own, own, self.ssem.at[i], self.gsem.at[i, k], self.near(k, 2)).start()
             return 0
         lax.fori_loop(1, self.nd // 2, body, 0)
         self.copy(own, own, self.ssem.at[i], self.gsem.at[i, 0], self.partner).start()
@@ -174,7 +178,7 @@
         half = self.nd // 2
 
         def body(k, _):
-            slot = buf.at[pl.ds(lax.rem(self.me + self.nd - 2 * k, self.nd) * n, n)]
+            slot = buf.at[pl.ds(self.near(k, -2) * n, n)]
             self.await_bytes(slot, self.gsem.at[i, k])
             self.copy(slot, slot, self.fsem.at[i], self.rsem.at[i], self.partner).start()
             return 0
@@ -185,11 +189,47 @@
         self.await_bytes(rest, self.fsem.at[i])
         self.await_bytes(buf.at[pl.ds(0, half * n)], self.ssem.at[i])
 
+    def slot(self, buf, off, part=None):
+        n = buf.shape[0] // self.nd
+        base = lax.rem(self.me + self.nd + 2 * off, self.nd) * n
+        if part is None:
+            return buf.at[pl.ds(base, n)]
+        return buf.at[pl.ds(base + part * (n // 2), n // 2)]
+
+    def relay(self, ref, i, recv, dev):
+        self.copy(ref, ref, self.ssem.at[i], recv, dev).start()
+
+    def relay_start(self, buf, i):
+        own = self.slot(buf, 0)
+        right, left = lax.rem(self.me + 2, self.nd), lax.rem(self.me + self.nd - 2, self.nd)
+        self.relay(own, i, self.gsem.at[i, 0], right)
+        self.relay(own, i, self.gsem.at[i, 4], left)
+        self.relay(own, i, self.rsem.at[i], self.partner)
+
+    def relay_step(self, buf, i, p):
+        right, left = lax.rem(self.me + 2, self.nd), lax.rem(self.me + self.nd - 2, self.nd)
+        for sign, base, dev, part in ((-1, 0, right, 0), (1, 4, left, 1)):
+            ref = self.slot(buf, sign * p)
+            self.await_bytes(ref, self.gsem.at[i, base + p - 1])
+            on = self.slot(buf, sign * p, part) if p == self.nd // 4 - 1 else ref
+            self.relay(on, i, self.gsem.at[i, base + p], dev)
+            self.relay(ref, i, self.rsem.at[i], self.partner)
+
+    def relay_finish(self, buf, i):
+        n = buf.shape[0] // self.nd
+        half = self.nd // 2
+        far = self.slot(buf, self.nd // 4)
+        for part in range(2):
+            self.await_bytes(self.slot(buf, self.nd // 4, part), self.gsem.at[i, 4 * part + self.nd // 4 - 1])
+        self.relay(far, i, self.rsem.at[i], self.partner)
+        self.await_bytes(buf.at[pl.ds(0, half * n)], self.rsem.at[i])
+        self.await_bytes(buf.at[pl.ds(0, (2 * half - 1) * n)], self.ssem.at[i])
+
     def swap_start(self, send, recv, i, off, rows):
         part = pl.ds(off, rows)
 
         def body(k, _):
-            d = lax.rem(self.me + k, self.nd)
+            d = self.near(k, 1)
             self.copy(send.at[d, part], recv.at[self.me, part], self.ssem.at[i], self.rsem.at[i], d).start()
             return 0
         lax.fori_loop(1, self.nd, body, 0)
@@ -242,13 +282,15 @@
     def col_project(load, b):
         loop(rl // 4, lambda t: project([load(4 * t + n) for n in range(4)], v.col_t[b], v.col_k[b], v.ct, v.ck, 4 * t, None))
 
-    def col_attend(load, b, finish, loc, gat):
-        def body(t):
+    def col_attend(first, count):
+        def body(u):
+            t = first + u
             rows = [2 * t, 2 * t + 1]
             keeps = [widen(spread(v.mask_col[pl.ds(i, 1), :], 128), 4 * ns) for i in rows]
             core(v.ct, v.ck, v.co, rows, gm, None, keeps)
-        loop(rl // 2, body)
-
+        loop(count, body)
+
+    def col_out(load, b, finish, loc, gat):
         def out(t):
             rows = [4 * t + n for n in range(4)]
             ups = [dot(v.co[i], v.col_o[b], 0, 0) for i in rows]
@@ -264,7 +306,7 @@
                 gat[me * rl + i] = c if b == 0 else a
         loop(rl // 4, out)
 
-    def opm(loc, gat, b, load, wb, piece):
+    def opm(loc, gat, b, load, wb, piece, between):
         v.gcol[...] = gat[...].astype(F32).reshape(v.gcol.shape)
         v.nrm[...] = dot(v.mask_col[...].astype(BF16), v.mask_b[...], 1, 0)
 
@@ -278,6 +320,7 @@
                 for i in range(rl):
                     v.xs[i, pl.ds(off, od), :] = x[od * i:od * i + od]
         loop(od // 4, grow)
+        between()
 
         def fold(t):
             rows = [4 * t + n for n in range(4)]
@@ -307,15 +350,24 @@
             finish(t, [residual(zload(i), u) for i, u in zip(rows, ups)])
         loop(rl // 2, body)
 
-    def send_pair(send, recv, i, rows):
+    def pair_pieces(t, pair, wb, piece):
+        ps = [dot(wb, layer_norm(x.astype(F32)), 1, 1) for x in pair]
+        for n, x in enumerate(ps):
+            piece[me * rl + 2 * t + n] = x.astype(BF16)
+
+    def send_pair(send, recv, i, rows, wb=None, piece=None):
         def finish(t, pair):
             stage(send, t, pair[0].astype(F32), pair[1].astype(F32), nd)
             comm.swap_start(send, recv, i, pl.multiple_of(2 * rows * t, 8), 2 * rows)
+            if piece is not None:
+                pair_pieces(t, pair, wb, piece)
         return finish
 
-    def keep_pair(out):
+    def keep_pair(out, wb=None, piece=None):
         def finish(t, pair):
             out[2 * t], out[2 * t + 1] = pair
+            if piece is not None:
+                pair_pieces(t, pair, wb, piece)
         return finish
 
     def turn(recv):
@@ -342,57 +394,64 @@
     def keep_four(t, new, newf):
         for n, x in enumerate(new):
             v.mc[4 * t + n] = x
-    col_attend(cload, 0, keep_four, v.loc0, v.g1)
-    comm.gather_start(v.g1, 1)
+    col_attend(0, rl // 2)
+    col_out(cload, 0, keep_four, v.loc0, v.g1)
+    comm.relay_start(v.g1, 1)
 
     c2load = lambda i: v.mc[i].astype(F32)
-    col_project(c2load, 1)
 
     def send_four(t, new, newf):
         for n in range(2):
             stage(v.s1, 2 * t + n, newf[2 * n], newf[2 * n + 1], nd)
-    col_attend(c2load, 1, send_four, v.loc1, v.g2)
-    comm.gather_finish(v.g1, 1)
-    opm(v.loc0, v.g1, 0, lambda i: v.z[i].astype(F32), v.ts_b[0], v.g3)
+    col_project(c2load, 1)
+    comm.relay_step(v.g1, 1, 1)
+    col_attend(0, rl // 4)
+    comm.relay_step(v.g1, 1, 2)
+    col_attend(rl // 4, rl // 4)
+    comm.relay_step(v.g1, 1, 3)
+    col_out(c2load, 1, send_four, v.loc1, v.g2)
+    comm.relay_finish(v.g1, 1)
+    comm.relay_start(v.g2, 2)
+    opm(v.loc0, v.g1, 0, lambda i: v.z[i].astype(F32), v.ts_b[0], v.g3, lambda: comm.relay_step(v.g2, 2, 1))
     comm.gather_start(v.g3, 3)
+    comm.relay_step(v.g2, 2, 2)
     tri_project(v.ts_t[0], v.ts_k[0])
     comm.gather_finish(v.g3, 3)
+    comm.relay_step(v.g2, 2, 3)
     spread_bias(v.g3, v.gf2, v.tbias, True, v.mask_r[...])
-    tri_attend(v.ts_o[0], send_pair(v.s2, v.r2, 9, rl))
-    comm.gather_start(v.g2, 2)
+    tri_attend(v.ts_o[0], send_pair(v.s2, v.r2, 9, rl, v.te_b[0], v.g4))
+    comm.gather_start(v.g4, 4)
     comm.swap_finish(v.s2, v.r2, 9)
     turn(v.r2)
-    bias_pieces(zload, rl, v.te_b[0], store_piece(v.g4))
-    comm.gather_start(v.g4, 4)
-    comm.swap_start(v.s1, v.r1, 10, 0, rows_m)
     tri_project(v.te_t[0], v.te_k[0])
     comm.gather_finish(v.g4, 4)
-    spread_bias(v.g4, v.gf2, v.tbias, True, v.mask_r[...])
-    tri_attend(v.te_o[0], keep_pair(v.zc))
-
-    bias_pieces(zload, rl, v.row_b[1], store_piece(v.g5))
-    comm.gather_start(v.g5, 5)
-    comm.gather_finish(v.g2, 2)
-    opm(v.loc1, v.g2, 1, zload, v.te_b[1], v.g6)
+    comm.swap_start(v.s1, v.r1, 10, 0, rows_m)
+    spread_bias(v.g4, v.gf2, v.tbias, False, v.mask_r[...])
+    tri_attend(v.te_o[0], keep_pair(v.zc, v.row_b[1], v.g5))
+
+    comm.relay_finish(v.g2, 2)
+    comm.relay_start(v.g5, 5)
+    opm(v.loc1, v.g2, 1, zload, v.te_b[1], v.g6, lambda: comm.relay_step(v.g5, 5, 1))
     comm.gather_start(v.g6, 6)
+    comm.relay_step(v.g5, 5, 2)
     comm.swap_finish(v.s1, v.r1, 10)
     fill(v.mwork, v.r1)
     rload = lambda s: take(v.mwork, s, nr, sl)
     row_project(rload, 1)
+    comm.relay_step(v.g5, 5, 3)
     tri_project(v.te_t[1], v.te_k[1])
-    comm.gather_finish(v.g5, 5)
     comm.gather_finish(v.g6, 6)
     spread_bias(v.g6, v.gf2, v.tbias, True, v.mask_r[...])
-    tri_attend(v.te_o[1], send_pair(v.s3, v.r3, 11, rl))
+    tri_attend(v.te_o[1], send_pair(v.s3, v.r3, 11, rl, v.ts_b[1], v.g7))
+    comm.gather_start(v.g7, 7)
+    comm.relay_finish(v.g5, 5)
     spread_bias(v.g5, v.gf, v.rbias, False, None)
     row_attend(rload, 1, keep_pair(v.m_out))
     comm.swap_finish(v.s3, v.r3, 11)
     turn(v.r3)
-    bias_pieces(zload, rl, v.ts_b[1], store_piece(v.g7))
-    comm.gather_start(v.g7, 7)
     tri_project(v.ts_t[1], v.ts_k[1])
     comm.gather_finish(v.g7, 7)
-    spread_bias(v.g7, v.gf2, v.tbias, True, v.mask_r[...])
+    spread_bias(v.g7, v.gf2, v.tbias, False, v.mask_r[...])
     tri_attend(v.ts_o[1], keep_pair(v.z_out))
 
 

time: 219 us -> 198 us (0.904)
  Pallas kernels: 201 us -> 179 us
    pallas_call x1, Pallas kernels: 201 us -> 179 us  [local_step(): pl.pallas_call(lambda *refs: kernel(names, outs, nd, refs), out_shape=[ja...]
where the time goes in v4:
time: 198 us; the launch traced here: 196 us
  Pallas kernels  179 us (90%)
  local copies, waits for them, and re-layouts  13.7 us (7%)
  other arithmetic  2.55 us (1%)
    pallas_call x1, Pallas kernels, local_step(): pl.pallas_call(lambda *refs: kernel(names, outs, nd, refs), out_shape=[ja...  179 us
    unnamed x21, local copies, waits for them, and re-layouts  7.87 us

profile of v4, /device:TPU:21, one launch (start us, length us, event | category | flops | bytes accessed | tf_op | source)
XLA Modules:
  0.0 196.4 jit_solution(7112179349472317062)
XLA Ops:
  0.6 0.7 copy-done.6
  1.3 0.5 convert_element_type.11
  1.8 1.0 fusion.5
  2.8 0.6 dynamic-slice_bitcast_fusion.refs_3_
  3.5 0.7 copy.67.refs_2_
  4.2 0.7 copy.68.refs_4_
  4.9 0.7 copy.77
  5.7 0.7 copy.58
  6.4 0.3 copy-done.5
  6.8 0.7 copy.80
  7.5 0.7 copy.62
  8.3 0.1 copy.81
  8.4 0.1 copy.65
  8.5 0.1 copy.66
  8.7 0.8 pad_maximum_fusion.refs_22_
  9.7 0.8 copy.71
  10.5 0.1 maximum_bitcast_fusion
  10.6 0.9 copy.50
  11.6 0.6 copy-done.1
  12.2 0.8 copy.74
  13.1 0.9 copy.54
  14.1 179.4 %shard_map.176 = (bf16[8,192,256]{2,1,0:T(8,128)(2,1)}, bf16[12,192,128]{2,1,0:T(8,128)(2,1)}) custom-call(bf16[8,192,256]{2,1,0:T(8,128)(2,1)} %refs_0_.1, bf16[12,192,128]{2,1,0:T(8,128)(2,1)} %refs_1_.1, f32[8,192]{1,0:T(8,128)} %copy.67.refs_2_, f32[12,128]{1,0:T(8,128)} %dynamic-slice_bitcast_fusion.refs_3_, bf16[128,192]{1,0:T(8,128)(2,1)} %copy.68.refs_4_, ...), custom_call_target="tpu_custom_call" | custom-call | tf_op jit(solution)/shard_map/pallas_call | solution.py:518
  193.5 2.1 %copy.84 = bf16[8,192,256]{2,1,0:T(8,128)(2,1)} copy(bf16[8,192,256]{2,1,0:T(8,128)(2,1)} %get-tuple-element.24) | data formatting | bytes 1572864
  195.6 0.8 copy.85
  (20 shorter events, 0.5 us)
Async XLA Ops:
  0.6 0.7 copy-start.6
  2.8 2.1 %copy-start.4 = (bf16[2,128,4,4,32]{1,4,3,2,0:T(8,128)(2,1)S(1)}, bf16[2,128,4,4,32]{1,4,3,2,0:T(8,128)(2,1)}, u32[]{:S(2)}) copy-start(bf16[2,128,4,4,32]{1,4,3,2,0:T(8,128)(2,1)} %param.29) | copy-start | bytes 786436
  5.7 1.0 copy-start.5
  6.7 1.5 copy-start.3
  8.4 1.2 copy-start
  10.6 1.5 copy-start.1
  193.5 2.1 %copy-start.2 = (bf16[12,192,128]{2,1,0:T(8,128)(2,1)S(1)}, bf16[12,192,128]{2,1,0:T(8,128)(2,1)}, u32[]{:S(2)}) copy-start(bf16[12,192,128]{2,1,0:T(8,128)(2,1)} %get-tuple-element.25) | copy-start | bytes 1769476

commit v5 on v4

--- a/solution.py
+++ b/solution.py
@@ -26,13 +26,14 @@
     return (cen * lax.rsqrt(var + 1e-5)).astype(BF16)
 
 
-def project(xs, wt, wk, t_ref, k_ref, first, kcol):
+def project(xs, w, t_ref, k_ref, first, kcol):
+    width = w.shape[0] // 4
     xl = [layer_norm(x) for x in xs]
-    ts = [dot(wt[...], v, 1, 1) for v in xl]
-    ks = [dot(v, wk[...], 1, 0) for v in xl]
-    for n, v in enumerate(ts):
-        t_ref[first + n] = v.astype(BF16)
-    for n, v in enumerate(ks):
+    for n, v in enumerate([dot(w[:width], v, 1, 1) for v in xl]):
+        t_ref[first + n, 0:width] = v.astype(BF16)
+    for n, v in enumerate([dot(w[2 * width:], v, 1, 1) for v in xl]):
+        t_ref[first + n, width:3 * width] = v.astype(BF16)
+    for n, v in enumerate([dot(v, w[width:2 * width], 1, 1) for v in xl]):
         if kcol is not None:
             v = v * kcol
         k_ref[first + n] = v.astype(BF16)
@@ -58,6 +59,7 @@
     for n, b, g in units:
         t = t_ref[b, 128 * g:128 * g + 128, :]
         scores.append(dot(k_ref[b, :, 128 * g:128 * g + 128], diagonal(t, 0, length), 1, 0))
+    yield
     probs = []
     dens = []
     for (n, b, g), s in zip(units, scores):
@@ -69,7 +71,9 @@
         e = jnp.exp2(s - jnp.max(s, axis=0, keepdims=True))
         dens.append(jnp.sum(e, axis=0, keepdims=True))
         probs.append(e.astype(BF16))
+    yield
     outs = [dot(t_ref[b, width + 128 * g:width + 128 * g + 128, :], p, 1, 0) for (n, b, g), p in zip(units, probs)]
+    yield
     for (n, b, g), o, den in zip(units, outs, dens):
         inv = 1.0 / den
         gate = jax.nn.sigmoid(t_ref[b, 2 * width + 128 * g:2 * width + 128 * g + 128, :].astype(F32))
@@ -78,6 +82,16 @@
             lanes = slice(length * r, length * r + length)
             parts.append(o[HEAD * r:HEAD * r + HEAD, lanes] * inv[:, lanes])
         o_ref[b, 128 * g:128 * g + 128, :] = (jnp.concatenate(parts, axis=0) * gate).astype(BF16)
+
+
+def interleave(*gens):
+    live = list(gens)
+    while live:
+        for gen in list(live):
+            try:
+                next(gen)
+            except StopIteration:
+                live.remove(gen)
 
 
 def residual(x, update):
@@ -228,11 +242,10 @@
     def swap_start(self, send, recv, i, off, rows):
         part = pl.ds(off, rows)
 
-        def body(k, _):
-            d = self.near(k, 1)
+        for k in range(1, self.nd):
+            off = (k + 1) // 2 if k % 2 else -(k // 2)
+            d = lax.rem(self.me + self.nd + off, self.nd)
             self.copy(send.at[d, part], recv.at[self.me, part], self.ssem.at[i], self.rsem.at[i], d).start()
-            return 0
-        lax.fori_loop(1, self.nd, body, 0)
         pltpu.make_async_copy(send.at[self.me, part], recv.at[self.me, part], self.rsem.at[i]).start()
 
     def swap_finish(self, send, recv, i):
@@ -249,7 +262,7 @@
     sl, nr, cm = v.m.shape
     rl, _, cz = v.z.shape
     ns = sl * nd
-    wm, wz = v.row_k.shape[2], v.ts_k.shape[2]
+    wm, wz = v.row_w.shape[1] // 4, v.ts_w.shape[1] // 4
     gm, gz = wm // 128, wz // 128
     od = v.opm_i.shape[1] // 2
     comm = Comm(nd, (v.ssem, v.rsem, v.fsem, v.gsem))
@@ -268,26 +281,35 @@
         lax.fori_loop(0, n, step, 0)
 
     def row_project(load, b):
-        loop(sl // 2, lambda t: project([load(2 * t), load(2 * t + 1)], v.row_t[b], v.row_k[b], v.rt, v.rk, 2 * t, None))
+        loop(sl // 2, lambda t: project([load(2 * t), load(2 * t + 1)], v.row_w.at[b], v.rt, v.rk, 2 * t, None))
 
     def row_attend(load, b, finish):
-        def body(t):
-            for n in range(2):
-                keep = widen(spread(v.mask_seq[pl.ds(2 * t + n, 1), :], 128), 4 * nr)
-                core(v.rt, v.rk, v.ro, [2 * t + n], gm, v.rbias, [keep])
+        def attend(s):
+            keep = widen(spread(v.mask_seq[pl.ds(s, 1), :], 128), 4 * nr)
+            return core(v.rt, v.rk, v.ro, [s], gm, v.rbias, [keep])
+
+        def back(t):
             ups = [dot(v.ro[2 * t + n], v.row_o[b], 0, 0) for n in range(2)]
-            finish(t, [residual(load(2 * t + n), ups[n]) for n in range(2)])
-        loop(sl // 2, body)
+            yield
+            yield from finish(t, [residual(load(2 * t + n), ups[n]) for n in range(2)])
+
+        def body(u):
+            interleave(back(u), attend(2 * u + 2))
+            interleave(attend(2 * u + 3))
+        interleave(attend(0))
+        interleave(attend(1))
+        loop(sl // 2 - 1, body)
+        interleave(back(sl // 2 - 1))
 
     def col_project(load, b):
-        loop(rl // 4, lambda t: project([load(4 * t + n) for n in range(4)], v.col_t[b], v.col_k[b], v.ct, v.ck, 4 * t, None))
+        loop(rl // 4, lambda t: project([load(4 * t + n) for n in range(4)], v.col_w.at[b], v.ct, v.ck, 4 * t, None))
 
     def col_attend(first, count):
         def body(u):
             t = first + u
             rows = [2 * t, 2 * t + 1]
             keeps = [widen(spread(v.mask_col[pl.ds(i, 1), :], 128), 4 * ns) for i in rows]
-            core(v.ct, v.ck, v.co, rows, gm, None, keeps)
+            interleave(core(v.ct, v.ck, v.co, rows, gm, None, keeps))
         loop(count, body)
 
     def col_out(load, b, finish, loc, gat):
@@ -308,7 +330,7 @@
 
     def opm(loc, gat, b, load, wb, piece, between):
         v.gcol[...] = gat[...].astype(F32).reshape(v.gcol.shape)
-        v.nrm[...] = dot(v.mask_col[...].astype(BF16), v.mask_b[...], 1, 0)
+        v.nrm[...] = dot(v.mask_col[...].astype(BF16), v.msa_mask[...].astype(F32).astype(BF16), 1, 0)
 
         def grow(t):
             left = loc[...].reshape(rl * od, ns)
@@ -324,7 +346,7 @@
 
         def fold(t):
             rows = [4 * t + n for n in range(4)]
-            ups = [dot(v.opm_o[b], v.xs[i], 1, 0) for i in rows]
+            ups = [dot(v.opm_w[b], v.xs[i], 1, 0) for i in rows]
             ups = [u / (1e-3 + v.nrm[pl.ds(i, 1), :]) for i, u in zip(rows, ups)]
             ups = [u.T for u in ups]
             new = [residual(load(i), u) for i, u in zip(rows, ups)]
@@ -339,35 +361,51 @@
     def zload(i):
         return v.zc[i].astype(F32)
 
-    def tri_project(wt, wk):
-        loop(rl // 4, lambda t: project([zload(4 * t + n) for n in range(4)], wt, wk, v.tt, v.tk, 4 * t, v.kc[...]))
+    def tri_project(w):
+        loop(rl // 4, lambda t: project([zload(4 * t + n) for n in range(4)], w, v.tt, v.tk, 4 * t, v.kc[...]))
 
     def tri_attend(wo, finish):
-        def body(t):
-            core(v.tt, v.tk, v.to, [2 * t, 2 * t + 1], gz, v.tbias, None)
-            rows = [2 * t, 2 * t + 1]
+        def attend(t):
+            return core(v.tt, v.tk, v.to, [4 * t + n for n in range(4)], gz, v.tbias, None)
+
+        def back(t):
+            rows = [4 * t + n for n in range(4)]
             ups = [dot(v.to[i], wo, 0, 0) for i in rows]
-            finish(t, [residual(zload(i), u) for i, u in zip(rows, ups)])
-        loop(rl // 2, body)
-
-    def pair_pieces(t, pair, wb, piece):
-        ps = [dot(wb, layer_norm(x.astype(F32)), 1, 1) for x in pair]
+            yield
+            yield from finish(t, [residual(zload(i), u) for i, u in zip(rows, ups)])
+
+        interleave(attend(0))
+        loop(rl // 4 - 1, lambda u: interleave(back(u), attend(u + 1)))
+        interleave(back(rl // 4 - 1))
+
+    def pieces(t, new, wb, piece):
+        ln = [layer_norm(x.astype(F32)) for x in new]
+        yield
+        ps = [dot(wb, x, 1, 1) for x in ln]
         for n, x in enumerate(ps):
-            piece[me * rl + 2 * t + n] = x.astype(BF16)
-
-    def send_pair(send, recv, i, rows, wb=None, piece=None):
-        def finish(t, pair):
-            stage(send, t, pair[0].astype(F32), pair[1].astype(F32), nd)
-            comm.swap_start(send, recv, i, pl.multiple_of(2 * rows * t, 8), 2 * rows)
+            piece[me * rl + len(new) * t + n] = x.astype(BF16)
+
+    def send(out, recv, i, rows, wb=None, piece=None):
+        def finish(t, new):
+            half = len(new) // 2
+            for n in range(half):
+                stage(out, half * t + n, new[2 * n].astype(F32), new[2 * n + 1].astype(F32), nd)
+            count = len(new) * rows
+            comm.swap_start(out, recv, i, pl.multiple_of(count * t, 8), count)
             if piece is not None:
-                pair_pieces(t, pair, wb, piece)
+                yield from pieces(t, new, wb, piece)
+            else:
+                yield
         return finish
 
-    def keep_pair(out, wb=None, piece=None):
-        def finish(t, pair):
-            out[2 * t], out[2 * t + 1] = pair
+    def keep(out, wb=None, piece=None):
+        def finish(t, new):
+            for n, x in enumerate(new):
+                out[len(new) * t + n] = x
             if piece is not None:
-                pair_pieces(t, pair, wb, piece)
+                yield from pieces(t, new, wb, piece)
+            else:
+                yield
         return finish
 
     def turn(recv):
@@ -375,16 +413,33 @@
         for b in range(rl):
             v.zc[b] = take(v.zwork, b, nr, rl).astype(BF16)
 
+    def mask_r():
+        return v.res_mask[...].astype(F32)
+
+    def prepare():
+        v.mask_t[...] = v.msa_mask[...].astype(F32).T
+        v.mask_seq[...] = v.msa_mask[pl.ds(pl.multiple_of(me * sl, sl), sl), :].astype(F32)
+        for i in range(rl):
+            v.mask_col[pl.ds(i, 1), :] = v.mask_t[pl.ds(me * rl + i, 1), :]
+        v.kc[...] = spread(mask_r(), wz)
+        size = od * od
+        v.gcol[0:size] = v.opm_o[0].astype(F32)
+        for q in range(od):
+            v.gcol[size + od * q:size + od * q + od] = v.gcol[pl.ds(q, od, stride=od), :]
+        for j in range(size // 128):
+            v.opm_w[0, :, 128 * j:128 * j + 128] = v.gcol[size + 128 * j:size + 128 * j + 128].T.astype(BF16)
+            v.opm_w[1, :, 128 * j:128 * j + 128] = v.opm_o[1, 128 * j:128 * j + 128, :].astype(F32).T.astype(BF16)
+
     comm.barrier_signal()
     bias_pieces(lambda i: v.z[i].astype(F32), rl, v.row_b[0], store_piece(v.g0))
-    v.kc[...] = spread(v.mask_r[...], wz)
     comm.barrier_wait()
     comm.gather_start(v.g0, 0)
     mload = lambda s: v.m[s].astype(F32)
     row_project(mload, 0)
+    prepare()
     comm.gather_finish(v.g0, 0)
     spread_bias(v.g0, v.gf, v.rbias, True, None)
-    row_attend(mload, 0, send_pair(v.s0, v.r0, 8, rl))
+    row_attend(mload, 0, send(v.s0, v.r0, 8, rl))
     comm.swap_finish(v.s0, v.r0, 8)
 
     fill(v.mwork, v.r0)
@@ -415,19 +470,19 @@
     opm(v.loc0, v.g1, 0, lambda i: v.z[i].astype(F32), v.ts_b[0], v.g3, lambda: comm.relay_step(v.g2, 2, 1))
     comm.gather_start(v.g3, 3)
     comm.relay_step(v.g2, 2, 2)
-    tri_project(v.ts_t[0], v.ts_k[0])
+    tri_project(v.ts_w.at[0])
     comm.gather_finish(v.g3, 3)
     comm.relay_step(v.g2, 2, 3)
-    spread_bias(v.g3, v.gf2, v.tbias, True, v.mask_r[...])
-    tri_attend(v.ts_o[0], send_pair(v.s2, v.r2, 9, rl, v.te_b[0], v.g4))
+    spread_bias(v.g3, v.gf2, v.tbias, True, mask_r())
+    tri_attend(v.ts_o[0], send(v.s2, v.r2, 9, rl, v.te_b[0], v.g4))
     comm.gather_start(v.g4, 4)
     comm.swap_finish(v.s2, v.r2, 9)
     turn(v.r2)
-    tri_project(v.te_t[0], v.te_k[0])
+    tri_project(v.te_w.at[0])
     comm.gather_finish(v.g4, 4)
     comm.swap_start(v.s1, v.r1, 10, 0, rows_m)
-    spread_bias(v.g4, v.gf2, v.tbias, False, v.mask_r[...])
-    tri_attend(v.te_o[0], keep_pair(v.zc, v.row_b[1], v.g5))
+    spread_bias(v.g4, v.gf2, v.tbias, False, mask_r())
+    tri_attend(v.te_o[0], keep(v.zc, v.row_b[1], v.g5))
 
     comm.relay_finish(v.g2, 2)
     comm.relay_start(v.g5, 5)
@@ -439,27 +494,26 @@
     rload = lambda s: take(v.mwork, s, nr, sl)
     row_project(rload, 1)
     comm.relay_step(v.g5, 5, 3)
-    tri_project(v.te_t[1], v.te_k[1])
+    tri_project(v.te_w.at[1])
     comm.gather_finish(v.g6, 6)
-    spread_bias(v.g6, v.gf2, v.tbias, True, v.mask_r[...])
-    tri_attend(v.te_o[1], send_pair(v.s3, v.r3, 11, rl, v.ts_b[1], v.g7))
+    spread_bias(v.g6, v.gf2, v.tbias, True, mask_r())
+    tri_attend(v.te_o[1], send(v.s3, v.r3, 11, rl, v.ts_b[1], v.g7))
     comm.gather_start(v.g7, 7)
     comm.relay_finish(v.g5, 5)
     spread_bias(v.g5, v.gf, v.rbias, False, None)
-    row_attend(rload, 1, keep_pair(v.m_out))
+    row_attend(rload, 1, keep(v.m_out))
     comm.swap_finish(v.s3, v.r3, 11)
     turn(v.r3)
-    tri_project(v.ts_t[1], v.ts_k[1])
+    tri_project(v.ts_w.at[1])
     comm.gather_finish(v.g7, 7)
-    spread_bias(v.g7, v.gf2, v.tbias, False, v.mask_r[...])
-    tri_attend(v.ts_o[1], keep_pair(v.z_out))
+    spread_bias(v.g7, v.gf2, v.tbias, False, mask_r())
+    tri_attend(v.ts_o[1], keep(v.z_out))
 
 
 def solution(mesh):
     nd = mesh.shape['dap']
 
     def local_step(m, z, msa_mask, res_mask, w_row_bias, w_row_in, w_row_out, w_col_in, w_col_out, w_opm_in, w_opm_out, w_ts_bias, w_ts_in, w_ts_out, w_te_bias, w_te_in, w_te_out):
-        me = lax.axis_index('dap')
         sl, nr, cm = m.shape
         rl, _, cz = z.shape
         ns = sl * nd
@@ -467,36 +521,15 @@
         wm, wz = hm * HEAD, ht * HEAD
         od = w_opm_in.shape[3]
 
-        maskf = msa_mask.astype(F32)
-        mask_seq = lax.dynamic_slice_in_dim(maskf, me * sl, sl, 0)
-        mask_col = lax.dynamic_slice_in_dim(maskf, me * rl, rl, 1).T
-        mask_b = msa_mask.astype(BF16)
-        mask_r = res_mask.astype(F32)[None, :]
-
-        def split(w, width):
-            c = w.shape[1]
-            w = w.reshape(2, c, 4, width)
-            wt = jnp.stack([w[:, :, 0], w[:, :, 2], w[:, :, 3]], axis=1)
-            return wt.transpose(0, 1, 3, 2).reshape(2, 3 * width, c), w[:, :, 1]
-
-        row_t, row_k = split(w_row_in, wm)
-        col_t, col_k = split(w_col_in, wm)
-        ts_t, ts_k = split(w_ts_in, wz)
-        te_t, te_k = split(w_te_in, wz)
-        row_o = w_row_out.reshape(2, wm, cm)
-        col_o = w_col_out.reshape(2, wm, cm)
-        ts_o = w_ts_out.reshape(2, wz, cz)
-        te_o = w_te_out.reshape(2, wz, cz)
-        row_b = w_row_bias.transpose(0, 2, 1)
-        ts_b = w_ts_bias.transpose(0, 2, 1)
-        te_b = w_te_bias.transpose(0, 2, 1)
-        opm_i = w_opm_in.reshape(2, cm, 2 * od).transpose(0, 2, 1)
-        opm_o = jnp.stack([w_opm_out[0].transpose(2, 1, 0), w_opm_out[1].transpose(2, 0, 1)]).reshape(2, cz, od * od)
-
-        ins = dict(m=m, z=z, mask_seq=mask_seq, mask_col=mask_col, mask_b=mask_b, mask_r=mask_r,
-                   row_t=row_t, row_k=row_k, row_o=row_o, row_b=row_b, col_t=col_t, col_k=col_k, col_o=col_o,
-                   ts_t=ts_t, ts_k=ts_k, ts_o=ts_o, ts_b=ts_b, te_t=te_t, te_k=te_k, te_o=te_o, te_b=te_b,
-                   opm_i=opm_i, opm_o=opm_o)
+        def rows_of(w):
+            return jnp.moveaxis(w, 1, -1).reshape(2, -1, w.shape[1])
+
+        ins = dict(m=m, z=z, msa_mask=msa_mask, res_mask=res_mask[None, :],
+                   row_w=rows_of(w_row_in), row_o=w_row_out.reshape(2, wm, cm), row_b=rows_of(w_row_bias),
+                   col_w=rows_of(w_col_in), col_o=w_col_out.reshape(2, wm, cm),
+                   ts_w=rows_of(w_ts_in), ts_o=w_ts_out.reshape(2, wz, cz), ts_b=rows_of(w_ts_bias),
+                   te_w=rows_of(w_te_in), te_o=w_te_out.reshape(2, wz, cz), te_b=rows_of(w_te_bias),
+                   opm_i=rows_of(w_opm_in), opm_o=w_opm_out.reshape(2, od * od, cz))
         outs = dict(m_out=m, z_out=z)
         gm, gz = wm // 128, wz // 128
         xm, xz = (nd, sl * rl, cm), (nd, rl * rl, cz)
@@ -512,6 +545,7 @@
             rt=((sl, 3 * wm, nr), BF16), rk=((sl, nr, wm), BF16), ro=((sl, wm, nr), BF16),
             ct=((rl, 3 * wm, ns), BF16), ck=((rl, ns, wm), BF16), co=((rl, wm, ns), BF16),
             tt=((rl, 3 * wz, nr), BF16), tk=((rl, nr, wz), BF16), to=((rl, wz, nr), BF16),
+            mask_t=((nr, ns), F32), mask_seq=((sl, nr), F32), mask_col=((rl, ns), F32), opm_w=((2, cz, od * od), BF16),
             mc=((rl, ns, cm), BF16), zc=((rl, nr, cz), BF16), loc0=((rl, od, ns), BF16), loc1=((rl, od, ns), BF16))
         sems = dict(ssem=(12,), rsem=(12,), fsem=(8,), gsem=(8, nd // 2))
         names = list(ins) + list(outs) + list(scratch) + list(sems)

time: 198 us -> 184 us (0.929)
  local copies, waits for them, and re-layouts: 13.7 us -> 4.59 us
  other arithmetic: 2.55 us -> 0 us
    transpose x5 -> x0, local copies, waits for them, and re-layouts: 3.89 us -> none  [the longest x4 3.28 us: split(): return (wt.transpose(0, 1, 3, 2).reshape(2, 3 * width, c), w[:, :, 1])]
    unnamed x21 -> x5, local copies, waits for them, and re-layouts: 7.87 us -> 4.59 us
where the time goes in v5:
time: 184 us
  Pallas kernels  179 us (97%)
  local copies, waits for them, and re-layouts  4.59 us (2%)
    pallas_call x1, Pallas kernels, local_step(): pl.pallas_call(lambda *refs: kernel(names, outs, nd, refs), out_shape=[ja...  179 us
    unnamed x5, local copies, waits for them, and re-layouts  4.59 us

profile of v5, /device:TPU:21, one launch (start us, length us, event | category | flops | bytes accessed | tf_op | source)
XLA Modules:
  0.0 184.0 jit_solution(1127634886179287434)
XLA Ops:
  0.6 1.6 copy.19.refs_2_
  2.3 178.8 %shard_map.176 = (bf16[8,192,256]{2,1,0:T(8,128)(2,1)}, bf16[12,192,128]{2,1,0:T(8,128)(2,1)}) custom-call(bf16[8,192,256]{2,1,0:T(8,128)(2,1)} %refs_0_.1, bf16[12,192,128]{2,1,0:T(8,128)(2,1)} %refs_1_.1, s32[128,192]{1,0:T(8,128)} %copy.19.refs_2_, s32[1,192]{1,0:T(1,128)} %bitcast.37, bf16[2,1024,256]{2,1,0:T(8,128)(2,1)} %bitcast.24, ...), custom_call_target="tpu_custom_call" | custom-call | tf_op jit(solution)/shard_map/pallas_call | solution.py:552
  181.1 0.0 copy-start
  181.1 2.1 %copy.22 = bf16[8,192,256]{2,1,0:T(8,128)(2,1)} copy(bf16[8,192,256]{2,1,0:T(8,128)(2,1)} %get-tuple-element.4) | data formatting | bytes 1572864
  183.2 0.0 copy-done
  183.2 0.8 copy.23
Async XLA Ops:
  181.1 2.1 %copy-start = (bf16[12,192,128]{2,1,0:T(8,128)(2,1)S(1)}, bf16[12,192,128]{2,1,0:T(8,128)(2,1)}, u32[]{:S(2)}) copy-start(bf16[12,192,128]{2,1,0:T(8,128)(2,1)} %get-tuple-element.5) | copy-start | bytes 1769476

commit v6 on v5

--- a/solution.py
+++ b/solution.py
@@ -153,7 +153,7 @@
         self.nd = nd
         self.me = lax.axis_index('dap')
         self.partner = self.me + 1 - 2 * lax.rem(self.me, 2)
-        self.ssem, self.rsem, self.fsem, self.gsem = sems
+        self.ssem, self.rsem, self.fsem, self.gsem, self.xsem = sems
 
     def copy(self, src, dst, send, recv, dev):
         return pltpu.make_async_remote_copy(src_ref=src, dst_ref=dst, send_sem=send, recv_sem=recv,
@@ -177,80 +177,110 @@
     def await_bytes(self, ref, sem):
         pltpu.make_async_copy(ref, ref, sem).wait()
 
+    def at(self, chips, same=True):
+        base = self.me if same else self.partner
+        return lax.rem(base + self.nd + 2 * chips, self.nd)
+
+    def slot(self, buf, chips, start=0, count=None):
+        n = buf.shape[0] // self.nd
+        return buf.at[pl.ds(self.at(chips) * n + start, n if count is None else count)]
+
     def gather_start(self, buf, i):
-        n = buf.shape[0] // self.nd
-        own = buf.at[pl.ds(self.me * n, n)]
+        own = self.slot(buf, 0)
 
         def body(k, _):
-            self.copy(own, own, self.ssem.at[i], self.gsem.at[i, k], self.near(k, 2)).start()
+            self.copy(own, own, self.ssem.at[i], self.gsem.at[i, k, 0], self.near(k, 2)).start()
             return 0
-        lax.fori_loop(1, self.nd // 2, body, 0)
-        self.copy(own, own, self.ssem.at[i], self.gsem.at[i, 0], self.partner).start()
+        lax.fori_loop(1, self.nd // 2 - 1, body, 0)
+        self.copy(own, own, self.ssem.at[i], self.gsem.at[i, 0, 0], self.partner).start()
 
     def gather_finish(self, buf, i):
         n = buf.shape[0] // self.nd
         half = self.nd // 2
+        far = self.nd // 4
+
+        def across(ref):
+            self.copy(ref, ref, self.fsem.at[i], self.rsem.at[i], self.partner).start()
 
         def body(k, _):
             slot = buf.at[pl.ds(self.near(k, -2) * n, n)]
-            self.await_bytes(slot, self.gsem.at[i, k])
-            self.copy(slot, slot, self.fsem.at[i], self.rsem.at[i], self.partner).start()
+            self.await_bytes(slot, self.gsem.at[i, k, 0])
+            across(slot)
             return 0
-        lax.fori_loop(1, half, body, 0)
-        self.await_bytes(buf.at[pl.ds(0, n)], self.gsem.at[i, 0])
+        lax.fori_loop(1, half - 3, body, 0)
+        for part, sign in ((0, 1), (1, -1)):
+            self.await_bytes(self.slot(buf, sign * (1 - far)), self.gsem.at[i, half - 3 + part, 0])
+            on = self.slot(buf, sign * (1 - far), part * (n // 2), n // 2)
+            self.copy(on, on, self.fsem.at[i], self.gsem.at[i, half - 1 + part, 0], self.at(sign)).start()
+            across(self.slot(buf, sign * (1 - far)))
+        for part in range(2):
+            self.await_bytes(self.slot(buf, far, part * (n // 2), n // 2), self.gsem.at[i, half - 1 + part, 0])
+        across(self.slot(buf, far))
+        self.await_bytes(buf.at[pl.ds(0, n)], self.gsem.at[i, 0, 0])
         rest = buf.at[pl.ds(0, (half - 1) * n)]
         self.await_bytes(rest, self.rsem.at[i])
-        self.await_bytes(rest, self.fsem.at[i])
-        self.await_bytes(buf.at[pl.ds(0, half * n)], self.ssem.at[i])
-
-    def slot(self, buf, off, part=None):
-        n = buf.shape[0] // self.nd
-        base = lax.rem(self.me + self.nd + 2 * off, self.nd) * n
-        if part is None:
-            return buf.at[pl.ds(base, n)]
-        return buf.at[pl.ds(base + part * (n // 2), n // 2)]
+        self.await_bytes(buf.at[pl.ds(0, half * n)], self.fsem.at[i])
+        self.await_bytes(rest, self.ssem.at[i])
 
     def relay(self, ref, i, recv, dev):
         self.copy(ref, ref, self.ssem.at[i], recv, dev).start()
 
-    def relay_start(self, buf, i):
-        own = self.slot(buf, 0)
-        right, left = lax.rem(self.me + 2, self.nd), lax.rem(self.me + self.nd - 2, self.nd)
-        self.relay(own, i, self.gsem.at[i, 0], right)
-        self.relay(own, i, self.gsem.at[i, 4], left)
+    def relay_start(self, buf, i, c=0, nc=1):
+        m = buf.shape[0] // self.nd // nc
+        own = self.slot(buf, 0, c * m, m)
+        self.relay(own, i, self.gsem.at[i, 0, c], self.at(1))
+        self.relay(own, i, self.gsem.at[i, 4, c], self.at(-1))
         self.relay(own, i, self.rsem.at[i], self.partner)
 
-    def relay_step(self, buf, i, p):
-        right, left = lax.rem(self.me + 2, self.nd), lax.rem(self.me + self.nd - 2, self.nd)
-        for sign, base, dev, part in ((-1, 0, right, 0), (1, 4, left, 1)):
-            ref = self.slot(buf, sign * p)
-            self.await_bytes(ref, self.gsem.at[i, base + p - 1])
-            on = self.slot(buf, sign * p, part) if p == self.nd // 4 - 1 else ref
-            self.relay(on, i, self.gsem.at[i, base + p], dev)
+    def relay_step(self, buf, i, p, c=0, nc=1):
+        m = buf.shape[0] // self.nd // nc
+        for part, sign in ((0, 1), (1, -1)):
+            ref = self.slot(buf, -sign * p, c * m, m)
+            self.await_bytes(ref, self.gsem.at[i, 4 * part + p - 1, c])
+            on = self.slot(buf, -sign * p, c * m + part * (m // 2), m // 2) if p == self.nd // 4 - 1 else ref
+            self.relay(on, i, self.gsem.at[i, 4 * part + p, c], self.at(sign))
             self.relay(ref, i, self.rsem.at[i], self.partner)
 
-    def relay_finish(self, buf, i):
+    def relay_finish(self, buf, i, nc=1):
         n = buf.shape[0] // self.nd
+        m = n // nc
         half = self.nd // 2
-        far = self.slot(buf, self.nd // 4)
-        for part in range(2):
-            self.await_bytes(self.slot(buf, self.nd // 4, part), self.gsem.at[i, 4 * part + self.nd // 4 - 1])
-        self.relay(far, i, self.rsem.at[i], self.partner)
+        for c in range(nc):
+            for part in range(2):
+                ref = self.slot(buf, self.nd // 4, c * m + part * (m // 2), m // 2)
+                self.await_bytes(ref, self.gsem.at[i, 4 * part + self.nd // 4 - 1, c])
+        self.relay(self.slot(buf, self.nd // 4), i, self.rsem.at[i], self.partner)
         self.await_bytes(buf.at[pl.ds(0, half * n)], self.rsem.at[i])
         self.await_bytes(buf.at[pl.ds(0, (2 * half - 1) * n)], self.ssem.at[i])
 
-    def swap_start(self, send, recv, i, off, rows):
-        part = pl.ds(off, rows)
-
-        for k in range(1, self.nd):
-            off = (k + 1) // 2 if k % 2 else -(k // 2)
-            d = lax.rem(self.me + self.nd + off, self.nd)
-            self.copy(send.at[d, part], recv.at[self.me, part], self.ssem.at[i], self.rsem.at[i], d).start()
+    def swap_start(self, send, recv, via, i, t, rows):
+        part = pl.ds(pl.multiple_of(rows * t, 8), rows)
+        far = self.nd // 4
+        for same, sign in ((True, 1), (False, -1)):
+            x = 0 if same else 1
+            self.copy(send.at[self.at(far, same), part], via.at[x, part], self.ssem.at[i],
+                      self.xsem.at[i - 8, x, t], self.at(sign)).start()
+        for k in range(1, far):
+            for sign in (1, -1):
+                for same in (True, False):
+                    d = self.at(sign * k, same)
+                    self.copy(send.at[d, part], recv.at[self.me, part], self.ssem.at[i], self.rsem.at[i], d).start()
+        self.copy(send.at[self.partner, part], recv.at[self.me, part], self.ssem.at[i], self.rsem.at[i], self.partner).start()
         pltpu.make_async_copy(send.at[self.me, part], recv.at[self.me, part], self.rsem.at[i]).start()
 
-    def swap_finish(self, send, recv, i):
+    def swap_on(self, recv, via, i, t, rows):
+        part = pl.ds(pl.multiple_of(rows * t, 8), rows)
+        far = self.nd // 4
+        for same, sign in ((True, 1), (False, -1)):
+            x = 0 if same else 1
+            self.await_bytes(via.at[x, part], self.xsem.at[i - 8, x, t])
+            self.copy(via.at[x, part], recv.at[self.at(-sign), part], self.fsem.at[i], self.rsem.at[i],
+                      self.at(sign * (far - 1), same)).start()
+
+    def swap_finish(self, send, recv, via, i):
         self.await_bytes(recv, self.rsem.at[i])
         self.await_bytes(send.at[pl.ds(0, self.nd - 1)], self.ssem.at[i])
+        self.await_bytes(via, self.fsem.at[i])
 
 
 def kernel(names, outs, nd, refs):
@@ -265,7 +295,7 @@
     wm, wz = v.row_w.shape[1] // 4, v.ts_w.shape[1] // 4
     gm, gz = wm // 128, wz // 128
     od = v.opm_i.shape[1] // 2
-    comm = Comm(nd, (v.ssem, v.rsem, v.fsem, v.gsem))
+    comm = Comm(nd, (v.ssem, v.rsem, v.fsem, v.gsem, v.xsem))
     me = comm.me
     rows_m = sl * rl
 
@@ -301,18 +331,22 @@
         loop(sl // 2 - 1, body)
         interleave(back(sl // 2 - 1))
 
-    def col_project(load, b):
-        loop(rl // 4, lambda t: project([load(4 * t + n) for n in range(4)], v.col_w.at[b], v.ct, v.ck, 4 * t, None))
-
-    def col_attend(first, count):
+    def col_project(load, b, after=lambda t: None):
+        def body(t):
+            project([load(4 * t + n) for n in range(4)], v.col_w.at[b], v.ct, v.ck, 4 * t, None)
+            after(t)
+        loop(rl // 4, body)
+
+    def col_attend(first, count, after=lambda u: None):
         def body(u):
             t = first + u
             rows = [2 * t, 2 * t + 1]
             keeps = [widen(spread(v.mask_col[pl.ds(i, 1), :], 128), 4 * ns) for i in rows]
             interleave(core(v.ct, v.ck, v.co, rows, gm, None, keeps))
+            after(u)
         loop(count, body)
 
-    def col_out(load, b, finish, loc, gat):
+    def col_out(load, b, finish, loc, gat, after=lambda t: None):
         def out(t):
             rows = [4 * t + n for n in range(4)]
             ups = [dot(v.co[i], v.col_o[b], 0, 0) for i in rows]
@@ -326,6 +360,7 @@
                 a, c = ac[:od], ac[od:]
                 loc[i] = a if b == 0 else c
                 gat[me * rl + i] = c if b == 0 else a
+            after(t)
         loop(rl // 4, out)
 
     def opm(loc, gat, b, load, wb, piece, between):
@@ -385,13 +420,19 @@
         for n, x in enumerate(ps):
             piece[me * rl + len(new) * t + n] = x.astype(BF16)
 
-    def send(out, recv, i, rows, wb=None, piece=None):
+    def send(out, recv, via, i, rows, wb=None, piece=None):
         def finish(t, new):
             half = len(new) // 2
             for n in range(half):
                 stage(out, half * t + n, new[2 * n].astype(F32), new[2 * n + 1].astype(F32), nd)
             count = len(new) * rows
-            comm.swap_start(out, recv, i, pl.multiple_of(count * t, 8), count)
+            comm.swap_start(out, recv, via, i, t, count)
+            if isinstance(t, int):
+                comm.swap_on(recv, via, i, t - 1, count)
+            else:
+                @pl.when(t > 0)
+                def _():
+                    comm.swap_on(recv, via, i, t - 1, count)
             if piece is not None:
                 yield from pieces(t, new, wb, piece)
             else:
@@ -439,8 +480,9 @@
     prepare()
     comm.gather_finish(v.g0, 0)
     spread_bias(v.g0, v.gf, v.rbias, True, None)
-    row_attend(mload, 0, send(v.s0, v.r0, 8, rl))
-    comm.swap_finish(v.s0, v.r0, 8)
+    row_attend(mload, 0, send(v.s0, v.r0, v.x0, 8, rl))
+    comm.swap_on(v.r0, v.x0, 8, sl // 2 - 1, 2 * rl)
+    comm.swap_finish(v.s0, v.r0, v.x0, 8)
 
     fill(v.mwork, v.r0)
     cload = lambda i: take(v.mwork, i, ns, rl)
@@ -450,22 +492,19 @@
         for n, x in enumerate(new):
             v.mc[4 * t + n] = x
     col_attend(0, rl // 2)
-    col_out(cload, 0, keep_four, v.loc0, v.g1)
-    comm.relay_start(v.g1, 1)
+    nc = rl // 4
+    col_out(cload, 0, keep_four, v.loc0, v.g1, lambda t: comm.relay_start(v.g1, 1, t, nc))
 
     c2load = lambda i: v.mc[i].astype(F32)
 
     def send_four(t, new, newf):
         for n in range(2):
             stage(v.s1, 2 * t + n, newf[2 * n], newf[2 * n + 1], nd)
-    col_project(c2load, 1)
-    comm.relay_step(v.g1, 1, 1)
-    col_attend(0, rl // 4)
-    comm.relay_step(v.g1, 1, 2)
-    col_attend(rl // 4, rl // 4)
-    comm.relay_step(v.g1, 1, 3)
+    col_project(c2load, 1, lambda t: comm.relay_step(v.g1, 1, 1, t, nc))
+    col_attend(0, rl // 4, lambda t: comm.relay_step(v.g1, 1, 2, t, nc))
+    col_attend(rl // 4, rl // 4, lambda t: comm.relay_step(v.g1, 1, 3, t, nc))
     col_out(c2load, 1, send_four, v.loc1, v.g2)
-    comm.relay_finish(v.g1, 1)
+    comm.relay_finish(v.g1, 1, nc)
     comm.relay_start(v.g2, 2)
     opm(v.loc0, v.g1, 0, lambda i: v.z[i].astype(F32), v.ts_b[0], v.g3, lambda: comm.relay_step(v.g2, 2, 1))
     comm.gather_start(v.g3, 3)
@@ -474,22 +513,25 @@
     comm.gather_finish(v.g3, 3)
     comm.relay_step(v.g2, 2, 3)
     spread_bias(v.g3, v.gf2, v.tbias, True, mask_r())
-    tri_attend(v.ts_o[0], send(v.s2, v.r2, 9, rl, v.te_b[0], v.g4))
+    tri_attend(v.ts_o[0], send(v.s2, v.r2, v.x2, 9, rl, v.te_b[0], v.g4))
     comm.gather_start(v.g4, 4)
-    comm.swap_finish(v.s2, v.r2, 9)
+    comm.swap_on(v.r2, v.x2, 9, rl // 4 - 1, 4 * rl)
+    comm.swap_finish(v.s2, v.r2, v.x2, 9)
     turn(v.r2)
     tri_project(v.te_w.at[0])
     comm.gather_finish(v.g4, 4)
-    comm.swap_start(v.s1, v.r1, 10, 0, rows_m)
+    comm.swap_start(v.s1, v.r1, v.x1, 10, 0, rows_m)
     spread_bias(v.g4, v.gf2, v.tbias, False, mask_r())
     tri_attend(v.te_o[0], keep(v.zc, v.row_b[1], v.g5))
+
+    comm.swap_on(v.r1, v.x1, 10, 0, rows_m)
 
     comm.relay_finish(v.g2, 2)
     comm.relay_start(v.g5, 5)
     opm(v.loc1, v.g2, 1, zload, v.te_b[1], v.g6, lambda: comm.relay_step(v.g5, 5, 1))
     comm.gather_start(v.g6, 6)
     comm.relay_step(v.g5, 5, 2)
-    comm.swap_finish(v.s1, v.r1, 10)
+    comm.swap_finish(v.s1, v.r1, v.x1, 10)
     fill(v.mwork, v.r1)
     rload = lambda s: take(v.mwork, s, nr, sl)
     row_project(rload, 1)
@@ -497,12 +539,13 @@
     tri_project(v.te_w.at[1])
     comm.gather_finish(v.g6, 6)
     spread_bias(v.g6, v.gf2, v.tbias, True, mask_r())
-    tri_attend(v.te_o[1], send(v.s3, v.r3, 11, rl, v.ts_b[1], v.g7))
+    tri_attend(v.te_o[1], send(v.s3, v.r3, v.x3, 11, rl, v.ts_b[1], v.g7))
     comm.gather_start(v.g7, 7)
+    comm.swap_on(v.r3, v.x3, 11, rl // 4 - 1, 4 * rl)
     comm.relay_finish(v.g5, 5)
     spread_bias(v.g5, v.gf, v.rbias, False, None)
     row_attend(rload, 1, keep(v.m_out))
-    comm.swap_finish(v.s3, v.r3, 11)
+    comm.swap_finish(v.s3, v.r3, v.x3, 11)
     turn(v.r3)
     tri_project(v.ts_w.at[1])
     comm.gather_finish(v.g7, 7)
@@ -535,6 +578,7 @@
         xm, xz = (nd, sl * rl, cm), (nd, rl * rl, cz)
         grow, gtri, gopm = (nd * rl, hm, nr), (nd * rl, ht, nr), (nd * rl, od, ns)
         scratch = dict(
+            x0=((2,) + xm[1:], BF16), x1=((2,) + xm[1:], BF16), x2=((2,) + xz[1:], BF16), x3=((2,) + xz[1:], BF16),
             s0=(xm, BF16), r0=(xm, BF16), s1=(xm, BF16), r1=(xm, BF16),
             s2=(xz, BF16), r2=(xz, BF16), s3=(xz, BF16), r3=(xz, BF16),
             g0=(grow, BF16), g5=(grow, BF16), g1=(gopm, BF16), g2=(gopm, BF16),
@@ -547,7 +591,7 @@
             tt=((rl, 3 * wz, nr), BF16), tk=((rl, nr, wz), BF16), to=((rl, wz, nr), BF16),
             mask_t=((nr, ns), F32), mask_seq=((sl, nr), F32), mask_col=((rl, ns), F32), opm_w=((2, cz, od * od), BF16),
             mc=((rl, ns, cm), BF16), zc=((rl, nr, cz), BF16), loc0=((rl, od, ns), BF16), loc1=((rl, od, ns), BF16))
-        sems = dict(ssem=(12,), rsem=(12,), fsem=(8,), gsem=(8, nd // 2))
+        sems = dict(ssem=(12,), rsem=(12,), fsem=(12,), gsem=(8, nd // 2 + 1, 3), xsem=(4, 2, 4))
         names = list(ins) + list(outs) + list(scratch) + list(sems)
         return pl.pallas_call(
             lambda *refs: kernel(names, outs, nd, refs),

time: 184 us -> 197 us (1.071)
  Pallas kernels: 179 us -> 191 us
    pallas_call x1, Pallas kernels: 179 us -> 191 us  [local_step(): pl.pallas_call(lambda *refs: kernel(names, outs, nd, refs), out_shape=[ja...]
where the time goes in v6:
time: 197 us; the launch traced here: 196 us
  Pallas kernels  191 us (97%)
  local copies, waits for them, and re-layouts  4.59 us (2%)
    pallas_call x1, Pallas kernels, local_step(): pl.pallas_call(lambda *refs: kernel(names, outs, nd, refs), out_shape=[ja...  191 us
    unnamed x5, local copies, waits for them, and re-layouts  4.59 us

profile of v6, /device:TPU:21, one launch (start us, length us, event | category | flops | bytes accessed | tf_op | source)
XLA Modules:
  0.0 196.4 jit_solution(11550579820174458677)
XLA Ops:
  0.6 1.6 copy.19.refs_2_
  2.3 191.2 %shard_map.176 = (bf16[8,192,256]{2,1,0:T(8,128)(2,1)}, bf16[12,192,128]{2,1,0:T(8,128)(2,1)}) custom-call(bf16[8,192,256]{2,1,0:T(8,128)(2,1)} %refs_0_.1, bf16[12,192,128]{2,1,0:T(8,128)(2,1)} %refs_1_.1, s32[128,192]{1,0:T(8,128)} %copy.19.refs_2_, s32[1,192]{1,0:T(1,128)} %bitcast.37, bf16[2,1024,256]{2,1,0:T(8,128)(2,1)} %bitcast.24, ...), custom_call_target="tpu_custom_call" | custom-call | tf_op jit(solution)/shard_map/pallas_call | solution.py:596
  193.4 0.0 copy-start
  193.5 2.1 %copy.22 = bf16[8,192,256]{2,1,0:T(8,128)(2,1)} copy(bf16[8,192,256]{2,1,0:T(8,128)(2,1)} %get-tuple-element.4) | data formatting | bytes 1572864
  195.6 0.0 copy-done
  195.6 0.8 copy.23
Async XLA Ops:
  193.4 2.1 %copy-start = (bf16[12,192,128]{2,1,0:T(8,128)(2,1)S(1)}, bf16[12,192,128]{2,1,0:T(8,128)(2,1)}, u32[]{:S(2)}) copy-start(bf16[12,192,128]{2,1,0:T(8,128)(2,1)} %get-tuple-element.5) | copy-start | bytes 1769476

commit v7 on v6

--- a/solution.py
+++ b/solution.py
@@ -153,7 +153,7 @@
         self.nd = nd
         self.me = lax.axis_index('dap')
         self.partner = self.me + 1 - 2 * lax.rem(self.me, 2)
-        self.ssem, self.rsem, self.fsem, self.gsem, self.xsem = sems
+        self.ssem, self.rsem, self.fsem, self.gsem = sems
 
     def copy(self, src, dst, send, recv, dev):
         return pltpu.make_async_remote_copy(src_ref=src, dst_ref=dst, send_sem=send, recv_sem=recv,
@@ -191,36 +191,24 @@
         def body(k, _):
             self.copy(own, own, self.ssem.at[i], self.gsem.at[i, k, 0], self.near(k, 2)).start()
             return 0
-        lax.fori_loop(1, self.nd // 2 - 1, body, 0)
+        lax.fori_loop(1, self.nd // 2, body, 0)
         self.copy(own, own, self.ssem.at[i], self.gsem.at[i, 0, 0], self.partner).start()
 
     def gather_finish(self, buf, i):
         n = buf.shape[0] // self.nd
         half = self.nd // 2
-        far = self.nd // 4
-
-        def across(ref):
-            self.copy(ref, ref, self.fsem.at[i], self.rsem.at[i], self.partner).start()
 
         def body(k, _):
             slot = buf.at[pl.ds(self.near(k, -2) * n, n)]
             self.await_bytes(slot, self.gsem.at[i, k, 0])
-            across(slot)
+            self.copy(slot, slot, self.fsem.at[i], self.rsem.at[i], self.partner).start()
             return 0
-        lax.fori_loop(1, half - 3, body, 0)
-        for part, sign in ((0, 1), (1, -1)):
-            self.await_bytes(self.slot(buf, sign * (1 - far)), self.gsem.at[i, half - 3 + part, 0])
-            on = self.slot(buf, sign * (1 - far), part * (n // 2), n // 2)
-            self.copy(on, on, self.fsem.at[i], self.gsem.at[i, half - 1 + part, 0], self.at(sign)).start()
-            across(self.slot(buf, sign * (1 - far)))
-        for part in range(2):
-            self.await_bytes(self.slot(buf, far, part * (n // 2), n // 2), self.gsem.at[i, half - 1 + part, 0])
-        across(self.slot(buf, far))
+        lax.fori_loop(1, half, body, 0)
         self.await_bytes(buf.at[pl.ds(0, n)], self.gsem.at[i, 0, 0])
         rest = buf.at[pl.ds(0, (half - 1) * n)]
         self.await_bytes(rest, self.rsem.at[i])
-        self.await_bytes(buf.at[pl.ds(0, half * n)], self.fsem.at[i])
-        self.await_bytes(rest, self.ssem.at[i])
+        self.await_bytes(rest, self.fsem.at[i])
+        self.await_bytes(buf.at[pl.ds(0, half * n)], self.ssem.at[i])
 
     def relay(self, ref, i, recv, dev):
         self.copy(ref, ref, self.ssem.at[i], recv, dev).start()
@@ -253,34 +241,17 @@
         self.await_bytes(buf.at[pl.ds(0, half * n)], self.rsem.at[i])
         self.await_bytes(buf.at[pl.ds(0, (2 * half - 1) * n)], self.ssem.at[i])
 
-    def swap_start(self, send, recv, via, i, t, rows):
+    def swap_start(self, send, recv, i, t, rows):
         part = pl.ds(pl.multiple_of(rows * t, 8), rows)
-        far = self.nd // 4
-        for same, sign in ((True, 1), (False, -1)):
-            x = 0 if same else 1
-            self.copy(send.at[self.at(far, same), part], via.at[x, part], self.ssem.at[i],
-                      self.xsem.at[i - 8, x, t], self.at(sign)).start()
-        for k in range(1, far):
-            for sign in (1, -1):
-                for same in (True, False):
-                    d = self.at(sign * k, same)
-                    self.copy(send.at[d, part], recv.at[self.me, part], self.ssem.at[i], self.rsem.at[i], d).start()
-        self.copy(send.at[self.partner, part], recv.at[self.me, part], self.ssem.at[i], self.rsem.at[i], self.partner).start()
+        for k in range(1, self.nd):
+            off = (k + 1) // 2 if k % 2 else -(k // 2)
+            d = lax.rem(self.me + self.nd + off, self.nd)
+            self.copy(send.at[d, part], recv.at[self.me, part], self.ssem.at[i], self.rsem.at[i], d).start()
         pltpu.make_async_copy(send.at[self.me, part], recv.at[self.me, part], self.rsem.at[i]).start()
 
-    def swap_on(self, recv, via, i, t, rows):
-        part = pl.ds(pl.multiple_of(rows * t, 8), rows)
-        far = self.nd // 4
-        for same, sign in ((True, 1), (False, -1)):
-            x = 0 if same else 1
-            self.await_bytes(via.at[x, part], self.xsem.at[i - 8, x, t])
-            self.copy(via.at[x, part], recv.at[self.at(-sign), part], self.fsem.at[i], self.rsem.at[i],
-                      self.at(sign * (far - 1), same)).start()
-
-    def swap_finish(self, send, recv, via, i):
+    def swap_finish(self, send, recv, i):
         self.await_bytes(recv, self.rsem.at[i])
         self.await_bytes(send.at[pl.ds(0, self.nd - 1)], self.ssem.at[i])
-        self.await_bytes(via, self.fsem.at[i])
 
 
 def kernel(names, outs, nd, refs):
@@ -295,7 +266,7 @@
     wm, wz = v.row_w.shape[1] // 4, v.ts_w.shape[1] // 4
     gm, gz = wm // 128, wz // 128
     od = v.opm_i.shape[1] // 2
-    comm = Comm(nd, (v.ssem, v.rsem, v.fsem, v.gsem, v.xsem))
+    comm = Comm(nd, (v.ssem, v.rsem, v.fsem, v.gsem))
     me = comm.me
     rows_m = sl * rl
 
@@ -420,19 +391,13 @@
         for n, x in enumerate(ps):
             piece[me * rl + len(new) * t + n] = x.astype(BF16)
 
-    def send(out, recv, via, i, rows, wb=None, piece=None):
+    def send(out, recv, i, rows, wb=None, piece=None):
         def finish(t, new):
             half = len(new) // 2
             for n in range(half):
                 stage(out, half * t + n, new[2 * n].astype(F32), new[2 * n + 1].astype(F32), nd)
             count = len(new) * rows
-            comm.swap_start(out, recv, via, i, t, count)
-            if isinstance(t, int):
-                comm.swap_on(recv, via, i, t - 1, count)
-            else:
-                @pl.when(t > 0)
-                def _():
-                    comm.swap_on(recv, via, i, t - 1, count)
+            comm.swap_start(out, recv, i, t, count)
             if piece is not None:
                 yield from pieces(t, new, wb, piece)
             else:
@@ -480,9 +445,8 @@
     prepare()
     comm.gather_finish(v.g0, 0)
     spread_bias(v.g0, v.gf, v.rbias, True, None)
-    row_attend(mload, 0, send(v.s0, v.r0, v.x0, 8, rl))
-    comm.swap_on(v.r0, v.x0, 8, sl // 2 - 1, 2 * rl)
-    comm.swap_finish(v.s0, v.r0, v.x0, 8)
+    row_attend(mload, 0, send(v.s0, v.r0, 8, rl))
+    comm.swap_finish(v.s0, v.r0, 8)
 
     fill(v.mwork, v.r0)
     cload = lambda i: take(v.mwork, i, ns, rl)
@@ -513,25 +477,23 @@
     comm.gather_finish(v.g3, 3)
     comm.relay_step(v.g2, 2, 3)
     spread_bias(v.g3, v.gf2, v.tbias, True, mask_r())
-    tri_attend(v.ts_o[0], send(v.s2, v.r2, v.x2, 9, rl, v.te_b[0], v.g4))
+    tri_attend(v.ts_o[0], send(v.s2, v.r2, 9, rl, v.te_b[0], v.g4))
     comm.gather_start(v.g4, 4)
-    comm.swap_on(v.r2, v.x2, 9, rl // 4 - 1, 4 * rl)
-    comm.swap_finish(v.s2, v.r2, v.x2, 9)
+    comm.swap_finish(v.s2, v.r2, 9)
     turn(v.r2)
     tri_project(v.te_w.at[0])
     comm.gather_finish(v.g4, 4)
-    comm.swap_start(v.s1, v.r1, v.x1, 10, 0, rows_m)
+    comm.swap_start(v.s1, v.r1, 10, 0, rows_m)
     spread_bias(v.g4, v.gf2, v.tbias, False, mask_r())
     tri_attend(v.te_o[0], keep(v.zc, v.row_b[1], v.g5))
 
-    comm.swap_on(v.r1, v.x1, 10, 0, rows_m)
 
     comm.relay_finish(v.g2, 2)
     comm.relay_start(v.g5, 5)
     opm(v.loc1, v.g2, 1, zload, v.te_b[1], v.g6, lambda: comm.relay_step(v.g5, 5, 1))
     comm.gather_start(v.g6, 6)
     comm.relay_step(v.g5, 5, 2)
-    comm.swap_finish(v.s1, v.r1, v.x1, 10)
+    comm.swap_finish(v.s1, v.r1, 10)
     fill(v.mwork, v.r1)
     rload = lambda s: take(v.mwork, s, nr, sl)
     row_project(rload, 1)
@@ -539,13 +501,12 @@
     tri_project(v.te_w.at[1])
     comm.gather_finish(v.g6, 6)
     spread_bias(v.g6, v.gf2, v.tbias, True, mask_r())
-    tri_attend(v.te_o[1], send(v.s3, v.r3, v.x3, 11, rl, v.ts_b[1], v.g7))
+    tri_attend(v.te_o[1], send(v.s3, v.r3, 11, rl, v.ts_b[1], v.g7))
     comm.gather_start(v.g7, 7)
-    comm.swap_on(v.r3, v.x3, 11, rl // 4 - 1, 4 * rl)
     comm.relay_finish(v.g5, 5)
     spread_bias(v.g5, v.gf, v.rbias, False, None)
     row_attend(rload, 1, keep(v.m_out))
-    comm.swap_finish(v.s3, v.r3, v.x3, 11)
+    comm.swap_finish(v.s3, v.r3, 11)
     turn(v.r3)
     tri_project(v.ts_w.at[1])
     comm.gather_finish(v.g7, 7)
@@ -578,7 +539,6 @@
         xm, xz = (nd, sl * rl, cm), (nd, rl * rl, cz)
         grow, gtri, gopm = (nd * rl, hm, nr), (nd * rl, ht, nr), (nd * rl, od, ns)
         scratch = dict(
-            x0=((2,) + xm[1:], BF16), x1=((2,) + xm[1:], BF16), x2=((2,) + xz[1:], BF16), x3=((2,) + xz[1:], BF16),
             s0=(xm, BF16), r0=(xm, BF16), s1=(xm, BF16), r1=(xm, BF16),
             s2=(xz, BF16), r2=(xz, BF16), s3=(xz, BF16), r3=(xz, BF16),
             g0=(grow, BF16), g5=(grow, BF16), g1=(gopm, BF16), g2=(gopm, BF16),
@@ -591,7 +551,7 @@
             tt=((rl, 3 * wz, nr), BF16), tk=((rl, nr, wz), BF16), to=((rl, wz, nr), BF16),
             mask_t=((nr, ns), F32), mask_seq=((sl, nr), F32), mask_col=((rl, ns), F32), opm_w=((2, cz, od * od), BF16),
             mc=((rl, ns, cm), BF16), zc=((rl, nr, cz), BF16), loc0=((rl, od, ns), BF16), loc1=((rl, od, ns), BF16))
-        sems = dict(ssem=(12,), rsem=(12,), fsem=(12,), gsem=(8, nd // 2 + 1, 3), xsem=(4, 2, 4))
+        sems = dict(ssem=(12,), rsem=(12,), fsem=(8,), gsem=(8, nd // 2, 3))
         names = list(ins) + list(outs) + list(scratch) + list(sems)
         return pl.pallas_call(
             lambda *refs: kernel(names, outs, nd, refs),

time: 197 us -> 185 us (0.939)
  Pallas kernels: 191 us -> 178 us
    pallas_call x1, Pallas kernels: 191 us -> 178 us  [local_step(): pl.pallas_call(lambda *refs: kernel(names, outs, nd, refs), out_shape=[ja...]
where the time goes in v7:
time: 185 us; the launch traced here: 183 us
  Pallas kernels  178 us (96%)
  local copies, waits for them, and re-layouts  4.59 us (2%)
    pallas_call x1, Pallas kernels, local_step(): pl.pallas_call(lambda *refs: kernel(names, outs, nd, refs), out_shape=[ja...  178 us
    unnamed x5, local copies, waits for them, and re-layouts  4.59 us

profile of v7, /device:TPU:21, one launch (start us, length us, event | category | flops | bytes accessed | tf_op | source)
XLA Modules:
  0.0 182.9 jit_solution(13556992868879037135)
XLA Ops:
  0.6 1.6 copy.19.refs_2_
  2.3 177.6 %shard_map.176 = (bf16[8,192,256]{2,1,0:T(8,128)(2,1)}, bf16[12,192,128]{2,1,0:T(8,128)(2,1)}) custom-call(bf16[8,192,256]{2,1,0:T(8,128)(2,1)} %refs_0_.1, bf16[12,192,128]{2,1,0:T(8,128)(2,1)} %refs_1_.1, s32[128,192]{1,0:T(8,128)} %copy.19.refs_2_, s32[1,192]{1,0:T(1,128)} %bitcast.37, bf16[2,1024,256]{2,1,0:T(8,128)(2,1)} %bitcast.24, ...), custom_call_target="tpu_custom_call" | custom-call | tf_op jit(solution)/shard_map/pallas_call | solution.py:556
  179.9 0.0 copy-start
  179.9 2.1 %copy.22 = bf16[8,192,256]{2,1,0:T(8,128)(2,1)} copy(bf16[8,192,256]{2,1,0:T(8,128)(2,1)} %get-tuple-element.4) | data formatting | bytes 1572864
  182.0 0.0 copy-done
  182.0 0.8 copy.23
Async XLA Ops:
  179.9 2.1 %copy-start = (bf16[12,192,128]{2,1,0:T(8,128)(2,1)S(1)}, bf16[12,192,128]{2,1,0:T(8,128)(2,1)}, u32[]{:S(2)}) copy-start(bf16[12,192,128]{2,1,0:T(8,128)(2,1)} %get-tuple-element.5) | copy-start | bytes 1769476

commit v8 on v7

--- a/solution.py
+++ b/solution.py
@@ -138,14 +138,16 @@
         bias[g] = value
 
 
-def bias_pieces(load, count, wb, store):
+def bias_pieces(load, count, wb, store, after):
     def body(t, _):
         zl = [layer_norm(load(4 * t + n)) for n in range(4)]
         ps = [dot(wb, v, 1, 1) for v in zl]
         for n, v in enumerate(ps):
             store(4 * t + n, v.astype(BF16))
+        after(t)
         return 0
-    lax.fori_loop(0, count // 4, body, 0)
+    body(0, 0)
+    lax.fori_loop(1, count // 4, body, 0)
 
 
 class Comm:
@@ -185,10 +187,12 @@
         n = buf.shape[0] // self.nd
         return buf.at[pl.ds(self.at(chips) * n + start, n if count is None else count)]
 
-    def gather_start(self, buf, i):
-        own = self.slot(buf, 0)
-
-        def body(k, _):
+    def gather_start(self, buf, i, c=0, nc=1):
+        m = buf.shape[0] // self.nd // nc
+        own = self.slot(buf, 0, c * m, m)
+
+        def body(j, _):
+            k = self.nd // 2 - j
             self.copy(own, own, self.ssem.at[i], self.gsem.at[i, k, 0], self.near(k, 2)).start()
             return 0
         lax.fori_loop(1, self.nd // 2, body, 0)
@@ -243,7 +247,7 @@
 
     def swap_start(self, send, recv, i, t, rows):
         part = pl.ds(pl.multiple_of(rows * t, 8), rows)
-        for k in range(1, self.nd):
+        for k in range(self.nd - 1, 0, -1):
             off = (k + 1) // 2 if k % 2 else -(k // 2)
             d = lax.rem(self.me + self.nd + off, self.nd)
             self.copy(send.at[d, part], recv.at[self.me, part], self.ssem.at[i], self.rsem.at[i], d).start()
@@ -254,7 +258,7 @@
         self.await_bytes(send.at[pl.ds(0, self.nd - 1)], self.ssem.at[i])
 
 
-def kernel(names, outs, nd, refs):
+def kernel(names, late, nd, refs):
     r = dict(zip(names, refs))
     class N:
         pass
@@ -266,6 +270,14 @@
     wm, wz = v.row_w.shape[1] // 4, v.ts_w.shape[1] // 4
     gm, gz = wm // 128, wz // 128
     od = v.opm_i.shape[1] // 2
+    def late_start():
+        for n, name in enumerate(late):
+            pltpu.make_async_copy(r['hbm_' + name], r[name], v.lsem.at[n]).start()
+
+    def late_wait():
+        for n, name in enumerate(late):
+            pltpu.make_async_copy(r['hbm_' + name], r[name], v.lsem.at[n]).wait()
+
     comm = Comm(nd, (v.ssem, v.rsem, v.fsem, v.gsem))
     me = comm.me
     rows_m = sl * rl
@@ -334,7 +346,7 @@
             after(t)
         loop(rl // 4, out)
 
-    def opm(loc, gat, b, load, wb, piece, between):
+    def opm(loc, gat, b, load, wb, piece, i_piece, between):
         v.gcol[...] = gat[...].astype(F32).reshape(v.gcol.shape)
         v.nrm[...] = dot(v.mask_col[...].astype(BF16), v.msa_mask[...].astype(F32).astype(BF16), 1, 0)
 
@@ -362,6 +374,7 @@
             ps = [dot(wb, x, 1, 1) for x in ln]
             for i, x in zip(rows, ps):
                 piece[me * rl + i] = x.astype(BF16)
+            comm.gather_start(piece, i_piece, t, rl // 4)
         loop(rl // 4, fold)
 
     def zload(i):
@@ -437,9 +450,15 @@
             v.opm_w[1, :, 128 * j:128 * j + 128] = v.opm_o[1, 128 * j:128 * j + 128, :].astype(F32).T.astype(BF16)
 
     comm.barrier_signal()
-    bias_pieces(lambda i: v.z[i].astype(F32), rl, v.row_b[0], store_piece(v.g0))
-    comm.barrier_wait()
-    comm.gather_start(v.g0, 0)
+    late_start()
+    nc = rl // 4
+
+    def first_send(t):
+        if isinstance(t, int) and t == 0:
+            comm.barrier_wait()
+        comm.gather_start(v.g0, 0, t, nc)
+    bias_pieces(lambda i: v.z[i].astype(F32), rl, v.row_b[0], store_piece(v.g0), first_send)
+    late_wait()
     mload = lambda s: v.m[s].astype(F32)
     row_project(mload, 0)
     prepare()
@@ -456,7 +475,6 @@
         for n, x in enumerate(new):
             v.mc[4 * t + n] = x
     col_attend(0, rl // 2)
-    nc = rl // 4
     col_out(cload, 0, keep_four, v.loc0, v.g1, lambda t: comm.relay_start(v.g1, 1, t, nc))
 
     c2load = lambda i: v.mc[i].astype(F32)
@@ -470,8 +488,7 @@
     col_out(c2load, 1, send_four, v.loc1, v.g2)
     comm.relay_finish(v.g1, 1, nc)
     comm.relay_start(v.g2, 2)
-    opm(v.loc0, v.g1, 0, lambda i: v.z[i].astype(F32), v.ts_b[0], v.g3, lambda: comm.relay_step(v.g2, 2, 1))
-    comm.gather_start(v.g3, 3)
+    opm(v.loc0, v.g1, 0, lambda i: v.z[i].astype(F32), v.ts_b[0], v.g3, 3, lambda: comm.relay_step(v.g2, 2, 1))
     comm.relay_step(v.g2, 2, 2)
     tri_project(v.ts_w.at[0])
     comm.gather_finish(v.g3, 3)
@@ -490,8 +507,7 @@
 
     comm.relay_finish(v.g2, 2)
     comm.relay_start(v.g5, 5)
-    opm(v.loc1, v.g2, 1, zload, v.te_b[1], v.g6, lambda: comm.relay_step(v.g5, 5, 1))
-    comm.gather_start(v.g6, 6)
+    opm(v.loc1, v.g2, 1, zload, v.te_b[1], v.g6, 6, lambda: comm.relay_step(v.g5, 5, 1))
     comm.relay_step(v.g5, 5, 2)
     comm.swap_finish(v.s1, v.r1, 10)
     fill(v.mwork, v.r1)
@@ -552,11 +568,15 @@
             mask_t=((nr, ns), F32), mask_seq=((sl, nr), F32), mask_col=((rl, ns), F32), opm_w=((2, cz, od * od), BF16),
             mc=((rl, ns, cm), BF16), zc=((rl, nr, cz), BF16), loc0=((rl, od, ns), BF16), loc1=((rl, od, ns), BF16))
         sems = dict(ssem=(12,), rsem=(12,), fsem=(8,), gsem=(8, nd // 2, 3))
-        names = list(ins) + list(outs) + list(scratch) + list(sems)
+        late = [k for k in ins if k not in ('z', 'row_b')]
+        for k in late:
+            scratch[k] = (ins[k].shape, ins[k].dtype)
+        sems['lsem'] = (len(late),)
+        names = ['hbm_' + k if k in late else k for k in ins] + list(outs) + list(scratch) + list(sems)
         return pl.pallas_call(
-            lambda *refs: kernel(names, outs, nd, refs),
+            lambda *refs: kernel(names, late, nd, refs),
             out_shape=[jax.ShapeDtypeStruct(o.shape, o.dtype) for o in outs.values()],
-            in_specs=[pl.BlockSpec(memory_space=pltpu.VMEM)] * len(ins),
+            in_specs=[pl.BlockSpec(memory_space=pl.ANY if k in late else pltpu.VMEM) for k in ins],
             out_specs=[pl.BlockSpec(memory_space=pltpu.VMEM)] * len(outs),
             scratch_shapes=[pltpu.VMEM(*x) for x in scratch.values()] + [pltpu.SemaphoreType.DMA(x) for x in sems.values()],
             compiler_params=pltpu.CompilerParams(collective_id=0, has_side_effects=True, vmem_limit_bytes=67043328),

time: 185 us -> 177 us (0.957)
  Pallas kernels: 178 us -> 171 us
    pallas_call x1, Pallas kernels: 178 us -> 171 us  [local_step(): pl.pallas_call(lambda *refs: kernel(names, late, nd, refs), out_shape=[ja...]
where the time goes in v8:
time: 177 us; the launch traced here: 176 us
  Pallas kernels  171 us (97%)
  local copies, waits for them, and re-layouts  4.59 us (3%)
    pallas_call x1, Pallas kernels, local_step(): pl.pallas_call(lambda *refs: kernel(names, late, nd, refs), out_shape=[ja...  171 us
    unnamed x5, local copies, waits for them, and re-layouts  4.59 us

profile of v8, /device:TPU:21, one launch (start us, length us, event | category | flops | bytes accessed | tf_op | source)
XLA Modules:
  0.0 176.4 jit_solution(1291456603434119362)
XLA Ops:
  0.6 1.6 copy.19.refs_2_
  2.3 171.2 %shard_map.176 = (bf16[8,192,256]{2,1,0:T(8,128)(2,1)}, bf16[12,192,128]{2,1,0:T(8,128)(2,1)}) custom-call(bf16[8,192,256]{2,1,0:T(8,128)(2,1)} %refs_0_.1, bf16[12,192,128]{2,1,0:T(8,128)(2,1)} %refs_1_.1, s32[128,192]{1,0:T(8,128)} %copy.19.refs_2_, s32[1,192]{1,0:T(1,128)} %bitcast.37, bf16[2,1024,256]{2,1,0:T(8,128)(2,1)} %bitcast.24, ...), custom_call_target="tpu_custom_call" | custom-call | tf_op jit(solution)/shard_map/pallas_call | solution.py:576
  173.4 0.0 copy-start
  173.5 2.1 %copy.22 = bf16[8,192,256]{2,1,0:T(8,128)(2,1)} copy(bf16[8,192,256]{2,1,0:T(8,128)(2,1)} %get-tuple-element.4) | data formatting | bytes 1572864
  175.6 0.0 copy-done
  175.6 0.8 copy.23
Async XLA Ops:
  173.4 2.1 %copy-start = (bf16[12,192,128]{2,1,0:T(8,128)(2,1)S(1)}, bf16[12,192,128]{2,1,0:T(8,128)(2,1)}, u32[]{:S(2)}) copy-start(bf16[12,192,128]{2,1,0:T(8,128)(2,1)} %get-tuple-element.5) | copy-start | bytes 1769476
